TPU v7x, 32 devices: a whole 2x2x4 slice. The times are simulated.
32 devices in a mesh: fsdp: 2 (over x), ctx: 4 (over z), tp: 4 (over y, core).
Axes of the slice: x: 2, y: 2, z: 4, core: 2. Of those that a mesh axis runs over, the one named last changes fastest.
Arguments:
- tokens: bfloat16 [2, 4096, 1024], P('fsdp', 'ctx'), may hold values from -6 to 6
- condition: float32 [2, 1024], replicated, may hold values from -6 to 6
- cotangent: bfloat16 [2, 4096, 1024], P('fsdp', 'ctx'), may hold values from -6 to 6
- joint_weight: float32 [1024, 3072], P(('fsdp', 'ctx'), 'tp'), may hold values from -0.1875 to 0.1875
- joint_moments: float32 [2, 1024, 3072], P(None, ('fsdp', 'ctx'), 'tp'), as said below
- output_weight: float32 [1024, 1024], P(('fsdp', 'ctx'), 'tp'), may hold values from -3 to 3
- output_moments: float32 [2, 1024, 1024], P(None, ('fsdp', 'ctx'), 'tp'), as said below
- expand_weight: float32 [1024, 4096], P(('fsdp', 'ctx'), 'tp'), may hold values from -0.1875 to 0.1875
- expand_moments: float32 [2, 1024, 4096], P(None, ('fsdp', 'ctx'), 'tp'), as said below
- shrink_weight: float32 [1024, 4096], P(('fsdp', 'ctx'), 'tp'), may hold values from -0.09375 to 0.09375
- shrink_moments: float32 [2, 1024, 4096], P(None, ('fsdp', 'ctx'), 'tp'), as said below
- modulate_weight: float32 [1024, 6144], P(('fsdp', 'ctx'), 'tp'), may hold values from -0.1875 to 0.1875
- modulate_moments: float32 [2, 1024, 6144], P(None, ('fsdp', 'ctx'), 'tp'), as said below
- attention_bias: float32 [2048], P('tp'), may hold values from -3 to 3
- attention_moments: float32 [2, 2048], P(None, 'tp'), as said below
- hidden_bias: float32 [4096], P('tp'), may hold values from -3 to 3
- hidden_moments: float32 [2, 4096], P(None, 'tp'), as said below
- condition_bias: float32 [6144], P('tp'), may hold values from -3 to 3
- condition_moments: float32 [2, 6144], P(None, 'tp'), as said below
- residual_bias: float32 [2, 1024], replicated, may hold values from -3 to 3
- residual_moments: float32 [2, 2, 1024], replicated, as said below
Outputs:
- mixed: bfloat16 [2, 4096, 1024], P('fsdp', 'ctx')
- tokens_grad: float32 [2, 4096, 1024], P('fsdp', 'ctx')
- condition_grad: float32 [2, 1024], P('fsdp')
- grad_norm: float32 [], replicated
- joint_updated: float32 [1024, 3072], P(('fsdp', 'ctx'), 'tp')
- joint_averages: float32 [2, 1024, 3072], P(None, ('fsdp', 'ctx'), 'tp')
- output_updated: float32 [1024, 1024], P(('fsdp', 'ctx'), 'tp')
- output_averages: float32 [2, 1024, 1024], P(None, ('fsdp', 'ctx'), 'tp')
- expand_updated: float32 [1024, 4096], P(('fsdp', 'ctx'), 'tp')
- expand_averages: float32 [2, 1024, 4096], P(None, ('fsdp', 'ctx'), 'tp')
- shrink_updated: float32 [1024, 4096], P(('fsdp', 'ctx'), 'tp')
- shrink_averages: float32 [2, 1024, 4096], P(None, ('fsdp', 'ctx'), 'tp')
- modulate_updated: float32 [1024, 6144], P(('fsdp', 'ctx'), 'tp')
- modulate_averages: float32 [2, 1024, 6144], P(None, ('fsdp', 'ctx'), 'tp')
- attention_updated: float32 [2048], P('tp')
- attention_averages: float32 [2, 2048], P(None, 'tp')
- hidden_updated: float32 [4096], P('tp')
- hidden_averages: float32 [2, 4096], P(None, 'tp')
- condition_updated: float32 [6144], P('tp')
- condition_averages: float32 [2, 6144], P(None, 'tp')
- residual_updated: float32 [2, 1024], replicated
- residual_averages: float32 [2, 2, 1024], replicated
Inputs may be any that keep to these rules, and one draw needn't show every extreme that they name: `joint_moments`: the roots of the second moments (index 1 of the first dimension) are positive. `output_moments`: the roots of the second moments are positive. `expand_moments`: the roots of the second moments are positive. `shrink_moments`: the roots of the second moments are positive. `modulate_moments`: the roots of the second moments are positive. `attention_moments`: the roots of the second moments are positive. `hidden_moments`: the roots of the second moments are positive. `condition_moments`: the roots of the second moments are positive. `residual_moments`: the roots of the second moments are positive.
All inputs are finite; a program needn't handle non-finite values.
Results may differ from a plain program's by a relative error of at most 0.0095.
The roundings to bfloat16 on the way count: a program that leaves them out, or rounds other values in their place, can miss the bound.
Values may be sent and summed in bfloat16 or wider, within the bound.
A program may use at most 256 MiB of HBM per device.

v0:
```python
from functools import partial

import jax
import jax.numpy as jnp
from jax import lax
from jax.sharding import PartitionSpec as P

HEAD_DIM = 64
ADAM_STEP = 10


norm_epsilon = 1e-06
first_decay = 0.9
second_decay = 0.999
adam_epsilon = 1e-08
learning_rate = 0.05
weight_decay = 0.1
clip_limit = 1.0


def dot_last(left_side, right_side):
    return lax.dot_general(
        left_side, right_side, (((1,), (1,)), ((), ())), preferred_element_type=jnp.float32
    )


def dot_first(left_side, right_side):
    return lax.dot_general(
        left_side, right_side, (((0,), (0,)), ((), ())), preferred_element_type=jnp.float32
    )


def exact_first(left_side, right_side):
    return lax.dot_general(
        left_side,
        right_side,
        (((0,), (0,)), ((), ())),
        precision=lax.Precision.HIGHEST,
        preferred_element_type=jnp.float32,
    )


def exact_last(left_side, right_side):
    return lax.dot_general(
        left_side,
        right_side,
        (((1,), (1,)), ((), ())),
        precision=lax.Precision.HIGHEST,
        preferred_element_type=jnp.float32,
    )


def normalize(values):
    center = values - jnp.mean(values, axis=-1, keepdims=True)
    inverse = lax.rsqrt(jnp.mean(center * center, axis=-1, keepdims=True) + norm_epsilon)
    return (center * inverse, inverse)


def normalize_back(grad_normed, normed, inverse):
    return inverse * (
        grad_normed
        - jnp.mean(grad_normed, axis=-1, keepdims=True)
        - normed * jnp.mean(grad_normed * normed, axis=-1, keepdims=True)
    )


def branch_total(partial_sum):
    return lax.psum(partial_sum, "tp")


def attend_forward(queries, keys_all, values_all, score_scale, block_rows):
    row_count, head_count, head_width = queries.shape

    def one_block(query_block):
        scores = (
            jnp.einsum("qhd,khd->hqk", query_block, keys_all, preferred_element_type=jnp.float32)
            * score_scale
        )
        row_peak = jnp.max(scores, axis=-1, keepdims=True)
        raised = jnp.exp(scores - row_peak)
        row_total = jnp.sum(raised, axis=-1, keepdims=True)
        weights = (raised / row_total).astype(jnp.bfloat16)
        output = jnp.einsum("hqk,khd->qhd", weights, values_all, preferred_element_type=jnp.float32)
        return (output.astype(jnp.bfloat16), row_peak + jnp.log(row_total))

    outputs, logsum = lax.map(
        one_block, queries.reshape(row_count // block_rows, block_rows, head_count, head_width)
    )
    return (outputs.reshape(row_count, head_count * head_width), logsum)


def attend_backward(queries, keys_all, values_all, output_grad, logsum, score_scale, block_rows):
    row_count, head_count, head_width = queries.shape

    def one_block(running, pieces):
        key_total, value_total = running
        query_block, grad_block, logsum_block = pieces
        scores = (
            jnp.einsum("qhd,khd->hqk", query_block, keys_all, preferred_element_type=jnp.float32)
            * score_scale
        )
        probability = jnp.exp(scores - logsum_block)
        weights = probability.astype(jnp.bfloat16)
        value_total = value_total + jnp.einsum(
            "hqk,qhd->khd", weights, grad_block, preferred_element_type=jnp.float32
        )
        prob_grad = jnp.einsum(
            "qhd,khd->hqk", grad_block, values_all, preferred_element_type=jnp.float32
        )
        center = jnp.sum(probability * prob_grad, axis=-1, keepdims=True)
        score_low = (probability * (prob_grad - center)).astype(jnp.bfloat16)
        query_grad = (
            jnp.einsum("hqk,khd->qhd", score_low, keys_all, preferred_element_type=jnp.float32)
            * score_scale
        )
        key_total = (
            key_total
            + jnp.einsum("hqk,qhd->khd", score_low, query_block, preferred_element_type=jnp.float32)
            * score_scale
        )
        return ((key_total, value_total), query_grad)

    zero_start = jnp.zeros(keys_all.shape, jnp.float32)
    count_blocks = row_count // block_rows
    pieces = (
        queries.reshape(count_blocks, block_rows, head_count, head_width),
        output_grad.reshape(count_blocks, block_rows, head_count, head_width),
        logsum,
    )
    (key_total, value_total), query_grads = lax.scan(one_block, (zero_start, zero_start), pieces)
    return (query_grads.reshape(row_count, head_count, head_width), key_total, value_total)


def adam_step(master, moments, gradient, clip_factor, decay_rate):
    scaled = clip_factor * gradient
    first_moment = first_decay * moments[0] + (1.0 - first_decay) * scaled
    second_moment = second_decay * moments[1] * moments[1] + (1.0 - second_decay) * scaled * scaled
    first_hat = first_moment / (1.0 - first_decay**ADAM_STEP)
    second_hat = second_moment / (1.0 - second_decay**ADAM_STEP)
    updated = master - learning_rate * (
        first_hat / (jnp.sqrt(second_hat) + adam_epsilon) + decay_rate * master
    )
    return (updated, jnp.stack([first_moment, jnp.sqrt(second_moment)]))


def local(
    tokens,
    condition,
    cotangent,
    joint_weight,
    joint_moments,
    output_weight,
    output_moments,
    expand_weight,
    expand_moments,
    shrink_weight,
    shrink_moments,
    modulate_weight,
    modulate_moments,
    attention_bias,
    attention_moments,
    hidden_bias,
    hidden_moments,
    condition_bias,
    condition_moments,
    residual_bias,
    residual_moments,
):
    latent_count, row_count, model_width = tokens.shape
    head_count = joint_weight.shape[1] // (3 * HEAD_DIM)
    inner_width = head_count * HEAD_DIM
    block_rows = min(512, row_count)
    score_scale = HEAD_DIM ** (-0.5)
    joint_full, output_full, expand_full, shrink_full, modulate_full = (
        lax.all_gather(joint_weight.astype(jnp.bfloat16), ("fsdp", "ctx"), axis=0, tiled=True),
        lax.all_gather(output_weight.astype(jnp.bfloat16), ("fsdp", "ctx"), axis=0, tiled=True),
        lax.all_gather(expand_weight.astype(jnp.bfloat16), ("fsdp", "ctx"), axis=0, tiled=True),
        lax.all_gather(shrink_weight.astype(jnp.bfloat16), ("fsdp", "ctx"), axis=0, tiled=True),
        lax.all_gather(modulate_weight.astype(jnp.bfloat16), ("fsdp", "ctx"), axis=0, tiled=True),
    )
    condition_here = lax.dynamic_slice_in_dim(
        condition, lax.axis_index("fsdp") * latent_count, latent_count, 0
    )
    condition_act, silu_pull = jax.vjp(jax.nn.silu, condition_here)
    condition_low = condition_act.astype(jnp.bfloat16)
    modulation_part = (
        jnp.dot(condition_low, modulate_full, preferred_element_type=jnp.float32) + condition_bias
    )
    modulation = lax.all_gather(modulation_part, "tp", axis=1, tiled=True)
    spans = [
        modulation[:, span_index * model_width : (span_index + 1) * model_width][:, None, :]
        for span_index in range(6)
    ]
    shift_first, scale_first, gate_first, shift_second, scale_second, gate_second = spans
    inputs = tokens.astype(jnp.float32)
    normed_first, inverse_first = normalize(inputs)
    hidden_first = (
        (normed_first * (1.0 + scale_first) + shift_first)
        .astype(jnp.bfloat16)
        .reshape(-1, model_width)
    )
    bias_pairs = attention_bias.reshape(head_count, 2, HEAD_DIM)
    joint_offset = jnp.stack(
        [bias_pairs[:, 0], jnp.zeros_like(bias_pairs[:, 0]), bias_pairs[:, 1]], axis=1
    ).reshape(-1)
    joint_low = (
        jnp.dot(hidden_first, joint_full, preferred_element_type=jnp.float32) + joint_offset
    ).astype(jnp.bfloat16)
    joint_low = joint_low.reshape(latent_count, row_count, head_count, 3, HEAD_DIM)
    queries = joint_low[:, :, :, 0, :]
    keys_low = joint_low[:, :, :, 1, :].reshape(latent_count, row_count, inner_width)
    values_low = joint_low[:, :, :, 2, :].reshape(latent_count, row_count, inner_width)
    keys_gathered, values_gathered = (
        lax.all_gather(keys_low, "ctx", axis=1, tiled=True),
        lax.all_gather(values_low, "ctx", axis=1, tiled=True),
    )
    total_rows = keys_gathered.shape[1]
    latent = 0
    attended_one, logsum_one = attend_forward(
        queries[latent],
        keys_gathered[latent].reshape(total_rows, head_count, HEAD_DIM),
        values_gathered[latent].reshape(total_rows, head_count, HEAD_DIM),
        score_scale,
        block_rows,
    )
    attended_list = [attended_one]
    logsum_list = [logsum_one]
    attended_low = jnp.stack(attended_list).reshape(-1, inner_width)
    attn_part = dot_last(attended_low, output_full).reshape(latent_count, row_count, model_width)
    attn_value = branch_total(attn_part) + residual_bias[0]
    middle = inputs + gate_first * attn_value
    normed_second, inverse_second = normalize(middle)
    second_low = (normed_second * (1.0 + scale_second) + shift_second).astype(jnp.bfloat16)
    hidden_second = second_low.reshape(-1, model_width)
    expand_pre = (
        jnp.dot(hidden_second, expand_full, preferred_element_type=jnp.float32) + hidden_bias
    )
    activated, gelu_pull = jax.vjp(partial(jax.nn.gelu, approximate=True), expand_pre)
    activated_low = activated.astype(jnp.bfloat16)
    shrink_part = dot_last(activated_low, shrink_full).reshape(latent_count, row_count, model_width)
    result_grad = cotangent.astype(jnp.float32)
    shrink_value = branch_total(shrink_part) + residual_bias[1]
    result = middle + gate_second * shrink_value
    mixed = result.astype(jnp.bfloat16)
    gate_second_grad = jnp.sum(result_grad * shrink_value, axis=1)
    shrink_grad = gate_second * result_grad
    residual_second_grad = jnp.sum(shrink_grad, axis=(0, 1))
    shrink_low = shrink_grad.reshape(-1, model_width).astype(jnp.bfloat16)
    shrink_weight_grad = dot_first(shrink_low, activated_low)
    activated_grad = jnp.dot(shrink_low, shrink_full, preferred_element_type=jnp.float32)
    expand_grad = gelu_pull(activated_grad)[0]
    hidden_bias_grad = jnp.sum(expand_grad, axis=0)
    expand_low = expand_grad.astype(jnp.bfloat16)
    expand_weight_grad = dot_first(hidden_second, expand_low)
    second_part = dot_last(expand_low, expand_full).reshape(latent_count, row_count, model_width)
    second_input_grad = branch_total(second_part)
    shift_second_grad = jnp.sum(second_input_grad, axis=1)
    scale_second_grad = jnp.sum(second_input_grad * normed_second, axis=1)
    middle_grad = result_grad + normalize_back(
        second_input_grad * (1.0 + scale_second), normed_second, inverse_second
    )
    gate_first_grad = jnp.sum(middle_grad * attn_value, axis=1)
    attn_grad = gate_first * middle_grad
    residual_first_rows = jnp.sum(attn_grad, axis=1)
    attn_share_low = attn_grad.astype(jnp.bfloat16)
    attn_low = attn_share_low.reshape(-1, model_width)
    output_weight_grad = dot_first(attn_low, attended_low)
    attended_grad = (
        jnp.dot(attn_low, output_full, preferred_element_type=jnp.float32)
        .astype(jnp.bfloat16)
        .reshape(latent_count, row_count, head_count, HEAD_DIM)
    )
    latent = 0
    query_one, key_one, value_one = attend_backward(
        queries[latent],
        keys_gathered[latent].reshape(total_rows, head_count, HEAD_DIM),
        values_gathered[latent].reshape(total_rows, head_count, HEAD_DIM),
        attended_grad[latent],
        logsum_list[latent],
        score_scale,
        block_rows,
    )
    query_list = [query_one]
    key_list = [key_one.reshape(total_rows, inner_width)]
    value_list = [value_one.reshape(total_rows, inner_width)]
    key_grad_here, value_grad_here = (
        lax.psum_scatter(jnp.stack(key_list), "ctx", scatter_dimension=1, tiled=True),
        lax.psum_scatter(jnp.stack(value_list), "ctx", scatter_dimension=1, tiled=True),
    )
    query_grad_all = jnp.stack(query_list)
    key_grad_heads = key_grad_here.reshape(latent_count, row_count, head_count, HEAD_DIM)
    value_grad_heads = value_grad_here.reshape(latent_count, row_count, head_count, HEAD_DIM)
    attention_bias_grad = jnp.stack(
        [jnp.sum(query_grad_all, axis=(0, 1)), jnp.sum(value_grad_heads, axis=(0, 1))], axis=1
    ).reshape(-1)
    joint_grad = (
        jnp.stack([query_grad_all, key_grad_heads, value_grad_heads], axis=3)
        .reshape(-1, 3 * inner_width)
        .astype(jnp.bfloat16)
    )
    joint_weight_grad = dot_first(hidden_first, joint_grad)
    first_part = dot_last(joint_grad, joint_full).reshape(latent_count, row_count, model_width)
    first_input_grad = branch_total(first_part)
    shift_first_grad = jnp.sum(first_input_grad, axis=1)
    scale_first_grad = jnp.sum(first_input_grad * normed_first, axis=1)
    tokens_grad_here = middle_grad + normalize_back(
        first_input_grad * (1.0 + scale_first), normed_first, inverse_first
    )
    stat_local = jnp.concatenate(
        [
            shift_first_grad,
            scale_first_grad,
            gate_first_grad,
            shift_second_grad,
            scale_second_grad,
            gate_second_grad,
            residual_first_rows,
        ],
        axis=1,
    )
    modulation_grad = stat_local[:, : 6 * model_width]
    residual_first_grad = jnp.sum(stat_local[:, 6 * model_width :], axis=0)
    part_columns = modulate_full.shape[1]
    modulation_part_grad = lax.dynamic_slice_in_dim(
        modulation_grad, lax.axis_index("tp") * part_columns, part_columns, 1
    )
    condition_bias_grad = jnp.sum(modulation_part_grad, axis=0)
    condition_act_grad = exact_last(modulation_part_grad, modulate_full.astype(jnp.float32))
    condition_term = silu_pull(condition_act_grad)[0]
    condition_grad = lax.psum(condition_term, ("ctx", "tp"))
    modulate_local = exact_first(condition_low.astype(jnp.float32), modulation_part_grad)
    joint_sum, output_sum, expand_sum, shrink_sum, modulate_sum = (
        lax.psum_scatter(joint_weight_grad, ("fsdp", "ctx"), scatter_dimension=0, tiled=True),
        lax.psum_scatter(output_weight_grad, ("fsdp", "ctx"), scatter_dimension=0, tiled=True),
        lax.psum_scatter(expand_weight_grad, ("fsdp", "ctx"), scatter_dimension=0, tiled=True),
        lax.psum_scatter(shrink_weight_grad, ("fsdp", "ctx"), scatter_dimension=0, tiled=True),
        lax.psum_scatter(modulate_local, ("fsdp", "ctx"), scatter_dimension=0, tiled=True),
    )
    attention_sum, hidden_sum, condition_bias_sum, residual_sum = lax.psum(
        (
            attention_bias_grad,
            hidden_bias_grad,
            condition_bias_grad,
            jnp.stack([residual_first_grad, residual_second_grad]),
        ),
        ("fsdp", "ctx"),
    )
    lead_flag = (lax.axis_index(("fsdp", "ctx")) == 0).astype(jnp.float32)
    tensor_lead = (lax.axis_index("tp") == 0).astype(jnp.float32)
    weight_squares = (
        jnp.sum(joint_sum * joint_sum)
        + jnp.sum(output_sum * output_sum)
        + jnp.sum(expand_sum * expand_sum)
        + jnp.sum(shrink_sum * shrink_sum)
        + jnp.sum(modulate_sum * modulate_sum)
    )
    bias_squares = (
        jnp.sum(attention_sum * attention_sum)
        + jnp.sum(hidden_sum * hidden_sum)
        + jnp.sum(condition_bias_sum * condition_bias_sum)
        + tensor_lead * jnp.sum(residual_sum * residual_sum)
    )
    squares = lax.psum(weight_squares + lead_flag * bias_squares, ("fsdp", "ctx", "tp"))
    grad_norm = jnp.sqrt(squares)
    clip_factor = jnp.minimum(1.0, clip_limit / (grad_norm + 1e-06))
    joint_updated, joint_averages = adam_step(
        joint_weight, joint_moments, joint_sum, clip_factor, weight_decay
    )
    output_updated, output_averages = adam_step(
        output_weight, output_moments, output_sum, clip_factor, weight_decay
    )
    expand_updated, expand_averages = adam_step(
        expand_weight, expand_moments, expand_sum, clip_factor, weight_decay
    )
    shrink_updated, shrink_averages = adam_step(
        shrink_weight, shrink_moments, shrink_sum, clip_factor, weight_decay
    )
    modulate_updated, modulate_averages = adam_step(
        modulate_weight, modulate_moments, modulate_sum, clip_factor, weight_decay
    )
    attention_updated, attention_averages = adam_step(
        attention_bias, attention_moments, attention_sum, clip_factor, 0.0
    )
    hidden_updated, hidden_averages = adam_step(
        hidden_bias, hidden_moments, hidden_sum, clip_factor, 0.0
    )
    condition_updated, condition_averages = adam_step(
        condition_bias, condition_moments, condition_bias_sum, clip_factor, 0.0
    )
    residual_updated, residual_averages = adam_step(
        residual_bias, residual_moments, residual_sum, clip_factor, 0.0
    )
    return (
        mixed,
        tokens_grad_here,
        condition_grad,
        grad_norm,
        joint_updated,
        joint_averages,
        output_updated,
        output_averages,
        expand_updated,
        expand_averages,
        shrink_updated,
        shrink_averages,
        modulate_updated,
        modulate_averages,
        attention_updated,
        attention_averages,
        hidden_updated,
        hidden_averages,
        condition_updated,
        condition_averages,
        residual_updated,
        residual_averages,
    )


def solution(mesh):
    return jax.shard_map(
        local,
        mesh=mesh,
        in_specs=(
            P("fsdp", "ctx", None),
            P(),
            P("fsdp", "ctx", None),
            P(("fsdp", "ctx"), "tp"),
            P(None, ("fsdp", "ctx"), "tp"),
            P(("fsdp", "ctx"), "tp"),
            P(None, ("fsdp", "ctx"), "tp"),
            P(("fsdp", "ctx"), "tp"),
            P(None, ("fsdp", "ctx"), "tp"),
            P(("fsdp", "ctx"), "tp"),
            P(None, ("fsdp", "ctx"), "tp"),
            P(("fsdp", "ctx"), "tp"),
            P(None, ("fsdp", "ctx"), "tp"),
            P("tp"),
            P(None, "tp"),
            P("tp"),
            P(None, "tp"),
            P("tp"),
            P(None, "tp"),
            P(),
            P(),
        ),
        out_specs=(
            P("fsdp", "ctx", None),
            P("fsdp", "ctx", None),
            P("fsdp", None),
            P(),
            P(("fsdp", "ctx"), "tp"),
            P(None, ("fsdp", "ctx"), "tp"),
            P(("fsdp", "ctx"), "tp"),
            P(None, ("fsdp", "ctx"), "tp"),
            P(("fsdp", "ctx"), "tp"),
            P(None, ("fsdp", "ctx"), "tp"),
            P(("fsdp", "ctx"), "tp"),
            P(None, ("fsdp", "ctx"), "tp"),
            P(("fsdp", "ctx"), "tp"),
            P(None, ("fsdp", "ctx"), "tp"),
            P("tp"),
            P(None, "tp"),
            P("tp"),
            P(None, "tp"),
            P("tp"),
            P(None, "tp"),
            P(),
            P(),
        ),
        check_vma=False,
    )
```

profile of v0, /device:TPU:0, one launch (start us, length us, event | category | flops | bytes accessed | tf_op | source)
XLA Modules:
  0.0 1681.0 jit_solution(9704894449292168960)
XLA Ops:
  14.9 58.6 %all-gather.9.cloned.1.call-done = bf16[1024,1536]{1,0:T(8,128)(2,1)} async-done(((bf16[128,1536]{1,0:T(8,128)(2,1)}), bf16[1024,1536]{1,0:T(8,128)(2,1)}) %all-gather.9.cloned.1.call-update) | async-done | bytes 3145744 | tf_op jit(solution)/shard_map/all_gather | solution.py:179
  81.8 37.3 %all-gather.11.cloned.1.call-done = bf16[1024,768]{1,0:T(8,128)(2,1)} async-done(((bf16[128,768]{1,0:T(8,128)(2,1)}), bf16[1024,768]{1,0:T(8,128)(2,1)}) %all-gather.11.cloned.1.call-update) | async-done | bytes 1572880 | tf_op jit(solution)/shard_map/all_gather | solution.py:175
  124.5 38.0 %all_gather.29 = bf16[1024,256]{1,0:T(8,128)(2,1)} all-gather(bf16[128,256]{1,0:T(8,128)(2,1)S(1)} %convert_element_type.98), channel_id=1, replica_groups=mesh['fsdp'=2,'ctx'=4,'tp'=4] {'fsdp','ctx'}, dimensions={0}, use_global_device_ids=true | all-gather | bytes 589824 | tf_op jit(solution)/shard_map/all_gather | solution.py:176
  175.4 47.0 %all-gather.15.cloned.1.call-done = bf16[1,4096,256]{1,2,0:T(8,128)(2,1)} async-done(((bf16[1,1024,256]{1,2,0:T(8,128)(2,1)}), bf16[1,4096,256]{1,2,0:T(8,128)(2,1)}) %all-gather.15.cloned.1.call-update) | async-done | bytes 2097168 | tf_op jit(solution)/shard_map/all_gather | solution.py:215
  222.4 87.8 %while.27 = (s32[]{:T(128)}, bf16[2,512,4,64]{1,3,2,0:T(8,128)(2,1)}, f32[2,4,512,1]{2,1,3,0:T(4,128)S(1)}, bf16[2,512,4,64]{1,3,2,0:T(8,128)(2,1)S(1)}, bf16[40...) while((s32[]{:T(128)}, bf16[2,512,4,64]{1,3,2,0:T(8,128)(2,1)}, ...), condition=%wide.region_5.6_spmd, body=%wide.region_2.5_spmd.sunk | while | flops 2223110144 | bytes 113836144 | solution.py:86
  319.5 80.4 %all-reduce.6.cloned.1.call-done = f32[1,1024,1024]{2,1,0:T(8,128)} async-done(((f32[1,1024,1024]{2,1,0:T(8,128)}), f32[1,1024,1024]{2,1,0:T(8,128)}) %all-reduce.6.cloned.1.call-update) | async-done | bytes 4194320 | tf_op jit(solution)/shard_map/psum | solution.py:68
  405.5 46.2 %all-gather.17.cloned.1.call-done = bf16[1024,1024]{1,0:T(8,128)(2,1)} async-done(((bf16[128,1024]{1,0:T(8,128)(2,1)}), bf16[1024,1024]{1,0:T(8,128)(2,1)}) %all-gather.17.cloned.1.call-update) | async-done | bytes 2097168 | tf_op jit(solution)/shard_map/all_gather | solution.py:177
  459.1 43.0 %all-gather.19.cloned.1.call-done = bf16[1024,1024]{1,0:T(8,128)(2,1)} async-done(((bf16[128,1024]{1,0:T(8,128)(2,1)}), bf16[1024,1024]{1,0:T(8,128)(2,1)}) %all-gather.19.cloned.1.call-update) | async-done | bytes 2097168 | tf_op jit(solution)/shard_map/all_gather | solution.py:178
  515.7 84.1 %all-reduce.8.cloned.1.call-done = f32[1,1024,1024]{2,1,0:T(8,128)} async-done(((f32[1,1024,1024]{2,1,0:T(8,128)}), f32[1,1024,1024]{2,1,0:T(8,128)}) %all-reduce.8.cloned.1.call-update) | async-done | bytes 4194320 | tf_op jit(solution)/shard_map/psum | solution.py:68
  617.2 194.2 %while.28 = (s32[]{:T(128)}, f32[4096,4,64]{0,2,1:T(8,128)}, f32[4096,4,64]{0,2,1:T(8,128)}, f32[2,512,4,64]{1,3,2,0:T(8,128)}, bf16[2,512,4,64]{1,3,2,0:T(8,128...) while((s32[]{:T(128)}, f32[4096,4,64]{0,2,1:T(8,128)}, ...), condition=%wide.region_15.16_spmd.clone, body=%wide.region_13.15_spmd.clone.sunk | while | flops 5474744320 | bytes 351854816 | solution.py:130
  646.5 22.7 %multiply_reduce_fusion.22 = (f32[4,512]{1,0:T(4,128)S(1)}, f32[4,512,4096]{2,1,0:T(8,128)}) fusion(f32[4,512,4096]{2,1,0:T(8,128)} %fusion.174, f32[4,512]{1,0:T(4,128)S(1)} %dynamic-slice_bitcast_fusion.2, bf16[4096,4,64]{0,2,1:T(8,128)(2,1)S(1)} %copy-done.7, bf16[2,512,4,64]{1,3,2,0:T(8,128)(2,1)} %get-tuple-element.436, s32[]{:T(128)S(6)} %copy.82), kind=kOutput, calls=%fused_computation.15.clone.1 | convolution fusion | flops 1107294208 | bytes 69484544 | tf_op jit(solution)/shard_map/while/body/eval_jaxpr/qhd,khd->hqk/dot_general | solution.py:107
  669.2 27.5 %multiply_convert_fusion.6 = bf16[4,512,4096]{2,1,0:T(8,128)(2,1)} fusion(f32[4,512,4096]{2,1,0:T(8,128)} %get-tuple-element.384, f32[4,512,4096]{2,1,0:T(8,128)} %fusion.174, f32[4,512]{1,0:T(4,128)S(1)} %get-tuple-element.385, f32[4,512]{1,0:T(4,128)S(1)} %dynamic-slice_bitcast_fusion.2), kind=kLoop, calls=%fused_computation.14.clone.1 | loop fusion | flops 41943040 | bytes 83902464 | tf_op jit(solution)/shard_map/while/body/eval_jaxpr/convert_element_type | solution.py:111
  742.9 22.7 %multiply_reduce_fusion.22 = (f32[4,512]{1,0:T(4,128)S(1)}, f32[4,512,4096]{2,1,0:T(8,128)}) fusion(f32[4,512,4096]{2,1,0:T(8,128)} %fusion.174, f32[4,512]{1,0:T(4,128)S(1)} %dynamic-slice_bitcast_fusion.2, bf16[4096,4,64]{0,2,1:T(8,128)(2,1)S(1)} %copy-done.7, bf16[2,512,4,64]{1,3,2,0:T(8,128)(2,1)} %get-tuple-element.436, s32[]{:T(128)S(6)} %copy.82), kind=kOutput, calls=%fused_computation.15.clone.1 | convolution fusion | flops 1107294208 | bytes 69484544 | tf_op jit(solution)/shard_map/while/body/eval_jaxpr/qhd,khd->hqk/dot_general | solution.py:107
  765.6 27.5 %multiply_convert_fusion.6 = bf16[4,512,4096]{2,1,0:T(8,128)(2,1)} fusion(f32[4,512,4096]{2,1,0:T(8,128)} %get-tuple-element.384, f32[4,512,4096]{2,1,0:T(8,128)} %fusion.174, f32[4,512]{1,0:T(4,128)S(1)} %get-tuple-element.385, f32[4,512]{1,0:T(4,128)S(1)} %dynamic-slice_bitcast_fusion.2), kind=kLoop, calls=%fused_computation.14.clone.1 | loop fusion | flops 41943040 | bytes 83902464 | tf_op jit(solution)/shard_map/while/body/eval_jaxpr/convert_element_type | solution.py:111
  821.1 67.4 %reduce-scatter.10.cloned.1.call-done = f32[1,1024,256]{1,2,0:T(8,128)} async-done(((f32[1,4096,256]{1,2,0:T(8,128)}), f32[1,1024,256]{1,2,0:T(8,128)}) %reduce-scatter.10.cloned.1.call-update) | async-done | bytes 1048592 | tf_op jit(solution)/shard_map/reduce_scatter | solution.py:288
  888.5 79.5 %reduce-scatter.8.cloned.1.call-done = f32[1,1024,256]{1,2,0:T(8,128)} async-done(((f32[1,4096,256]{1,2,0:T(8,128)}), f32[1,1024,256]{1,2,0:T(8,128)}) %reduce-scatter.8.cloned.1.call-update) | async-done | bytes 1048592 | tf_op jit(solution)/shard_map/reduce_scatter | solution.py:287
  1004.0 124.7 %all-reduce.10.cloned.1.call-done = (f32[1,1024,1024]{2,1,0:T(8,128)}, f32[1,1024,1024]{2,1,0:T(8,128)}) async-done(((f32[1,1024,1024]{2,1,0:T(8,128)}, f32[1,1024,1024]{2,1,0:T(8,128)}), (f32[1,1024,1024]{2,1,0:T(8,128)}, f32[1,1024,1024]{2,1,0:T(8,128)})) %all-reduce.10.cloned.1.call-update) | async-done | bytes 8388624 | tf_op jit(solution)/shard_map/psum | solution.py:68
  1143.5 53.5 %reduce-scatter.14.cloned.1.call-done = f32[128,256]{1,0:T(8,128)} async-done(((f32[1024,256]{1,0:T(8,128)}), f32[128,256]{1,0:T(8,128)}) %reduce-scatter.14.cloned.1.call-update) | async-done | bytes 131088 | tf_op jit(solution)/shard_map/reduce_scatter | solution.py:334
  1198.5 89.4 %reduce-scatter.16.cloned.1.call-done = f32[128,1024]{1,0:T(8,128)} async-done(((f32[1024,1024]{1,0:T(8,128)}), f32[128,1024]{1,0:T(8,128)}) %reduce-scatter.16.cloned.1.call-update) | async-done | bytes 524304 | tf_op jit(solution)/shard_map/reduce_scatter | solution.py:335
  1289.6 89.6 %reduce-scatter.18.cloned.1.call-done = f32[128,1024]{1,0:T(8,128)} async-done(((f32[1024,1024]{1,0:T(8,128)}), f32[128,1024]{1,0:T(8,128)}) %reduce-scatter.18.cloned.1.call-update) | async-done | bytes 524304 | tf_op jit(solution)/shard_map/reduce_scatter | solution.py:336
  1382.6 37.1 %all-reduce = (f32[512]{0:T(512)S(1)}, f32[1024]{0:T(1024)S(1)}, f32[1536]{0:T(1024)S(1)}, f32[2,1024]{1,0:T(2,128)S(1)}) all-reduce(f32[512]{0:T(512)S(1)} %reshape.325, f32[1024]{0:T(1024)S(1)} %copy-done.71, f32[1536]{0:T(1024)S(1)} %dynamic-slice_reduce_fusion, ...), channel_id=1, replica_groups=mesh['fsdp'=2,'ctx'=4,'tp'=4] {'fsdp','ctx'}, use_global_device_ids=true, to_apply=%region_40.41 | all-reduce | flops 5120 | bytes 40960 | tf_op jit(solution)/shard_map/psum | solution.py:339
  1461.8 116.2 %reduce-scatter.20.cloned.1.call-done = f32[128,1536]{1,0:T(8,128)} async-done(((f32[1024,1536]{1,0:T(8,128)}), f32[128,1536]{1,0:T(8,128)}) %reduce-scatter.20.cloned.1.call-update) | async-done | bytes 786448 | tf_op jit(solution)/shard_map/reduce_scatter | solution.py:337
  1580.6 32.5 %psum.74 = f32[1,1024]{1,0:T(1,128)} all-reduce(f32[1,1024]{1,0:T(1,128)} %fusion.94), channel_id=1, replica_groups=mesh['fsdp'=2,'ctx'=4,'tp'=4] {'ctx','tp'}, use_global_device_ids=true, to_apply=%region_27.28 | all-reduce | flops 1024 | bytes 8192 | tf_op jit(solution)/shard_map/psum | solution.py:330
  1613.1 36.9 %psum.79 = f32[]{:T(128)} all-reduce(f32[]{:T(128)S(6)} %add.395), channel_id=1, replica_groups=mesh['fsdp'=2,'ctx'=4,'tp'=4] {'fsdp','ctx','tp'}, use_global_device_ids=true, to_apply=%region_51.52 | all-reduce | flops 1 | bytes 8 | tf_op jit(solution)/shard_map/psum | solution.py:363
  (320 shorter events, 396.0 us)
Async XLA Ops:
  7.2 66.3 %all-gather.9.cloned.1.call-start = ((), (), s32[]{:S(2)}) async-start(), calls=%async_computation.7 | async-start | bytes 3538944 | tf_op jit(solution)/shard_map/all_gather | solution.py:179
  9.4 109.7 %all-gather.11.cloned.1.call-start = ((), (), s32[]{:S(2)}) async-start(), calls=%async_computation.8 | async-start | bytes 1769472 | tf_op jit(solution)/shard_map/all_gather | solution.py:175
  11.1 164.3 %all-gather.13.cloned.1.call-start = ((), (), s32[]{:S(2)}) async-start(), calls=%async_computation.9 | async-start | bytes 2621440 | tf_op jit(solution)/shard_map/all_gather | solution.py:214
  123.8 98.6 %all-gather.15.cloned.1.call-start = ((), (), s32[]{:S(2)}) async-start(), calls=%async_computation.10 | async-start | bytes 2621440 | tf_op jit(solution)/shard_map/all_gather | solution.py:215
  124.4 275.5 %all-reduce.6.cloned.1.call-start = ((), (), s32[]{:S(2)}) async-start(), calls=%async_computation.11 | async-start | bytes 8388608 | tf_op jit(solution)/shard_map/psum | solution.py:68
  315.5 136.2 %all-gather.17.cloned.1.call-start = ((), (), s32[]{:S(2)}) async-start(), calls=%async_computation.12 | async-start | bytes 2359296 | tf_op jit(solution)/shard_map/all_gather | solution.py:177
  317.5 184.6 %all-gather.19.cloned.1.call-start = ((), (), s32[]{:S(2)}) async-start(), calls=%async_computation.13 | async-start | bytes 2359296 | tf_op jit(solution)/shard_map/all_gather | solution.py:178
  318.3 281.5 %all-reduce.8.cloned.1.call-start = ((), (), s32[]{:S(2)}) async-start(), calls=%async_computation.14 | async-start | bytes 8388608 | tf_op jit(solution)/shard_map/psum | solution.py:68
  402.9 202.4 %copy-start.37 = (f32[1024]{0:T(1024)}, f32[1024]{0:T(1024)S(1)}, u32[]{:S(2)}) copy-start(f32[1024]{0:T(1024)S(1)} %broadcast_multiply_fusion.5) | copy-start | bytes 12292
  515.6 372.9 %reduce-scatter.10.cloned.1.call-start = ((), (), s32[]{:S(2)}) async-start(), calls=%async_computation.16 | async-start | bytes 5242880 | tf_op jit(solution)/shard_map/reduce_scatter | solution.py:288
  811.4 156.6 %reduce-scatter.8.cloned.1.call-start = ((), (), s32[]{:S(2)}) async-start(), calls=%async_computation.15 | async-start | bytes 5242880 | tf_op jit(solution)/shard_map/reduce_scatter | solution.py:287
  812.0 316.7 %all-reduce.10.cloned.1.call-start = ((), (), s32[]{:S(2)}) async-start(), calls=%async_computation.22 | async-start | bytes 16777216 | tf_op jit(solution)/shard_map/psum | solution.py:68
  975.2 221.7 %reduce-scatter.14.cloned.1.call-start = ((), (), s32[]{:S(2)}) async-start(), calls=%async_computation.18 | async-start | bytes 1179648 | tf_op jit(solution)/shard_map/reduce_scatter | solution.py:334
  980.1 307.7 %reduce-scatter.16.cloned.1.call-start = ((), (), s32[]{:S(2)}) async-start(), calls=%async_computation.19 | async-start | bytes 4718592 | tf_op jit(solution)/shard_map/reduce_scatter | solution.py:335
  988.5 390.8 %reduce-scatter.18.cloned.1.call-start = ((), (), s32[]{:S(2)}) async-start(), calls=%async_computation.20 | async-start | bytes 4718592 | tf_op jit(solution)/shard_map/reduce_scatter | solution.py:336
  996.9 460.5 %reduce-scatter.12.cloned.1.call-start = ((), (), s32[]{:S(2)}) async-start(), calls=%async_computation.17 | async-start | bytes 3538944 | tf_op jit(solution)/shard_map/reduce_scatter | solution.py:333
  1003.9 574.1 %reduce-scatter.20.cloned.1.call-start = ((), (), s32[]{:S(2)}) async-start(), calls=%async_computation.21 | async-start | bytes 7077888 | tf_op jit(solution)/shard_map/reduce_scatter | solution.py:337
  1140.8 241.8 %copy-start.60 = (f32[1024]{0:T(1024)S(1)}, f32[1024]{0:T(1024)}, u32[]{:S(2)}) copy-start(f32[1024]{0:T(1024)} %get-tuple-element.184) | copy-start | bytes 12292
  1140.8 241.8 %copy-start.71 = (f32[1024]{0:T(1024)S(1)}, f32[1024]{0:T(1024)}, u32[]{:S(2)}) copy-start(f32[1024]{0:T(1024)} %get-tuple-element.280) | copy-start | bytes 12292
  1429.9 220.8 %copy-start.48 = (f32[1536]{0:T(1024)S(1)}, f32[1536]{0:T(1024)}, u32[]{:S(2)}) copy-start(f32[1536]{0:T(1024)} %param.42) | copy-start | bytes 18436
  1429.9 232.0 %copy-start.29 = (f32[128,768]{1,0:T(8,128)S(1)}, f32[128,768]{1,0:T(8,128)}, u32[]{:S(2)}) copy-start(f32[128,768]{1,0:T(8,128)} %param.28) | copy-start | bytes 1179652
  1435.5 229.8 %copy-start.23 = (f32[128,1024]{1,0:T(8,128)S(1)}, f32[128,1024]{1,0:T(8,128)}, u32[]{:S(2)}) copy-start(f32[128,1024]{1,0:T(8,128)} %param.34) | copy-start | bytes 1572868
  1435.5 229.8 %copy-start.26 = (f32[128,1024]{1,0:T(8,128)S(1)}, f32[128,1024]{1,0:T(8,128)}, u32[]{:S(2)}) copy-start(f32[128,1024]{1,0:T(8,128)} %reduce-scatter.18.cloned.1.call-done) | copy-start | bytes 1572868
  1435.5 229.8 %copy-start.30 = (f32[2,128,1024]{2,1,0:T(8,128)S(1)}, f32[2,128,1024]{2,1,0:T(8,128)}, u32[]{:S(2)}) copy-start(f32[2,128,1024]{2,1,0:T(8,128)} %param.35) | copy-start | bytes 3145732
  (71 other events, 1907.6 us)
Sparse Core Ops, SparseCore 0:
  10.7 62.7 all-gather.8
  76.1 42.8 all-gather.10
  124.0 51.4 all-gather.12
  177.4 44.9 all-gather.14
  315.6 84.2 all-reduce.5
  402.5 49.1 all-gather.16
  454.4 47.6 all-gather.18
  515.7 84.0 all-reduce.7
  811.5 76.9 reduce-scatter.9
  890.6 77.2 reduce-scatter.7
  975.3 153.3 all-reduce.9
  1132.6 64.3 reduce-scatter.13
  1200.6 87.2 reduce-scatter.15
  1291.3 87.8 reduce-scatter.17
  1382.7 74.7 reduce-scatter.11
  1460.9 117.0 reduce-scatter.19
where the time goes:
time: 1690 us; the launch traced here: 1680 us
  waiting for transfers between devices  1050 us (62%)
  matrix products  265 us (16%)
  other arithmetic  163 us (10%)
  blocking collectives  150 us (9%)
  local copies, waits for them, and re-layouts  25.2 us (1%)
  between operations  22.6 us (1%)
    psum x3, waiting for transfers between devices, branch_total(): return lax.psum(partial_sum, 'tp')  289 us
    reduce_scatter x1, waiting for transfers between devices, local(): lax.psum_scatter(modulate_local, ('fsdp', 'ctx'), scatter_dimension=0, ti...  116 us
    reduce_scatter x1, waiting for transfers between devices, local(): lax.psum_scatter(shrink_weight_grad, ('fsdp', 'ctx'), scatter_dimension=0...  89.6 us
    reduce_scatter x1, waiting for transfers between devices, local(): lax.psum_scatter(expand_weight_grad, ('fsdp', 'ctx'), scatter_dimension=0...  89.4 us
    reduce_scatter x1, waiting for transfers between devices, local(): lax.psum_scatter(jnp.stack(key_list), 'ctx', scatter_dimension=1, tiled=T...  79.5 us
    reduce_scatter x1, waiting for transfers between devices, local(): lax.psum_scatter(jnp.stack(value_list), 'ctx', scatter_dimension=1, tiled...  67.4 us
    all_gather x1, waiting for transfers between devices, local(): lax.all_gather(modulate_weight.astype(jnp.bfloat16), ('fsdp', 'ctx'), axi...  58.6 us
    dot_general x4, matrix products, one_block(): jnp.einsum('qhd,khd->hqk', query_block, keys_all, preferred_element_type=...  56 us
  transfers between devices with their start and end apart: 16, of which 16 were waited for; matrix products, arithmetic and copies ran while one was open for 5% of the time, Pallas kernels for 0%

commit v1 on v0

v1 whole, which is shorter than its diff:
```python
from functools import partial

import jax
import jax.numpy as jnp
from jax import lax
from jax.experimental import pallas as pl
from jax.experimental.pallas import tpu as pltpu
from jax.sharding import PartitionSpec as P

HEAD_DIM = 64
ADAM_STEP = 10
F32 = jnp.float32
BF16 = jnp.bfloat16
MESH = pl.DeviceIdType.MESH
DMA = pltpu.SemaphoreType.DMA

norm_epsilon = 1e-06
first_decay = 0.9
second_decay = 0.999
adam_epsilon = 1e-08
learning_rate = 0.05
weight_decay = 0.1
clip_limit = 1.0
GELU_SCALE = 0.7978845608028654
GELU_CUBE = 0.044715


def dot(a, b, ca, cb):
    return lax.dot_general(a, b, (((ca,), (cb,)), ((), ())), preferred_element_type=F32)


def aligned(start, size):
    return pl.ds(pl.multiple_of(start, size), size)


def greet(peers):
    barrier = pltpu.get_barrier_semaphore()
    for peer in peers:
        pl.semaphore_signal(barrier, inc=1, device_id=peer, device_id_type=MESH)
    pl.semaphore_wait(barrier, len(peers))


def remote(source, target, send_sem, recv_sem, peer):
    return pltpu.make_async_remote_copy(
        src_ref=source,
        dst_ref=target,
        send_sem=send_sem,
        recv_sem=recv_sem,
        device_id=peer,
        device_id_type=MESH,
    )


def vmem(count):
    return [pl.BlockSpec(memory_space=pltpu.VMEM)] * count


def shape(dims, dtype):
    return jax.ShapeDtypeStruct(dims, dtype)


def cost(micros, flops=0):
    return pl.CostEstimate(flops=flops, bytes_accessed=int(micros * 3.0e6), transcendentals=0)


def call(body, name, outs, scratch, ident, micros):
    def run(*args):
        return pl.pallas_call(
            body,
            out_shape=outs,
            in_specs=vmem(len(args)),
            out_specs=vmem(len(outs)),
            scratch_shapes=scratch,
            compiler_params=pltpu.CompilerParams(
                collective_id=ident, has_side_effects=True, vmem_limit_bytes=63000000
            ),
            cost_estimate=cost(micros),
            name=name,
        )(*args)

    return run


def transposed(block):
    return block.astype(F32).T.astype(BF16)


def row_of(mod, start, width, part):
    pieces = []
    for at in range(start, start + width, 128):
        pieces.append(mod[at // part, pl.ds((at % part) // 128, 1), :])
    return jnp.concatenate(pieces, axis=1)


def centred(values):
    center = values - jnp.mean(values, axis=-1, keepdims=True)
    inverse = lax.rsqrt(jnp.mean(center * center, axis=-1, keepdims=True) + norm_epsilon)
    return center * inverse, inverse


def normal_back(grad, normed, inverse):
    return inverse * (
        grad
        - jnp.mean(grad, axis=-1, keepdims=True)
        - normed * jnp.mean(grad * normed, axis=-1, keepdims=True)
    )


def tp_places():
    mine = lax.axis_index("tp")
    partner = mine + 1 - 2 * lax.rem(mine, 2)
    cross = lax.rem(mine + 2, 4)
    far = lax.rem(partner + 2, 4)
    return mine, partner, cross, far


def entry_body(
    nf, nc, tok, weight, cond, modw, cbias, offset,
    joint, hidden, weight_t, mod,
    wbuf, pbuf, pland, normed, zsend, zrecv, xsend, xrecv, psend, precv, msend, mrecv,
):
    f, c, t = lax.axis_index("fsdp"), lax.axis_index("ctx"), lax.axis_index("tp")
    group = nf * nc
    mine = f * nc + c
    rows, width = tok.shape
    part = modw.shape[1]
    strips = part // 128

    def place(offset_):
        other = lax.rem(mine + offset_, group)
        return other // nc, lax.rem(other, nc)

    peers = []
    for o in range(1, group):
        pf, pc = place(o)
        peers.append({"fsdp": pf, "ctx": pc})
    for o in range(1, 4):
        peers.append({"tp": lax.rem(t + o, 4)})
    partial_mod = dot(cond[...], modw[...].astype(BF16), 1, 0)
    for latent in range(nf):
        for k in range(strips):
            pbuf[latent, pl.ds(k, 1), :] = partial_mod[latent : latent + 1, 128 * k : 128 * k + 128]
    wbuf[mine] = weight[...].astype(BF16)
    greet(peers)
    pcopies = []
    for o in range(1, group):
        pf, pc = place(o)
        copy = remote(pbuf.at[pf], pland.at[mine], psend.at[o], precv.at[o], {"fsdp": pf, "ctx": pc})
        copy.start()
        pcopies.append(copy)
    zcopies, xcopies = [], []
    for o in range(1, nc):
        copy = remote(
            wbuf.at[mine], wbuf.at[mine], zsend.at[o], zrecv.at[o], {"ctx": lax.rem(c + o, nc)}
        )
        copy.start()
        zcopies.append(copy)

    def across(slot, o):
        for fo in range(1, nf):
            copy = remote(
                wbuf.at[slot], wbuf.at[slot], xsend.at[fo, o], xrecv.at[fo, o],
                {"fsdp": lax.rem(f + fo, nf)},
            )
            copy.start()
            xcopies.append(copy)

    across(mine, 0)
    pland[mine] = pbuf[f]
    step = 256
    for at in range(0, rows, step):
        normed[at : at + step, :] = centred(tok[at : at + step, :].astype(F32))[0]
    for o in (1, 3, 2) if nc == 4 else range(1, nc):
        zcopies[o - 1].wait_recv()
        across(f * nc + lax.rem(c - o + nc, nc), o)
    for copy in pcopies:
        copy.wait_recv()
    total = pland[0]
    for k in range(1, group):
        total = total + pland[k]
    mod[t] = total + cbias[...]
    mcopies = []
    for o in range(1, 4):
        copy = remote(
            mod.at[t], mod.at[t], msend.at[o], mrecv.at[o], {"tp": lax.rem(t + o, 4)}
        )
        copy.start()
        mcopies.append(copy)
    for copy in mcopies:
        copy.wait_recv()
    shift = row_of(mod, 0, width, part)
    scale = row_of(mod, width, width, part)
    for at in range(0, rows, step):
        hidden[at : at + step, :] = (
            normed[at : at + step, :] * (1.0 + scale) + shift
        ).astype(BF16)
    for copy in xcopies:
        copy.wait_recv()
    deep = weight.shape[0]
    for k in range(group):
        weight_t[:, k * deep : (k + 1) * deep] = transposed(wbuf[k])
    for at in range(0, rows, step):
        joint[:, at : at + step] = (
            dot(weight_t[...], hidden[at : at + step, :], 1, 1) + offset[...]
        ).astype(BF16)
    for copy in pcopies + zcopies + xcopies + mcopies:
        copy.wait_send()


def entry(nf, nc, tok, weight, cond, modw, cbias, offset):
    rows, width = tok.shape
    deep, columns = weight.shape
    group = nf * nc
    return call(
        partial(entry_body, nf, nc),
        "entry",
        (
            shape((columns, rows), BF16),
            shape((rows, width), BF16),
            shape((columns, width), BF16),
            shape((4,) + cbias.shape, F32),
        ),
        [
            pltpu.VMEM((group, deep, columns), BF16),
            pltpu.VMEM((nf,) + cbias.shape, F32),
            pltpu.VMEM((group,) + cbias.shape, F32),
            pltpu.VMEM((rows, width), F32),
            DMA((nc,)), DMA((nc,)), DMA((nf, nc)), DMA((nf, nc)),
            DMA((group,)), DMA((group,)), DMA((4,)), DMA((4,)),
        ],
        1,
        30,
    )(tok, weight, cond, modw, cbias, offset)


def attend_body(
    nc, x, att, qkv, out, lse,
    stage, land, keys, scores, send, recv, osend, orecv,
):
    c = lax.axis_index("ctx")
    rows = x.shape[1]
    total = rows * nc
    hd = HEAD_DIM
    bq, bk = scores.shape[1], 512
    per = rows // bq
    greet([{"ctx": lax.rem(c + o, nc)} for o in range(1, nc)])
    copies = []
    for o in range(1, nc):
        dst = lax.rem(c + o, nc)
        copy = remote(
            x.at[aligned(dst * 3 * hd, 3 * hd), :], qkv.at[:, aligned(c * rows, rows)],
            send.at[o], recv.at[o], {"ctx": dst},
        )
        copy.start()
        copies.append(copy)
    qkv[:, aligned(c * rows, rows)] = x[aligned(c * 3 * hd, 3 * hd), :]
    for copy in copies:
        copy.wait_recv()
    for at in range(0, total, 1024):
        keys[at : at + 1024, :] = transposed(qkv[hd : 2 * hd, at : at + 1024])

    def block(i, carry):
        o = 1 + i // per
        owner = lax.rem(c + o, nc)
        sub = lax.rem(i, per)
        where = aligned(owner * rows + sub * bq, bq)
        query = qkv[0:hd, where] * BF16(hd**-0.5)
        peak = None
        for at in range(0, total, bk):
            s = dot(keys[at : at + bk, :], query, 1, 0)
            scores[at : at + bk, :] = s
            high = jnp.max(s.reshape(bk // 8, 8, bq), axis=0)
            peak = high if peak is None else jnp.maximum(peak, high)
        peak = jnp.max(peak, axis=0, keepdims=True)
        acc, mass = None, None
        for at in range(0, total, bk):
            p = jnp.exp(scores[at : at + bk, :] - peak)
            low = jnp.sum(p.reshape(bk // 8, 8, bq), axis=0)
            mass = low if mass is None else mass + low
            term = dot(qkv[2 * hd : 3 * hd, at : at + bk], p.astype(BF16), 1, 0)
            acc = term if acc is None else acc + term
        mass = jnp.sum(mass, axis=0, keepdims=True)
        acc = acc * (1.0 / mass)
        out[:, where] = acc
        lse[:, where] = peak + jnp.log(mass)
        stage[owner, :, aligned(sub * bq, bq)] = acc.astype(BF16)

        @pl.when(jnp.logical_and(sub == per - 1, o < nc))
        def _():
            remote(
                stage.at[owner], land.at[c], osend.at[o], orecv.at[o], {"ctx": owner}
            ).start()

        return carry

    lax.fori_loop(0, per * nc, block, 0)
    land[c] = stage[c]
    for o in range(1, nc):
        dst = lax.rem(c + o, nc)
        copy = remote(stage.at[dst], land.at[c], osend.at[o], orecv.at[o], {"ctx": dst})
        copy.wait_recv()
        copy.wait_send()
    for k in range(nc):
        att[k * hd : (k + 1) * hd, :] = land[k]
    for copy in copies:
        copy.wait_send()


def attend(nc, x):
    rows = x.shape[1]
    total = rows * nc
    hd = HEAD_DIM
    bq = min(512, rows)
    return call(
        partial(attend_body, nc),
        "attend",
        (
            shape((nc * hd, rows), BF16),
            shape((3 * hd, total), BF16),
            shape((hd, total), F32),
            shape((1, total), F32),
        ),
        [
            pltpu.VMEM((nc, hd, rows), BF16),
            pltpu.VMEM((nc, hd, rows), BF16),
            pltpu.VMEM((total, hd), BF16),
            pltpu.VMEM((total, bq), F32),
            DMA((nc,)), DMA((nc,)), DMA((nc,)), DMA((nc,)),
        ],
        2,
        70,
    )(x)


def project_body(
    att, weight, tok, mod, bias,
    value, middle, hidden,
    sbuf, rbuf, send, recv, gsend, grecv,
):
    mine, partner, cross, far = tp_places()
    own = value.shape[0]
    width = tok.shape[1]
    part = mod.shape[1] * 128
    att_t = [None]

    def piece(at):
        return dot(
            att[:, aligned(at * own, own)].astype(F32).T.astype(BF16), weight[...], 1, 1
        )

    greet([{"tp": lax.rem(mine + o, 4)} for o in range(1, 4)])
    sbuf[0] = piece(far).astype(BF16)
    first = remote(sbuf.at[0], rbuf.at[0], send.at[0], recv.at[0], {"tp": partner})
    first.start()
    sbuf[1] = piece(partner).astype(BF16)
    second = remote(sbuf.at[1], rbuf.at[1], send.at[1], recv.at[1], {"tp": partner})
    second.start()
    crossing = piece(cross)
    first.wait_recv()
    sbuf[2] = (crossing + rbuf[0].astype(F32)).astype(BF16)
    third = remote(sbuf.at[2], rbuf.at[2], send.at[2], recv.at[2], {"tp": cross})
    third.start()
    held = piece(mine)
    second.wait_recv()
    held = held + rbuf[1].astype(F32) + bias[0:1, :]
    third.wait_recv()
    held = held + rbuf[2].astype(F32)
    value[...] = held
    gate = row_of(mod, 2 * width, width, part)
    shift = row_of(mod, 3 * width, width, part)
    scale = row_of(mod, 4 * width, width, part)
    mid = tok[aligned(mine * own, own), :].astype(F32) + gate * held
    middle[...] = mid
    hidden[mine] = (centred(mid)[0] * (1.0 + scale) + shift).astype(BF16)
    copies = gather_start(hidden, mine, partner, cross, gsend, grecv)
    gather_end(hidden, copies, mine, partner, cross, gsend, grecv)
    for copy in (first, second, third):
        copy.wait_send()


def gather_start(slots, mine, partner, cross, send, recv):
    over = remote(slots.at[mine], slots.at[mine], send.at[0], recv.at[0], {"tp": cross})
    over.start()
    near = remote(slots.at[mine], slots.at[mine], send.at[1], recv.at[1], {"tp": partner})
    near.start()
    return over, near


def gather_end(slots, copies, mine, partner, cross, send, recv):
    over, near = copies
    over.wait_recv()
    relay = remote(slots.at[cross], slots.at[cross], send.at[2], recv.at[2], {"tp": partner})
    relay.start()
    near.wait_recv()
    relay.wait_recv()
    for copy in (over, near, relay):
        copy.wait_send()


def project(att, weight, tok, mod, bias):
    rows, width = tok.shape
    own = rows // 4
    return call(
        project_body,
        "project",
        (shape((own, width), F32), shape((own, width), F32), shape((4, own, width), BF16)),
        [
            pltpu.VMEM((3, own, width), BF16),
            pltpu.VMEM((3, own, width), BF16),
            DMA((3,)), DMA((3,)), DMA((3,)), DMA((3,)),
        ],
        3,
        36,
    )(att, weight, tok, mod, bias)


def branch_body(
    hidden, cot, expand, shrink, hbias, mod, middle, value,
    attn_low, mid_grad, shrink_grad, expand_grad, stats, hstats, sh_cross, sh_own,
    gbuf, abuf, ebuf, sbuf, rbuf, shold, tsend, trecv, send, recv, gsend, grecv,
):
    mine, partner, cross, far = tp_places()
    own, width = middle.shape
    part = mod.shape[1] * 128
    gate_first = row_of(mod, 2 * width, width, part)
    scale_second = row_of(mod, 4 * width, width, part)
    gate_second = row_of(mod, 5 * width, width, part)
    greet([{"tp": lax.rem(mine + o, 4)} for o in range(1, 4)])
    column = None
    copies = []
    held = None
    for turn, at in enumerate((far, partner, cross, mine)):
        where = aligned(at * own, own)
        grad = gate_second * cot[where, :].astype(F32)
        low = grad.astype(BF16)
        gbuf[where, :] = low
        if turn == 3:
            stats[3:4, :] = jnp.sum(grad, axis=0, keepdims=True)
        u = dot(hidden[at], expand[...], 1, 0) + hbias[...]
        squared = u * u
        th = jnp.tanh(GELU_SCALE * (u + GELU_CUBE * squared * u))
        act = (0.5 * u * (1.0 + th)).astype(BF16)
        abuf[where, :] = act
        slope = 0.5 * (1.0 + th) + 0.5 * u * (1.0 - th * th) * (
            GELU_SCALE * (1.0 + 3.0 * GELU_CUBE * squared)
        )
        pull = dot(low, shrink[...], 1, 0) * slope
        tally = jnp.sum(pull, axis=0, keepdims=True)
        column = tally if column is None else column + tally
        pull = pull.astype(BF16)
        ebuf[where, :] = pull
        back = dot(pull, expand[...], 1, 1)
        forth = dot(act, shrink[...], 1, 1)
        if turn < 2:
            sbuf[turn] = back.astype(BF16)
            copy = remote(sbuf.at[turn], rbuf.at[turn], send.at[turn], recv.at[turn], {"tp": partner})
            copy.start()
            copies.append(copy)
            shold[turn] = forth.astype(BF16)
            copy = remote(
                shold.at[turn], shold.at[2 + turn], tsend.at[turn], trecv.at[turn], {"tp": partner}
            )
            copy.start()
            copies.append(copy)
        elif turn == 2:
            copies[0].wait_recv()
            sbuf[2] = (back + rbuf[0].astype(F32)).astype(BF16)
            third = remote(sbuf.at[2], rbuf.at[2], send.at[2], recv.at[2], {"tp": cross})
            third.start()
            copies[1].wait_recv()
            sh_cross[...] = (forth + shold[2].astype(F32)).astype(BF16)
        else:
            copies[2].wait_recv()
            held = back + rbuf[1].astype(F32)
            copies[3].wait_recv()
            sh_own[...] = forth + shold[3].astype(F32)
    hstats[...] = column
    step = 256
    for at in range(0, width, step):
        shrink_grad[at : at + step, :] = dot(
            gbuf[:, at : at + step], abuf[...], 0, 0
        ).astype(BF16)
    third.wait_recv()
    grad_in = held + rbuf[2].astype(F32)
    normed, inverse = centred(middle[...])
    stats[0:1, :] = jnp.sum(grad_in, axis=0, keepdims=True)
    stats[1:2, :] = jnp.sum(grad_in * normed, axis=0, keepdims=True)
    mgrad = cot[aligned(mine * own, own), :].astype(F32) + normal_back(
        grad_in * (1.0 + scale_second), normed, inverse
    )
    mid_grad[...] = mgrad
    agrad = gate_first * mgrad
    attn_low[mine] = agrad.astype(BF16)
    gathers = gather_start(attn_low, mine, partner, cross, gsend, grecv)
    stats[2:3, :] = jnp.sum(mgrad * value[...], axis=0, keepdims=True)
    stats[4:5, :] = jnp.sum(agrad, axis=0, keepdims=True)
    stats[5:8, :] = jnp.zeros((3, width), F32)
    flat = hidden.shape[0] * own
    for at in range(0, width, step):
        expand_grad[at : at + step, :] = dot(
            hidden[:, :, at : at + step].reshape(flat, step), ebuf[...], 0, 0
        ).astype(BF16)
    gather_end(attn_low, gathers, mine, partner, cross, gsend, grecv)
    for copy in copies + [third]:
        copy.wait_send()


def branch(hidden, cot, expand, shrink, hbias, mod, middle, value):
    rows, width = cot.shape
    own = rows // 4
    units = expand.shape[1]
    return call(
        branch_body,
        "branch",
        (
            shape((4, own, width), BF16),
            shape((own, width), F32),
            shape((width, units), BF16),
            shape((width, units), BF16),
            shape((8, width), F32),
            shape((1, units), F32),
            shape((own, width), BF16),
            shape((own, width), F32),
        ),
        [
            pltpu.VMEM((rows, width), BF16),
            pltpu.VMEM((rows, units), BF16),
            pltpu.VMEM((rows, units), BF16),
            pltpu.VMEM((3, own, width), BF16),
            pltpu.VMEM((3, own, width), BF16),
            pltpu.VMEM((4, own, width), BF16),
            DMA((2,)), DMA((2,)), DMA((3,)), DMA((3,)), DMA((3,)), DMA((3,)),
        ],
        4,
        45,
    )(hidden, cot, expand, shrink, hbias, mod, middle, value)


def retreat_body(
    nc, attn_low, weight, att, qkv, out, lse, sh_cross, sh_own, middle, cot, mod, bias,
    joint_grad, weight_grad, bias_grad, mixed, gate_grad,
    dout, dost, keys, vals, dq, stage, rland, wt, delta, send, recv, jsend, jrecv,
    csend, crecv, gsend, grecv,
):
    c = lax.axis_index("ctx")
    mine, partner, cross, far = tp_places()
    own, width = middle.shape
    rows = att.shape[1]
    total = rows * nc
    hd = HEAD_DIM
    bk = bq = 512
    per = rows // bk
    part = mod.shape[1] * 128
    wt[...] = transposed(weight[...])
    low = attn_low[...].reshape(rows, width)
    dost[...] = dot(wt[...], low, 1, 1).astype(BF16)
    greet(
        [{"ctx": lax.rem(c + o, nc)} for o in range(1, nc)]
        + [{"tp": lax.rem(mine + o, 4)} for o in range(1, 4)]
    )
    copies = []
    for o in range(1, nc):
        dst = lax.rem(c + o, nc)
        copy = remote(
            dost.at[aligned(dst * hd, hd), :], dout.at[:, aligned(c * rows, rows)],
            send.at[o], recv.at[o], {"ctx": dst},
        )
        copy.start()
        copies.append(copy)
    crossing = remote(sh_cross, rland, csend, crecv, {"tp": cross})
    crossing.start()
    dout[:, aligned(c * rows, rows)] = dost[aligned(c * hd, hd), :]
    weight_grad[...] = dot(att[...], low, 1, 0).T.astype(BF16)
    for at in range(0, total, 1024):
        keys[at : at + 1024, :] = transposed(qkv[hd : 2 * hd, at : at + 1024])
        vals[at : at + 1024, :] = transposed(qkv[2 * hd : 3 * hd, at : at + 1024])
    dq[...] = jnp.zeros_like(dq)
    for copy in copies:
        copy.wait_recv()
    for at in range(0, total, 1024):
        delta[:, at : at + 1024] = jnp.sum(
            dout[:, at : at + 1024].astype(F32) * out[:, at : at + 1024], axis=0, keepdims=True
        )
    vsum_start = jnp.zeros((hd, 1), F32)

    def block(i, vsum):
        o = 1 + i // per
        owner = lax.rem(c + o, nc)
        sub = lax.rem(i, per)
        where = aligned(owner * rows + sub * bk, bk)
        key, val, key_t = keys[where, :], vals[where, :], qkv[hd : 2 * hd, where]
        dk, dv = None, None
        for at in range(0, total, bq):
            query = qkv[0:hd, at : at + bq] * BF16(hd**-0.5)
            grad = dout[:, at : at + bq]
            p = jnp.exp(dot(key, query, 1, 0) - lse[:, at : at + bq])
            ds = (p * (dot(val, grad, 1, 0) - delta[:, at : at + bq])).astype(BF16)
            tv = dot(grad, p.astype(BF16), 1, 1)
            tk = dot(query, ds, 1, 1)
            dv = tv if dv is None else dv + tv
            dk = tk if dk is None else dk + tk
            dq[:, at : at + bq] += dot(key_t, ds, 1, 0)
        put = aligned(sub * bk, bk)
        stage[owner, hd : 2 * hd, put] = dk.astype(BF16)
        stage[owner, 2 * hd : 3 * hd, put] = dv.astype(BF16)

        @pl.when(jnp.logical_and(sub == per - 1, o < nc))
        def _():
            remote(
                stage.at[owner, pl.ds(hd, 2 * hd), :], joint_grad.at[c, pl.ds(hd, 2 * hd), :],
                jsend.at[0, o], jrecv.at[0, o], {"ctx": owner},
            ).start()

        @pl.when(i == 2)
        def _():
            crossing.wait_recv()
            value = sh_own[...] + rland[...].astype(F32) + bias[1:2, :]
            gate = row_of(mod, 5 * width, width, part)
            mixed[mine] = (middle[...] + gate * value).astype(BF16)
            gather_start(mixed, mine, partner, cross, gsend, grecv)
            gate_grad[...] = jnp.sum(
                cot[aligned(mine * own, own), :].astype(F32) * value, axis=0, keepdims=True
            )

        return vsum + jnp.sum(dv, axis=1, keepdims=True)

    vsum = lax.fori_loop(0, per * nc, block, vsum_start)
    qsum = jnp.zeros((hd, 1), F32)
    dqs = []
    for o in range(1, nc + 1):
        owner = lax.rem(c + o, nc)
        piece = dq[:, aligned(owner * rows, rows)] * (hd**-0.5)
        qsum = qsum + jnp.sum(piece, axis=1, keepdims=True)
        stage[owner, 0:hd, :] = piece.astype(BF16)
        if o < nc:
            copy = remote(
                stage.at[owner, pl.ds(0, hd), :], joint_grad.at[c, pl.ds(0, hd), :],
                jsend.at[1, o], jrecv.at[1, o], {"ctx": owner},
            )
            copy.start()
            dqs.append(copy)
    joint_grad[c] = stage[c]
    bias_grad[0:hd, :] = jnp.broadcast_to(qsum, (hd, 128))
    bias_grad[hd : 2 * hd, :] = jnp.broadcast_to(vsum, (hd, 128))
    over = remote(mixed.at[mine], mixed.at[mine], gsend.at[0], grecv.at[0], {"tp": cross})
    near = remote(mixed.at[mine], mixed.at[mine], gsend.at[1], grecv.at[1], {"tp": partner})
    gather_end(mixed, (over, near), mine, partner, cross, gsend, grecv)
    for o in range(1, nc):
        dst = lax.rem(c + o, nc)
        copy = remote(
            stage.at[dst, pl.ds(hd, 2 * hd), :], joint_grad.at[c, pl.ds(hd, 2 * hd), :],
            jsend.at[0, o], jrecv.at[0, o], {"ctx": dst},
        )
        copy.wait_recv()
        copy.wait_send()
        dqs[o - 1].wait_recv()
        dqs[o - 1].wait_send()
    for copy in copies + [crossing]:
        copy.wait_send()


def retreat(nc, attn_low, weight, att, qkv, out, lse, sh_cross, sh_own, middle, cot, mod, bias):
    rows, width = cot.shape
    own = rows // 4
    total = rows * nc
    hd = HEAD_DIM
    return call(
        partial(retreat_body, nc),
        "retreat",
        (
            shape((nc, 3 * hd, rows), BF16),
            shape((width, nc * hd), BF16),
            shape((2 * hd, 128), F32),
            shape((4, own, width), BF16),
            shape((1, width), F32),
        ),
        [
            pltpu.VMEM((hd, total), BF16),
            pltpu.VMEM((nc * hd, rows), BF16),
            pltpu.VMEM((total, hd), BF16),
            pltpu.VMEM((total, hd), BF16),
            pltpu.VMEM((hd, total), F32),
            pltpu.VMEM((nc, 3 * hd, rows), BF16),
            pltpu.VMEM((own, width), BF16),
            pltpu.VMEM((nc * hd, width), BF16),
            pltpu.VMEM((1, total), F32),
            DMA((nc,)), DMA((nc,)), DMA((2, nc)), DMA((2, nc)),
            DMA, DMA, DMA((3,)), DMA((3,)),
        ],
        5,
        100,
    )(attn_low, weight, att, qkv, out, lse, sh_cross, sh_own, middle, cot, mod, bias)


def leave_body(
    joint_grad, weight_t, hidden, tok, mid_grad, mod,
    weight_grad, tokens_grad, stats,
    sbuf, rbuf, send, recv, gsend, grecv,
):
    mine, partner, cross, far = tp_places()
    own, width = mid_grad.shape
    part = mod.shape[1] * 128
    columns = weight_t.shape[0]

    def piece(at):
        block = joint_grad[:, :, aligned(at * own, own)].reshape(columns, own)
        return dot(block.astype(F32).T.astype(BF16), weight_t[...], 1, 0)

    greet([{"tp": lax.rem(mine + o, 4)} for o in range(1, 4)])
    sbuf[0] = piece(far).astype(BF16)
    first = remote(sbuf.at[0], rbuf.at[0], send.at[0], recv.at[0], {"tp": partner})
    first.start()
    sbuf[1] = piece(partner).astype(BF16)
    second = remote(sbuf.at[1], rbuf.at[1], send.at[1], recv.at[1], {"tp": partner})
    second.start()
    crossing = piece(cross)
    first.wait_recv()
    sbuf[2] = (crossing + rbuf[0].astype(F32)).astype(BF16)
    third = remote(sbuf.at[2], rbuf.at[2], send.at[2], recv.at[2], {"tp": cross})
    third.start()
    held = piece(mine)
    second.wait_recv()
    held = held + rbuf[1].astype(F32)
    normed, inverse = centred(tok[aligned(mine * own, own), :].astype(F32))
    flat = joint_grad[...].reshape(columns, tok.shape[0])
    step = 256
    for at in range(0, width, step):
        weight_grad[at : at + step, :] = dot(flat, hidden[:, at : at + step], 1, 0).T.astype(BF16)
    third.wait_recv()
    grad_in = held + rbuf[2].astype(F32)
    scale = row_of(mod, width, width, part)
    stats[0:1, :] = jnp.sum(grad_in, axis=0, keepdims=True)
    stats[1:2, :] = jnp.sum(grad_in * normed, axis=0, keepdims=True)
    stats[2:8, :] = jnp.zeros((6, width), F32)
    tokens_grad[mine] = (
        mid_grad[...] + normal_back(grad_in * (1.0 + scale), normed, inverse)
    ).astype(BF16)
    copies = gather_start(tokens_grad, mine, partner, cross, gsend, grecv)
    gather_end(tokens_grad, copies, mine, partner, cross, gsend, grecv)
    for copy in (first, second, third):
        copy.wait_send()


def leave(joint_grad, weight_t, hidden, tok, mid_grad, mod):
    rows, width = tok.shape
    own = rows // 4
    return call(
        leave_body,
        "leave",
        (
            shape((width, weight_t.shape[0]), BF16),
            shape((4, own, width), BF16),
            shape((8, width), F32),
        ),
        [
            pltpu.VMEM((3, own, width), BF16),
            pltpu.VMEM((3, own, width), BF16),
            DMA((3,)), DMA((3,)), DMA((3,)), DMA((3,)),
        ],
        6,
        36,
    )(joint_grad, weight_t, hidden, tok, mid_grad, mod)


def tally_body(nf, nc, pieces, gathered, land, total, asend, arecv, bsend, brecv):
    f, c, t = lax.axis_index("fsdp"), lax.axis_index("ctx"), lax.axis_index("tp")
    inner = nc * 4
    group = nf * nc
    here = c * 4 + t
    mine = f * nc + c
    peers = []
    for o in range(1, inner):
        other = lax.rem(here + o, inner)
        peers.append({"ctx": other // 4, "tp": lax.rem(other, 4)})
    outer = []
    for o in range(1, group):
        other = lax.rem(mine + o, group)
        outer.append({"fsdp": other // nc, "ctx": lax.rem(other, nc)})
    greet(peers + outer)
    copies = []
    for o in range(1, inner):
        other = lax.rem(here + o, inner)
        copy = remote(pieces.at[other], land.at[here], asend.at[o], arecv.at[o], peers[o - 1])
        copy.start()
        copies.append(copy)
    land[here] = pieces[here]
    for copy in copies:
        copy.wait_recv()
    acc = land[0]
    for k in range(1, inner):
        acc = acc + land[k]
    total[...] = acc
    gathered[mine] = acc
    second = []
    for o in range(1, group):
        copy = remote(total, gathered.at[mine], bsend.at[o], brecv.at[o], outer[o - 1])
        copy.start()
        second.append(copy)
    for copy in second:
        copy.wait_recv()
    for copy in copies + second:
        copy.wait_send()


def tally(nf, nc, pieces):
    inner, high, lanes = pieces.shape
    group = nf * nc
    return call(
        partial(tally_body, nf, nc),
        "tally",
        (shape((group, high, lanes), F32),),
        [
            pltpu.VMEM((inner, high, lanes), F32),
            pltpu.VMEM((high, lanes), F32),
            DMA((inner,)), DMA((inner,)), DMA((group,)), DMA((group,)),
        ],
        7,
        12,
    )(pieces)[0]


def finish_body(nf, nc, piece, gathered, land, total, asend, arecv, bsend, brecv):
    f, c, t = lax.axis_index("fsdp"), lax.axis_index("ctx"), lax.axis_index("tp")
    group = nf * nc
    mine = f * nc + c
    peers = [{"tp": lax.rem(t + o, 4)} for o in range(1, 4)]
    outer = []
    for o in range(1, group):
        other = lax.rem(mine + o, group)
        outer.append({"fsdp": other // nc, "ctx": lax.rem(other, nc)})
    greet(peers + outer)
    copies = []
    for o in range(1, 4):
        copy = remote(piece, land.at[t], asend.at[o], arecv.at[o], peers[o - 1])
        copy.start()
        copies.append(copy)
    land[t] = piece[...]
    for copy in copies:
        copy.wait_recv()
    acc = land[0] + land[1] + land[2] + land[3]
    total[...] = acc
    gathered[mine] = acc
    second = []
    for o in range(1, group):
        copy = remote(total, gathered.at[mine], bsend.at[o], brecv.at[o], outer[o - 1])
        copy.start()
        second.append(copy)
    for copy in second:
        copy.wait_recv()
    for copy in copies + second:
        copy.wait_send()


def finish(nf, nc, piece):
    high, lanes = piece.shape
    group = nf * nc
    return call(
        partial(finish_body, nf, nc),
        "finish",
        (shape((group, high, lanes), F32),),
        [
            pltpu.VMEM((4, high, lanes), F32),
            pltpu.VMEM((high, lanes), F32),
            DMA((4,)), DMA((4,)), DMA((group,)), DMA((group,)),
        ],
        8,
        10,
    )(piece)[0]


def adam_step(master, moments, gradient, clip_factor, decay_rate):
    scaled = clip_factor * gradient
    first_moment = first_decay * moments[0] + (1.0 - first_decay) * scaled
    second_moment = second_decay * moments[1] * moments[1] + (1.0 - second_decay) * scaled * scaled
    first_hat = first_moment / (1.0 - first_decay**ADAM_STEP)
    second_hat = second_moment / (1.0 - second_decay**ADAM_STEP)
    updated = master - learning_rate * (
        first_hat / (jnp.sqrt(second_hat) + adam_epsilon) + decay_rate * master
    )
    return (updated, jnp.stack([first_moment, jnp.sqrt(second_moment)]))


def local(
    nf,
    nc,
    tokens,
    condition,
    cotangent,
    joint_weight,
    joint_moments,
    output_weight,
    output_moments,
    expand_weight,
    expand_moments,
    shrink_weight,
    shrink_moments,
    modulate_weight,
    modulate_moments,
    attention_bias,
    attention_moments,
    hidden_bias,
    hidden_moments,
    condition_bias,
    condition_moments,
    residual_bias,
    residual_moments,
):
    latent_count, rows, width = tokens.shape
    heads = joint_weight.shape[1] // (3 * HEAD_DIM)
    assert latent_count == 1 and heads == nc and lax.axis_size("tp") == 4
    f, c, t = lax.axis_index("fsdp"), lax.axis_index("ctx"), lax.axis_index("tp")
    mine = f * nc + c
    deep, part = modulate_weight.shape
    units = expand_weight.shape[1]
    tok, cot = tokens[0], cotangent[0]

    def gather(weight):
        return lax.all_gather(weight.astype(BF16), ("fsdp", "ctx"), axis=0, tiled=True)

    output_full, expand_full, shrink_full = (
        gather(output_weight), gather(expand_weight), gather(shrink_weight)
    )

    condition_act, silu_pull = jax.vjp(jax.nn.silu, condition)
    condition_low = condition_act.astype(BF16)
    condition_here = lax.dynamic_slice_in_dim(condition_low, mine * deep, deep, 1)
    condition_pad = jnp.pad(condition_here, ((0, 16 - nf), (0, 0)))
    strips = part // 128
    high = -(-strips // 8) * 8
    bias_strips = jnp.pad(condition_bias.reshape(strips, 128), ((0, high - strips), (0, 0)))
    bias_pairs = attention_bias.reshape(heads, 2, HEAD_DIM)
    offset = jnp.stack(
        [bias_pairs[:, 0], jnp.zeros_like(bias_pairs[:, 0]), bias_pairs[:, 1]], axis=1
    ).reshape(-1, 1)
    joint_t, hidden_first, joint_full_t, mod = entry(
        nf, nc, tok, joint_weight, condition_pad, modulate_weight, bias_strips, offset
    )
    mod = mod[:, :strips]
    att_t, qkv, out, lse = attend(nc, joint_t)
    value, middle, hidden_second = project(att_t, output_full, tok, mod, residual_bias)
    (
        attn_low, mid_grad, shrink_grad, expand_grad, stats_second, hidden_stats, sh_cross, sh_own,
    ) = branch(
        hidden_second, cot, expand_full, shrink_full, hidden_bias[None, :], mod, middle, value
    )

    def scatter(grad):
        return lax.psum_scatter(
            grad, ("fsdp", "ctx"), scatter_dimension=0, tiled=True
        ).astype(F32)

    shrink_sum, expand_sum = scatter(shrink_grad), scatter(expand_grad)
    joint_grad, output_grad, head_bias, mixed, gate_second_grad = retreat(
        nc, attn_low, output_full, att_t, qkv, out, lse, sh_cross, sh_own, middle, cot, mod,
        residual_bias,
    )
    output_sum = scatter(output_grad)
    joint_weight_grad, tokens_grad, stats_first = leave(
        joint_grad, joint_full_t, hidden_first, tok, mid_grad, mod
    )
    joint_sum = scatter(joint_weight_grad)

    stats = jnp.stack(
        [
            stats_first[0], stats_first[1], stats_second[2],
            stats_second[0], stats_second[1], gate_second_grad[0],
        ]
    ).reshape(4, nc, part // nc // 128, 128)
    stats = stats.transpose(1, 0, 2, 3).reshape(nc * 4, -1, 128)
    residual = jnp.stack([stats_second[4], stats_second[3]]).reshape(nc, -1, 128)
    residual = jnp.repeat(residual, 4, axis=0)
    same = (jnp.arange(4) == t).astype(F32)[None, :, None, None]
    hidden_piece = (hidden_stats.reshape(nc, 1, -1, 128) * same).reshape(nc * 4, -1, 128)
    exact = (jnp.arange(nc * 4) == c * 4 + t).astype(F32)[:, None, None]
    head_piece = head_bias[:, 0].reshape(1, -1, 128) * exact
    pieces = jnp.concatenate([stats, residual, hidden_piece, head_piece], axis=1)
    counts = [stats.shape[1], residual.shape[1], hidden_piece.shape[1], head_piece.shape[1]]
    used = sum(counts)
    pieces = jnp.pad(pieces, ((0, 0), (0, -(-used // 8) * 8 - used), (0, 0)))
    sums = tally(nf, nc, pieces).reshape(nf, nc, -1, 128)
    edge = [0]
    for count in counts:
        edge.append(edge[-1] + count)
    modulation_grad = sums[:, :, edge[0] : edge[1]].reshape(nf, part)
    residual_sum = jnp.sum(sums[:, :, edge[1] : edge[2]], axis=0).reshape(2, width)
    hidden_sum = jnp.sum(sums[:, :, edge[2] : edge[3]], axis=0).reshape(units)
    attention_sum = jnp.sum(sums[:, :, edge[3] : edge[4]], axis=0).reshape(-1)
    condition_bias_sum = jnp.sum(modulation_grad, axis=0)
    low_rows = condition_here.astype(F32)
    if nf <= 4:
        modulate_sum = sum(
            low_rows[k][:, None] * modulation_grad[k][None, :] for k in range(nf)
        )
        wide = modulate_weight.astype(BF16).astype(F32)
        condition_part = jnp.stack(
            [jnp.sum(wide * modulation_grad[k][None, :], axis=1) for k in range(nf)]
        )
    else:
        modulate_sum = lax.dot_general(
            low_rows, modulation_grad, (((0,), (0,)), ((), ())),
            precision=lax.Precision.HIGHEST, preferred_element_type=F32,
        )
        condition_part = lax.dot_general(
            modulation_grad, modulate_weight.astype(BF16).astype(F32), (((1,), (1,)), ((), ())),
            precision=lax.Precision.HIGHEST, preferred_element_type=F32,
        )
    lead_flag = (mine == 0).astype(F32)
    tensor_lead = (t == 0).astype(F32)
    weight_squares = (
        jnp.sum(joint_sum * joint_sum)
        + jnp.sum(output_sum * output_sum)
        + jnp.sum(expand_sum * expand_sum)
        + jnp.sum(shrink_sum * shrink_sum)
        + jnp.sum(modulate_sum * modulate_sum)
    )
    bias_squares = (
        jnp.sum(attention_sum * attention_sum)
        + jnp.sum(hidden_sum * hidden_sum)
        + jnp.sum(condition_bias_sum * condition_bias_sum)
        + tensor_lead * jnp.sum(residual_sum * residual_sum)
    )
    squares_part = weight_squares + lead_flag * bias_squares
    tall = -(-(nf + 1) // 8) * 8
    lanes = max(128, deep)
    piece = jnp.concatenate(
        [
            jnp.pad(condition_part, ((0, 0), (0, lanes - deep))),
            jnp.full((1, lanes), squares_part),
            jnp.zeros((tall - nf - 1, lanes), F32),
        ]
    )
    done = finish(nf, nc, piece)
    squares = jnp.sum(done[:, nf, 0])
    grad_norm = jnp.sqrt(squares)
    clip_factor = jnp.minimum(1.0, clip_limit / (grad_norm + 1e-06))
    condition_act_grad = lax.dynamic_slice_in_dim(done, f, 1, 1)[:, 0, :deep].reshape(1, -1)
    condition_all = jnp.broadcast_to(condition_act_grad, condition.shape)
    condition_grad = lax.dynamic_slice_in_dim(silu_pull(condition_all)[0], f, 1, 0)

    joint_updated, joint_averages = adam_step(
        joint_weight, joint_moments, joint_sum, clip_factor, weight_decay
    )
    output_updated, output_averages = adam_step(
        output_weight, output_moments, output_sum, clip_factor, weight_decay
    )
    expand_updated, expand_averages = adam_step(
        expand_weight, expand_moments, expand_sum, clip_factor, weight_decay
    )
    shrink_updated, shrink_averages = adam_step(
        shrink_weight, shrink_moments, shrink_sum, clip_factor, weight_decay
    )
    modulate_updated, modulate_averages = adam_step(
        modulate_weight, modulate_moments, modulate_sum, clip_factor, weight_decay
    )
    attention_updated, attention_averages = adam_step(
        attention_bias, attention_moments, attention_sum, clip_factor, 0.0
    )
    hidden_updated, hidden_averages = adam_step(
        hidden_bias, hidden_moments, hidden_sum, clip_factor, 0.0
    )
    condition_updated, condition_averages = adam_step(
        condition_bias, condition_moments, condition_bias_sum, clip_factor, 0.0
    )
    residual_updated, residual_averages = adam_step(
        residual_bias, residual_moments, residual_sum, clip_factor, 0.0
    )
    return (
        mixed.reshape(1, rows, width),
        tokens_grad.reshape(1, rows, width).astype(F32),
        condition_grad,
        grad_norm,
        joint_updated,
        joint_averages,
        output_updated,
        output_averages,
        expand_updated,
        expand_averages,
        shrink_updated,
        shrink_averages,
        modulate_updated,
        modulate_averages,
        attention_updated,
        attention_averages,
        hidden_updated,
        hidden_averages,
        condition_updated,
        condition_averages,
        residual_updated,
        residual_averages,
    )


def solution(mesh):
    rows = P(("fsdp", "ctx"), "tp")
    pair = P(None, ("fsdp", "ctx"), "tp")
    tokens = P("fsdp", "ctx", None)
    small = (P("tp"), P(None, "tp"))
    return jax.shard_map(
        partial(local, mesh.shape["fsdp"], mesh.shape["ctx"]),
        mesh=mesh,
        in_specs=(tokens, P(), tokens) + (rows, pair) * 5 + small * 3 + (P(), P()),
        out_specs=(tokens, tokens, P("fsdp", None), P())
        + (rows, pair) * 5
        + small * 3
        + (P(), P()),
        check_vma=False,
    )
```

time: 1690 us -> 662 us (0.39)
  waiting for transfers between devices: 1050 us -> 196 us
  Pallas kernels: 0 us -> 355 us
  matrix products: 265 us -> 0 us
  other arithmetic: 163 us -> 40.3 us
  blocking collectives: 150 us -> 34.6 us
  local copies, waits for them, and re-layouts: 25.2 us -> 6.79 us
    pallas_call x0 -> x8, Pallas kernels: none -> 355 us  [run(): pl.pallas_call(body, out_shape=outs, in_specs=vmem(len(args)), out_specs=...]
    reduce_scatter x7 -> x4, waiting for transfers between devices: 518 us -> 194 us  [scatter(): lax.psum_scatter(grad, ('fsdp', 'ctx'), scatter_dimension=0, tiled=True)]
    psum x3 -> x0, waiting for transfers between devices: 289 us -> none  [branch_total(): return lax.psum(partial_sum, 'tp')]
    dot_general x28 -> x0, matrix products: 265 us -> none  [the longest x4 56 us: one_block(): jnp.einsum('qhd,khd->hqk', query_block, keys_all, preferred_element_type=...]
    all_gather x6 -> x2, waiting for transfers between devices: 245 us -> 0.04 us  [gather(): lax.all_gather(weight.astype(BF16), ('fsdp', 'ctx'), axis=0, tiled=True)]
    psum x3 -> x0, blocking collectives: 107 us -> none  [the longest x1 37.1 us: local(): lax.psum((attention_bias_grad, hidden_bias_grad, condition_bias_grad, jnp...]
    convert_element_type x9 -> x7, other arithmetic: 63.5 us -> 7.78 us  [the longest x1 4.19 us: local(): tokens_grad.reshape(1, rows, width).astype(F32)]
    reduce_sum x13 -> x6, other arithmetic: 57.1 us -> 5.5 us  [the longest x1 1.37 us: local(): squares = jnp.sum(done[:, nf, 0])]
  transfers between devices with their start and end apart: 16 -> 6, of which waited for: 16 -> 3; matrix products, arithmetic and copies ran while one was open for 5% -> 3% of each run, Pallas kernels for 0% -> 34%
where the time goes in v1:
time: 662 us; the launch traced here: 655 us
  Pallas kernels  355 us (54%)
  waiting for transfers between devices  196 us (30%)
  other arithmetic  40.3 us (6%)
  blocking collectives  34.6 us (5%)
  between operations  22.8 us (3%)
  local copies, waits for them, and re-layouts  6.79 us (1%)
    pallas_call x8, Pallas kernels, run(): pl.pallas_call(body, out_shape=outs, in_specs=vmem(len(args)), out_specs=...  355 us
    reduce_scatter x4, waiting for transfers between devices, scatter(): lax.psum_scatter(grad, ('fsdp', 'ctx'), scatter_dimension=0, tiled=True)  194 us
    all_gather x1, blocking collectives, gather(): lax.all_gather(weight.astype(BF16), ('fsdp', 'ctx'), axis=0, tiled=True)  34.6 us
  transfers between devices with their start and end apart: 6, of which 3 were waited for; matrix products, arithmetic and copies ran while one was open for 3% of the time, Pallas kernels for 34%

profile of v1, /device:TPU:0, one launch (start us, length us, event | category | flops | bytes accessed | tf_op | source)
XLA Modules:
  0.0 655.3 jit_solution(17710994494806658081)
XLA Ops:
  7.3 1.8 convert_element_type.71
  9.1 1.8 convert_element_type.72
  13.6 41.7 %entry.1 = (bf16[768,1024]{1,0:T(8,128)(2,1)}, bf16[1024,1024]{1,0:T(8,128)(2,1)}, bf16[768,1024]{1,0:T(8,128)(2,1)}, f32[4,16,128]{2,1,0:T(8,128)}) custom-call(bf16[1024,1024]{1,0:T(8,128)(2,1)} %bitcast.136, f32[128,768]{1,0:T(8,128)} %weight.1, bf16[16,128]{1,0:T(8,128)(2,1)} %pad.12.cond, f32[128,1536]{1,0:T(8,128)} %modw.1, f32[16,128]{1,0:T(8,128)} %pad.13.cbias, ...), custom_call_target="tpu_custom_call" | custom-call | bytes 90000000 | tf_op jit(solution)/shard_map/entry/pallas_call | solution.py:68
  55.3 89.4 %attend.1 = (bf16[256,1024]{1,0:T(8,128)(2,1)}, bf16[192,4096]{1,0:T(8,128)(2,1)}, f32[64,4096]{1,0:T(8,128)}, f32[1,4096]{1,0:T(1,128)}) custom-call(bf16[768,1024]{1,0:T(8,128)(2,1)} %get-tuple-element.49.x), custom_call_target="tpu_custom_call" | custom-call | bytes 210000000 | tf_op jit(solution)/shard_map/attend/pallas_call | solution.py:68
  144.7 34.6 %all_gather.9.weight = bf16[1024,256]{1,0:T(8,128)(2,1)} all-gather(bf16[128,256]{1,0:T(8,128)(2,1)S(1)} %convert_element_type.70), channel_id=1, replica_groups=mesh['fsdp'=2,'ctx'=4,'tp'=4] {'fsdp','ctx'}, dimensions={0}, use_global_device_ids=true | all-gather | bytes 589824 | tf_op jit(solution)/shard_map/all_gather | solution.py:918
  179.3 37.3 %project.1 = (f32[256,1024]{1,0:T(8,128)}, f32[256,1024]{1,0:T(8,128)}, bf16[4,256,1024]{2,1,0:T(8,128)(2,1)}) custom-call(bf16[256,1024]{1,0:T(8,128)(2,1)} %get-tuple-element.50.att, bf16[1024,256]{1,0:T(8,128)(2,1)} %all_gather.9.weight, bf16[1024,1024]{1,0:T(8,128)(2,1)} %bitcast.137, f32[4,12,128]{2,1,0:T(8,128)} %bitcast.143, f32[2,1024]{1,0:T(2,128)} %bias.3), custom_call_target="tpu_custom_call" | custom-call | bytes 108000000 | tf_op jit(solution)/shard_map/project/pallas_call | solution.py:68
  216.7 44.5 %branch.1 = (bf16[4,256,1024]{2,1,0:T(8,128)(2,1)}, f32[256,1024]{1,0:T(8,128)}, bf16[1024,1024]{1,0:T(8,128)(2,1)}, bf16[1024,1024]{1,0:T(8,128)(2,1)}, f32[8,1...) custom-call(bf16[4,256,1024]{2,1,0:T(8,128)(2,1)} %get-tuple-element.52.hidden, ...), custom_call_target="tpu_custom_call" | custom-call | bytes 135000000 | tf_op jit(solution)/shard_map/branch/pallas_call | solution.py:68
  261.2 75.7 %retreat.1 = (bf16[4,192,1024]{2,1,0:T(8,128)(2,1)}, bf16[1024,256]{1,0:T(8,128)(2,1)}, f32[128,128]{1,0:T(8,128)}, bf16[4,256,1024]{2,1,0:T(8,128)(2,1)}, f32[1,1024]{1,0:T(1,128)}) custom-call(bf16[4,256,1024]{2,1,0:T(8,128)(2,1)} %get-tuple-element.55.attn_low, bf16[1024,256]{1,0:T(8,128)(2,1)} %all_gather.9.weight, ...), custom_call_target="tpu_custom_call" | custom-call | bytes 300000000 | tf_op jit(solution)/shard_map/retreat/pallas_call | solution.py:68
  337.2 38.4 %leave.1 = (bf16[1024,768]{1,0:T(8,128)(2,1)}, bf16[4,256,1024]{2,1,0:T(8,128)(2,1)}, f32[8,1024]{1,0:T(8,128)}) custom-call(bf16[4,192,1024]{2,1,0:T(8,128)(2,1)} %get-tuple-element.62.joint_grad, bf16[768,1024]{1,0:T(8,128)(2,1)} %get-tuple-element.63.weight_t, bf16[1024,1024]{1,0:T(8,128)(2,1)} %get-tuple-element.64.hidden, bf16[1024,1024]{1,0:T(8,128)(2,1)} %bitcast.138, ...), custom_call_target="tpu_custom_call" | custom-call | bytes 108000000 | tf_op jit(solution)/shard_map/leave/pallas_call | solution.py:68
  379.0 17.0 %tally.1 = f32[8,16,128]{2,1,0:T(8,128)} custom-call(f32[16,16,128]{2,1,0:T(8,128)} %select_maximum_fusion.pieces), custom_call_target="tpu_custom_call" | custom-call | bytes 36000000 | tf_op jit(solution)/shard_map/tally/pallas_call | solution.py:68
  405.9 4.2 bitcast_convert_fusion
  410.1 1.5 fusion.28
  411.6 58.2 %reduce-scatter.5.cloned.1.call-done = bf16[128,768]{1,0:T(8,128)(2,1)} async-done(((bf16[1024,768]{1,0:T(8,128)(2,1)}), bf16[128,768]{1,0:T(8,128)(2,1)}) %reduce-scatter.5.cloned.1.call-update) | async-done | bytes 196624 | tf_op jit(solution)/shard_map/reduce_scatter | solution.py:948
  469.8 1.6 fusion.21
  472.7 67.8 %reduce-scatter.9.cloned.1.call-done = bf16[128,1024]{1,0:T(8,128)(2,1)} async-done(((bf16[1024,1024]{1,0:T(8,128)(2,1)}), bf16[128,1024]{1,0:T(8,128)(2,1)}) %reduce-scatter.9.cloned.1.call-update) | async-done | bytes 262160 | tf_op jit(solution)/shard_map/reduce_scatter | solution.py:948
  540.5 1.7 fusion.15
  542.8 68.4 %reduce-scatter.11.cloned.1.call-done = bf16[128,1024]{1,0:T(8,128)(2,1)} async-done(((bf16[1024,1024]{1,0:T(8,128)(2,1)}), bf16[128,1024]{1,0:T(8,128)(2,1)}) %reduce-scatter.11.cloned.1.call-update) | async-done | bytes 262160 | tf_op jit(solution)/shard_map/reduce_scatter | solution.py:948
  611.3 1.7 fusion.16
  615.0 10.9 %finish.1 = f32[8,8,128]{2,1,0:T(8,128)} custom-call(f32[8,128]{1,0:T(8,128)} %maximum_maximum_fusion.piece), custom_call_target="tpu_custom_call" | custom-call | bytes 30000000 | tf_op jit(solution)/shard_map/finish/pallas_call | solution.py:68
  625.9 1.4 slice_reduce_fusion.5
  628.7 1.7 multiply_subtract_fusion
  633.9 1.2 pad_maximum_fusion
  635.2 2.1 fusion.23
  645.6 1.3 copy.47
  (143 shorter events, 26.7 us)
Async XLA Ops:
  7.2 3.8 copy-start.25
  7.2 5.1 copy-start.18
  7.2 5.7 copy-start.19
  7.2 209.4 %all-gather.3.cloned.1.call-start = ((), (), s32[]{:S(2)}) async-start(), calls=%async_computation.4 | async-start | bytes 2359296 | tf_op jit(solution)/shard_map/all_gather | solution.py:918
  9.1 207.6 %all-gather.5.cloned.1.call-start = ((), (), s32[]{:S(2)}) async-start(), calls=%async_computation.5 | async-start | bytes 2359296 | tf_op jit(solution)/shard_map/all_gather | solution.py:918
  10.9 399.2 %reduce-scatter.7.cloned.1.call-start = ((), (), s32[]{:S(2)}) async-start(), calls=%async_computation.7 | async-start | bytes 589824 | tf_op jit(solution)/shard_map/reduce_scatter | solution.py:948
  13.6 131.1 %copy-start.12 = (f32[128,256]{1,0:T(8,128)S(1)}, f32[128,256]{1,0:T(8,128)}, u32[]{:S(2)}) copy-start(f32[128,256]{1,0:T(8,128)} %param.26) | copy-start | bytes 393220
  336.9 132.9 %reduce-scatter.5.cloned.1.call-start = ((), (), s32[]{:S(2)}) async-start(), calls=%async_computation.6 | async-start | bytes 1769472 | tf_op jit(solution)/shard_map/reduce_scatter | solution.py:948
  375.6 164.9 %reduce-scatter.9.cloned.1.call-start = ((), (), s32[]{:S(2)}) async-start(), calls=%async_computation.8 | async-start | bytes 2359296 | tf_op jit(solution)/shard_map/reduce_scatter | solution.py:948
  376.2 28.8 %copy-start = (f32[128,1536]{1,0:T(8,128)S(1)}, f32[128,1536]{1,0:T(8,128)}, u32[]{:S(2)}) copy-start(f32[128,1536]{1,0:T(8,128)} %modw.1) | copy-start | bytes 2359300
  376.2 235.1 %reduce-scatter.11.cloned.1.call-start = ((), (), s32[]{:S(2)}) async-start(), calls=%async_computation.9 | async-start | bytes 2359296 | tf_op jit(solution)/shard_map/reduce_scatter | solution.py:948
  405.9 222.2 %copy-start.1 = (f32[2,128,1536]{2,1,0:T(8,128)S(1)}, f32[2,128,1536]{2,1,0:T(8,128)}, u32[]{:S(2)}) copy-start(f32[2,128,1536]{2,1,0:T(8,128)} %param.33) | copy-start | bytes 4718596
  628.7 3.3 copy-start.16
  628.7 3.9 copy-start.23
  628.7 4.6 copy-start.24
  628.7 6.5 copy-start.9
  630.4 4.8 copy-start.3
  630.4 4.8 copy-start.4
  630.4 4.8 copy-start.6
  630.4 4.8 copy-start.7
  630.4 4.8 copy-start.8
  640.9 3.4 copy-start.15
  641.0 4.0 copy-start.20
  641.0 4.6 copy-start.2
  (10 other events, 22.1 us)
Sparse Core Ops, SparseCore 0:
  10.7 84.6 all-gather.2
  98.1 52.7 all-gather.4
  337.0 64.7 reduce-scatter.6
  405.1 64.6 reduce-scatter.4
  473.2 67.2 reduce-scatter.8
  543.9 67.3 reduce-scatter.10

commit v2 on v1

--- a/solution.py
+++ b/solution.py
@@ -106,6 +106,106 @@
     )
 
 
+def spread_own(buf, nf, nc, zs, zr, xs, xr, lanes=None):
+    f, c = lax.axis_index("fsdp"), lax.axis_index("ctx")
+    slot = f * nc + c
+    view = buf.at[slot] if lanes is None else buf.at[slot, :, lanes]
+    copies = [
+        remote(view, view, zs.at[o], zr.at[o], {"ctx": lax.rem(c + o, nc)}) for o in (1, 3, 2)
+    ]
+    return copies, spread_across(buf, nf, nc, 0, xs, xr, lanes)
+
+
+def spread_across(buf, nf, nc, o, xs, xr, lanes=None):
+    f, c = lax.axis_index("fsdp"), lax.axis_index("ctx")
+    slot = f * nc + lax.rem(c - o + nc, nc)
+    view = buf.at[slot] if lanes is None else buf.at[slot, :, lanes]
+    return [
+        remote(view, view, xs.at[fo, o], xr.at[fo, o], {"fsdp": lax.rem(f + fo, nf)})
+        for fo in range(1, nf)
+    ]
+
+
+def spread_start(*args):
+    along, across = spread_own(*args)
+    for copy in along + across:
+        copy.start()
+
+
+def spread_relay(buf, nf, nc, zs, zr, xs, xr, lanes=None):
+    along, _ = spread_own(buf, nf, nc, zs, zr, xs, xr, lanes)
+    for o, copy in zip((1, 3, 2), along):
+        copy.wait_recv()
+        for relay in spread_across(buf, nf, nc, o, xs, xr, lanes):
+            relay.start()
+
+
+def spread_end(buf, nf, nc, zs, zr, xs, xr, lanes=None):
+    along, across = spread_own(buf, nf, nc, zs, zr, xs, xr, lanes)
+    for o in (1, 3, 2):
+        across = across + spread_across(buf, nf, nc, o, xs, xr, lanes)
+    for copy in across:
+        copy.wait_recv()
+    for copy in along + across:
+        copy.wait_send()
+
+
+def spread_sems(nf, nc):
+    return [DMA((nc,)), DMA((nc,)), DMA((nf, nc)), DMA((nf, nc))]
+
+
+def swap_copies(grad, land, nf, send, recv):
+    f = lax.axis_index("fsdp")
+    return [
+        remote(
+            grad.at[lax.rem(f + fo, nf)], land.at[fo - 1], send.at[fo], recv.at[fo],
+            {"fsdp": lax.rem(f + fo, nf)},
+        )
+        for fo in range(1, nf)
+    ]
+
+
+def swap_sum(grad, land, out, nf):
+    f = lax.axis_index("fsdp")
+    for k in range(out.shape[0]):
+        total = grad[f, k].astype(F32)
+        for fo in range(1, nf):
+            total = total + land[fo - 1, k].astype(F32)
+        out[k] = total.astype(BF16)
+
+
+def deal_copies(parts, land, nc, send, recv):
+    c = lax.axis_index("ctx")
+    return [
+        remote(
+            parts.at[lax.rem(c + o, nc)], land.at[o - 1], send.at[o], recv.at[o],
+            {"ctx": lax.rem(c + o, nc)},
+        )
+        for o in (1, 3, 2)
+    ]
+
+
+def deal_sum(parts, land, nc):
+    total = parts[lax.axis_index("ctx")].astype(F32)
+    for o in range(1, nc):
+        total = total + land[o - 1].astype(F32)
+    return total
+
+
+def ring_peers(axis, size):
+    here = lax.axis_index(axis)
+    return [{axis: lax.rem(here + o, size)} for o in range(1, size)]
+
+
+def weight_peers(nf, nc):
+    f, c = lax.axis_index("fsdp"), lax.axis_index("ctx")
+    peers = []
+    for o in range(1, nf * nc):
+        other = lax.rem(f * nc + c + o, nf * nc)
+        peers.append({"fsdp": other // nc, "ctx": lax.rem(other, nc)})
+    return peers
+
+
 def tp_places():
     mine = lax.axis_index("tp")
     partner = mine + 1 - 2 * lax.rem(mine, 2)
@@ -115,9 +215,9 @@
 
 
 def entry_body(
-    nf, nc, tok, weight, cond, modw, cbias, offset,
-    joint, hidden, weight_t, mod,
-    wbuf, pbuf, pland, normed, zsend, zrecv, xsend, xrecv, psend, precv, msend, mrecv,
+    nf, nc, tok, weight, cond, modw, cbias, offset, extra,
+    joint, hidden, weight_t, mod, ebuf,
+    wbuf, pbuf, pland, normed, psend, precv, msend, mrecv, zs, zr, xs, xr, *esems,
 ):
     f, c, t = lax.axis_index("fsdp"), lax.axis_index("ctx"), lax.axis_index("tp")
     group = nf * nc
@@ -130,49 +230,26 @@
         other = lax.rem(mine + offset_, group)
         return other // nc, lax.rem(other, nc)
 
-    peers = []
-    for o in range(1, group):
-        pf, pc = place(o)
-        peers.append({"fsdp": pf, "ctx": pc})
-    for o in range(1, 4):
-        peers.append({"tp": lax.rem(t + o, 4)})
     partial_mod = dot(cond[...], modw[...].astype(BF16), 1, 0)
     for latent in range(nf):
         for k in range(strips):
             pbuf[latent, pl.ds(k, 1), :] = partial_mod[latent : latent + 1, 128 * k : 128 * k + 128]
     wbuf[mine] = weight[...].astype(BF16)
-    greet(peers)
+    ebuf[mine] = extra[...].astype(BF16)
+    greet(weight_peers(nf, nc) + ring_peers("tp", 4))
     pcopies = []
     for o in range(1, group):
         pf, pc = place(o)
         copy = remote(pbuf.at[pf], pland.at[mine], psend.at[o], precv.at[o], {"fsdp": pf, "ctx": pc})
         copy.start()
         pcopies.append(copy)
-    zcopies, xcopies = [], []
-    for o in range(1, nc):
-        copy = remote(
-            wbuf.at[mine], wbuf.at[mine], zsend.at[o], zrecv.at[o], {"ctx": lax.rem(c + o, nc)}
-        )
-        copy.start()
-        zcopies.append(copy)
-
-    def across(slot, o):
-        for fo in range(1, nf):
-            copy = remote(
-                wbuf.at[slot], wbuf.at[slot], xsend.at[fo, o], xrecv.at[fo, o],
-                {"fsdp": lax.rem(f + fo, nf)},
-            )
-            copy.start()
-            xcopies.append(copy)
-
-    across(mine, 0)
+    spread_start(wbuf, nf, nc, zs, zr, xs, xr)
     pland[mine] = pbuf[f]
     step = 256
     for at in range(0, rows, step):
         normed[at : at + step, :] = centred(tok[at : at + step, :].astype(F32))[0]
-    for o in (1, 3, 2) if nc == 4 else range(1, nc):
-        zcopies[o - 1].wait_recv()
-        across(f * nc + lax.rem(c - o + nc, nc), o)
+    spread_relay(wbuf, nf, nc, zs, zr, xs, xr)
+    spread_start(ebuf, nf, nc, *esems)
     for copy in pcopies:
         copy.wait_recv()
     total = pland[0]
@@ -194,8 +271,8 @@
         hidden[at : at + step, :] = (
             normed[at : at + step, :] * (1.0 + scale) + shift
         ).astype(BF16)
-    for copy in xcopies:
-        copy.wait_recv()
+    spread_end(wbuf, nf, nc, zs, zr, xs, xr)
+    spread_relay(ebuf, nf, nc, *esems)
     deep = weight.shape[0]
     for k in range(group):
         weight_t[:, k * deep : (k + 1) * deep] = transposed(wbuf[k])
@@ -203,11 +280,12 @@
         joint[:, at : at + step] = (
             dot(weight_t[...], hidden[at : at + step, :], 1, 1) + offset[...]
         ).astype(BF16)
-    for copy in pcopies + zcopies + xcopies + mcopies:
+    spread_end(ebuf, nf, nc, *esems)
+    for copy in pcopies + mcopies:
         copy.wait_send()
 
 
-def entry(nf, nc, tok, weight, cond, modw, cbias, offset):
+def entry(nf, nc, tok, weight, cond, modw, cbias, offset, extra):
     rows, width = tok.shape
     deep, columns = weight.shape
     group = nf * nc
@@ -219,23 +297,24 @@
             shape((rows, width), BF16),
             shape((columns, width), BF16),
             shape((4,) + cbias.shape, F32),
+            shape((group,) + extra.shape, BF16),
         ),
         [
             pltpu.VMEM((group, deep, columns), BF16),
             pltpu.VMEM((nf,) + cbias.shape, F32),
             pltpu.VMEM((group,) + cbias.shape, F32),
             pltpu.VMEM((rows, width), F32),
-            DMA((nc,)), DMA((nc,)), DMA((nf, nc)), DMA((nf, nc)),
             DMA((group,)), DMA((group,)), DMA((4,)), DMA((4,)),
-        ],
+        ]
+        + spread_sems(nf, nc) * 2,
         1,
         30,
-    )(tok, weight, cond, modw, cbias, offset)
+    )(tok, weight, cond, modw, cbias, offset, extra)
 
 
 def attend_body(
-    nc, x, att, qkv, out, lse,
-    stage, land, keys, scores, send, recv, osend, orecv,
+    nf, nc, x, extra, att, qkv, out, lse, ebuf,
+    stage, land, keys, scores, send, recv, osend, orecv, *esems,
 ):
     c = lax.axis_index("ctx")
     rows = x.shape[1]
@@ -243,7 +322,9 @@
     hd = HEAD_DIM
     bq, bk = scores.shape[1], 512
     per = rows // bq
-    greet([{"ctx": lax.rem(c + o, nc)} for o in range(1, nc)])
+    slot = lax.axis_index("fsdp") * nc + c
+    ebuf[slot] = extra[...].astype(BF16)
+    greet(ring_peers("ctx", nc) + ring_peers("fsdp", nf))
     copies = []
     for o in range(1, nc):
         dst = lax.rem(c + o, nc)
@@ -256,6 +337,7 @@
     qkv[:, aligned(c * rows, rows)] = x[aligned(c * 3 * hd, 3 * hd), :]
     for copy in copies:
         copy.wait_recv()
+    spread_start(ebuf, nf, nc, *esems)
     for at in range(0, total, 1024):
         keys[at : at + 1024, :] = transposed(qkv[hd : 2 * hd, at : at + 1024])
 
@@ -291,6 +373,10 @@
                 stage.at[owner], land.at[c], osend.at[o], orecv.at[o], {"ctx": owner}
             ).start()
 
+        @pl.when(i == per * nc - 3)
+        def _():
+            spread_relay(ebuf, nf, nc, *esems)
+
         return carry
 
     lax.fori_loop(0, per * nc, block, 0)
@@ -304,21 +390,23 @@
         att[k * hd : (k + 1) * hd, :] = land[k]
     for copy in copies:
         copy.wait_send()
-
-
-def attend(nc, x):
+    spread_end(ebuf, nf, nc, *esems)
+
+
+def attend(nf, nc, x, extra):
     rows = x.shape[1]
     total = rows * nc
     hd = HEAD_DIM
     bq = min(512, rows)
     return call(
-        partial(attend_body, nc),
+        partial(attend_body, nf, nc),
         "attend",
         (
             shape((nc * hd, rows), BF16),
             shape((3 * hd, total), BF16),
             shape((hd, total), F32),
             shape((1, total), F32),
+            shape((nf * nc,) + extra.shape, BF16),
         ),
         [
             pltpu.VMEM((nc, hd, rows), BF16),
@@ -326,29 +414,36 @@
             pltpu.VMEM((total, hd), BF16),
             pltpu.VMEM((total, bq), F32),
             DMA((nc,)), DMA((nc,)), DMA((nc,)), DMA((nc,)),
-        ],
+        ]
+        + spread_sems(nf, nc),
         2,
         70,
-    )(x)
+    )(x, extra)
 
 
 def project_body(
-    att, weight, tok, mod, bias,
-    value, middle, hidden,
-    sbuf, rbuf, send, recv, gsend, grecv,
+    nf, nc, part, att, weight, tok, mod, bias, early, late, other,
+    value, middle, hidden, expand, shrink,
+    sbuf, rbuf, send, recv, gsend, grecv, *sems,
 ):
     mine, partner, cross, far = tp_places()
     own = value.shape[0]
     width = tok.shape[1]
-    part = mod.shape[1] * 128
-    att_t = [None]
+    slot = lax.axis_index("fsdp") * nc + lax.axis_index("ctx")
+    split = early.shape[2]
+    lanes = pl.ds(split, split)
+    expand[:, :, 0:split] = early[...]
+    expand[slot, :, split : 2 * split] = late[...].astype(BF16)
+    shrink[slot] = other[...].astype(BF16)
 
     def piece(at):
         return dot(
             att[:, aligned(at * own, own)].astype(F32).T.astype(BF16), weight[...], 1, 1
         )
 
-    greet([{"tp": lax.rem(mine + o, 4)} for o in range(1, 4)])
+    greet(ring_peers("tp", 4) + ring_peers("ctx", nc) + ring_peers("fsdp", nf))
+    spread_start(expand, nf, nc, *sems[0:4], lanes)
+    spread_start(shrink, nf, nc, *sems[4:8])
     sbuf[0] = piece(far).astype(BF16)
     first = remote(sbuf.at[0], rbuf.at[0], send.at[0], recv.at[0], {"tp": partner})
     first.start()
@@ -373,9 +468,13 @@
     middle[...] = mid
     hidden[mine] = (centred(mid)[0] * (1.0 + scale) + shift).astype(BF16)
     copies = gather_start(hidden, mine, partner, cross, gsend, grecv)
+    spread_relay(expand, nf, nc, *sems[0:4], lanes)
     gather_end(hidden, copies, mine, partner, cross, gsend, grecv)
+    spread_relay(shrink, nf, nc, *sems[4:8])
     for copy in (first, second, third):
         copy.wait_send()
+    spread_end(expand, nf, nc, *sems[0:4], lanes)
+    spread_end(shrink, nf, nc, *sems[4:8])
 
 
 def gather_start(slots, mine, partner, cross, send, recv):
@@ -397,31 +496,34 @@
         copy.wait_send()
 
 
-def project(att, weight, tok, mod, bias):
+def project(nf, nc, part, att, weight, tok, mod, bias, early, late, other):
     rows, width = tok.shape
     own = rows // 4
     return call(
-        project_body,
+        partial(project_body, nf, nc, part),
         "project",
-        (shape((own, width), F32), shape((own, width), F32), shape((4, own, width), BF16)),
+        (
+            shape((own, width), F32), shape((own, width), F32), shape((4, own, width), BF16),
+            shape((nf * nc,) + other.shape, BF16), shape((nf * nc,) + other.shape, BF16),
+        ),
         [
             pltpu.VMEM((3, own, width), BF16),
             pltpu.VMEM((3, own, width), BF16),
             DMA((3,)), DMA((3,)), DMA((3,)), DMA((3,)),
-        ],
+        ]
+        + spread_sems(nf, nc) * 2,
         3,
         36,
-    )(att, weight, tok, mod, bias)
+    )(att, weight, tok, mod, bias, early, late, other)
 
 
 def branch_body(
-    hidden, cot, expand, shrink, hbias, mod, middle, value,
+    part, hidden, cot, expand, shrink, hbias, mod, middle, value,
     attn_low, mid_grad, shrink_grad, expand_grad, stats, hstats, sh_cross, sh_own,
     gbuf, abuf, ebuf, sbuf, rbuf, shold, tsend, trecv, send, recv, gsend, grecv,
 ):
     mine, partner, cross, far = tp_places()
     own, width = middle.shape
-    part = mod.shape[1] * 128
     gate_first = row_of(mod, 2 * width, width, part)
     scale_second = row_of(mod, 4 * width, width, part)
     gate_second = row_of(mod, 5 * width, width, part)
@@ -505,12 +607,12 @@
         copy.wait_send()
 
 
-def branch(hidden, cot, expand, shrink, hbias, mod, middle, value):
+def branch(part, hidden, cot, expand, shrink, hbias, mod, middle, value):
     rows, width = cot.shape
     own = rows // 4
     units = expand.shape[1]
     return call(
-        branch_body,
+        partial(branch_body, part),
         "branch",
         (
             shape((4, own, width), BF16),
@@ -537,10 +639,12 @@
 
 
 def retreat_body(
-    nc, attn_low, weight, att, qkv, out, lse, sh_cross, sh_own, middle, cot, mod, bias,
-    joint_grad, weight_grad, bias_grad, mixed, gate_grad,
-    dout, dost, keys, vals, dq, stage, rland, wt, delta, send, recv, jsend, jrecv,
-    csend, crecv, gsend, grecv,
+    nf, nc, part, attn_low, weight, att, qkv, out, lse, sh_cross, sh_own, middle, cot, mod, bias,
+    shrink_grad, expand_grad,
+    joint_grad, bias_grad, mixed, gate_grad, shrink_sum, expand_parts, output_parts,
+    dout, dost, keys, vals, dq, stage, rland, wt, delta, output_grad,
+    sland, eland, oland, shrink_parts, dland, send, recv, jsend, jrecv,
+    csend, crecv, gsend, grecv, ssend, srecv, esend, erecv, osend, orecv, dsend, drecv,
 ):
     c = lax.axis_index("ctx")
     mine, partner, cross, far = tp_places()
@@ -550,14 +654,16 @@
     hd = HEAD_DIM
     bk = bq = 512
     per = rows // bk
-    part = mod.shape[1] * 128
     wt[...] = transposed(weight[...])
     low = attn_low[...].reshape(rows, width)
     dost[...] = dot(wt[...], low, 1, 1).astype(BF16)
-    greet(
-        [{"ctx": lax.rem(c + o, nc)} for o in range(1, nc)]
-        + [{"tp": lax.rem(mine + o, 4)} for o in range(1, 4)]
-    )
+    greet(ring_peers("tp", 4) + ring_peers("ctx", nc) + ring_peers("fsdp", nf))
+    shrink_swap = swap_copies(shrink_grad, sland, nf, ssend, srecv)
+    expand_swap = swap_copies(expand_grad, eland, nf, esend, erecv)
+    output_swap = swap_copies(output_grad, oland, nf, osend, orecv)
+    shrink_deal = deal_copies(shrink_parts, dland, nc, dsend, drecv)
+    for copy in shrink_swap + expand_swap:
+        copy.start()
     copies = []
     for o in range(1, nc):
         dst = lax.rem(c + o, nc)
@@ -570,7 +676,10 @@
     crossing = remote(sh_cross, rland, csend, crecv, {"tp": cross})
     crossing.start()
     dout[:, aligned(c * rows, rows)] = dost[aligned(c * hd, hd), :]
-    weight_grad[...] = dot(att[...], low, 1, 0).T.astype(BF16)
+    flat = dot(att[...], low, 1, 0).T.astype(BF16)
+    output_grad[...] = flat.reshape(output_grad.shape)
+    for copy in output_swap:
+        copy.start()
     for at in range(0, total, 1024):
         keys[at : at + 1024, :] = transposed(qkv[hd : 2 * hd, at : at + 1024])
         vals[at : at + 1024, :] = transposed(qkv[2 * hd : 3 * hd, at : at + 1024])
@@ -611,6 +720,20 @@
                 jsend.at[0, o], jrecv.at[0, o], {"ctx": owner},
             ).start()
 
+        @pl.when(i == 3)
+        def _():
+            for copy in shrink_swap:
+                copy.wait_recv()
+            swap_sum(shrink_grad, sland, shrink_parts, nf)
+            for copy in shrink_deal:
+                copy.start()
+
+        @pl.when(i == 6)
+        def _():
+            for copy in expand_swap:
+                copy.wait_recv()
+            swap_sum(expand_grad, eland, expand_parts, nf)
+
         @pl.when(i == 2)
         def _():
             crossing.wait_recv()
@@ -639,6 +762,12 @@
             )
             copy.start()
             dqs.append(copy)
+    for copy in output_swap:
+        copy.wait_recv()
+    swap_sum(output_grad, oland, output_parts, nf)
+    for copy in shrink_deal:
+        copy.wait_recv()
+    shrink_sum[...] = deal_sum(shrink_parts, dland, nc)
     joint_grad[c] = stage[c]
     bias_grad[0:hd, :] = jnp.broadcast_to(qsum, (hd, 128))
     bias_grad[hd : 2 * hd, :] = jnp.broadcast_to(vsum, (hd, 128))
@@ -655,24 +784,33 @@
         copy.wait_send()
         dqs[o - 1].wait_recv()
         dqs[o - 1].wait_send()
-    for copy in copies + [crossing]:
+    for copy in copies + [crossing] + shrink_swap + expand_swap + output_swap + shrink_deal:
         copy.wait_send()
 
 
-def retreat(nc, attn_low, weight, att, qkv, out, lse, sh_cross, sh_own, middle, cot, mod, bias):
+def retreat(
+    nf, nc, part, attn_low, weight, att, qkv, out, lse, sh_cross, sh_own, middle, cot, mod, bias,
+    shrink_grad, expand_grad,
+):
     rows, width = cot.shape
     own = rows // 4
     total = rows * nc
     hd = HEAD_DIM
+    deep = width // (nf * nc)
+    units = shrink_grad.shape[1]
+    split = (nf, nc, deep, units)
+    shrink_grad, expand_grad = shrink_grad.reshape(split), expand_grad.reshape(split)
     return call(
-        partial(retreat_body, nc),
+        partial(retreat_body, nf, nc, part),
         "retreat",
         (
             shape((nc, 3 * hd, rows), BF16),
-            shape((width, nc * hd), BF16),
             shape((2 * hd, 128), F32),
             shape((4, own, width), BF16),
             shape((1, width), F32),
+            shape((deep, units), F32),
+            shape((nc, deep, units), BF16),
+            shape((nc, deep, nc * hd), BF16),
         ),
         [
             pltpu.VMEM((hd, total), BF16),
@@ -684,29 +822,46 @@
             pltpu.VMEM((own, width), BF16),
             pltpu.VMEM((nc * hd, width), BF16),
             pltpu.VMEM((1, total), F32),
+            pltpu.VMEM((nf, nc, deep, nc * hd), BF16),
+            pltpu.VMEM((nf - 1, nc, deep, units), BF16),
+            pltpu.VMEM((nf - 1, nc, deep, units), BF16),
+            pltpu.VMEM((nf - 1, nc, deep, nc * hd), BF16),
+            pltpu.VMEM((nc, deep, units), BF16),
+            pltpu.VMEM((nc - 1, deep, units), BF16),
             DMA((nc,)), DMA((nc,)), DMA((2, nc)), DMA((2, nc)),
             DMA, DMA, DMA((3,)), DMA((3,)),
-        ],
+        ]
+        + [DMA((nf,))] * 6
+        + [DMA((nc,))] * 2,
         5,
         100,
-    )(attn_low, weight, att, qkv, out, lse, sh_cross, sh_own, middle, cot, mod, bias)
+    )(
+        attn_low, weight, att, qkv, out, lse, sh_cross, sh_own, middle, cot, mod, bias,
+        shrink_grad, expand_grad,
+    )
 
 
 def leave_body(
-    joint_grad, weight_t, hidden, tok, mid_grad, mod,
-    weight_grad, tokens_grad, stats,
-    sbuf, rbuf, send, recv, gsend, grecv,
+    nf, nc, part, joint_grad, weight_t, hidden, tok, mid_grad, mod, expand_parts, output_parts,
+    joint_parts, tokens_grad, stats, expand_sum, output_sum,
+    sbuf, rbuf, joint_weight_grad, jland, eland, oland,
+    send, recv, jsend, jrecv, esend, erecv, osend, orecv,
 ):
     mine, partner, cross, far = tp_places()
     own, width = mid_grad.shape
-    part = mod.shape[1] * 128
     columns = weight_t.shape[0]
+    deep = expand_sum.shape[0]
 
     def piece(at):
         block = joint_grad[:, :, aligned(at * own, own)].reshape(columns, own)
         return dot(block.astype(F32).T.astype(BF16), weight_t[...], 1, 0)
 
-    greet([{"tp": lax.rem(mine + o, 4)} for o in range(1, 4)])
+    greet(ring_peers("tp", 4) + ring_peers("ctx", nc) + ring_peers("fsdp", nf))
+    expand_deal = deal_copies(expand_parts, eland, nc, esend, erecv)
+    output_deal = deal_copies(output_parts, oland, nc, osend, orecv)
+    joint_swap = swap_copies(joint_weight_grad, jland, nf, jsend, jrecv)
+    for copy in output_deal + expand_deal:
+        copy.start()
     sbuf[0] = piece(far).astype(BF16)
     first = remote(sbuf.at[0], rbuf.at[0], send.at[0], recv.at[0], {"tp": partner})
     first.start()
@@ -718,166 +873,396 @@
     sbuf[2] = (crossing + rbuf[0].astype(F32)).astype(BF16)
     third = remote(sbuf.at[2], rbuf.at[2], send.at[2], recv.at[2], {"tp": cross})
     third.start()
+    flat = joint_grad[...].reshape(columns, tok.shape[0])
+    rows_f = width // nf
+    step = max(128, min(256, rows_f))
+    for at in range(0, width, step):
+        block = dot(flat, hidden[:, at : at + step], 1, 0).T.astype(BF16)
+        for k in range(at // deep, (at + step) // deep):
+            joint_weight_grad[k // nc, k % nc] = block[k * deep - at : (k + 1) * deep - at, :]
+    for copy in joint_swap:
+        copy.start()
     held = piece(mine)
     second.wait_recv()
     held = held + rbuf[1].astype(F32)
     normed, inverse = centred(tok[aligned(mine * own, own), :].astype(F32))
-    flat = joint_grad[...].reshape(columns, tok.shape[0])
-    step = 256
-    for at in range(0, width, step):
-        weight_grad[at : at + step, :] = dot(flat, hidden[:, at : at + step], 1, 0).T.astype(BF16)
     third.wait_recv()
     grad_in = held + rbuf[2].astype(F32)
     scale = row_of(mod, width, width, part)
     stats[0:1, :] = jnp.sum(grad_in, axis=0, keepdims=True)
     stats[1:2, :] = jnp.sum(grad_in * normed, axis=0, keepdims=True)
     stats[2:8, :] = jnp.zeros((6, width), F32)
-    tokens_grad[mine] = (
+    tokens_grad[...] = (
         mid_grad[...] + normal_back(grad_in * (1.0 + scale), normed, inverse)
     ).astype(BF16)
-    copies = gather_start(tokens_grad, mine, partner, cross, gsend, grecv)
-    gather_end(tokens_grad, copies, mine, partner, cross, gsend, grecv)
-    for copy in (first, second, third):
+    for copy in output_deal:
+        copy.wait_recv()
+    output_sum[...] = deal_sum(output_parts, oland, nc)
+    for copy in expand_deal:
+        copy.wait_recv()
+    expand_sum[...] = deal_sum(expand_parts, eland, nc)
+    for copy in joint_swap:
+        copy.wait_recv()
+    swap_sum(joint_weight_grad, jland, joint_parts, nf)
+    for copy in [first, second, third] + output_deal + expand_deal + joint_swap:
         copy.wait_send()
 
 
-def leave(joint_grad, weight_t, hidden, tok, mid_grad, mod):
+def leave(nf, nc, part, joint_grad, weight_t, hidden, tok, mid_grad, mod, expand_parts, output_parts):
     rows, width = tok.shape
     own = rows // 4
+    columns = weight_t.shape[0]
+    deep, units = expand_parts.shape[1:]
+    inner = output_parts.shape[2]
     return call(
-        leave_body,
+        partial(leave_body, nf, nc, part),
         "leave",
         (
-            shape((width, weight_t.shape[0]), BF16),
-            shape((4, own, width), BF16),
+            shape((nc, deep, columns), BF16),
+            shape((own, width), BF16),
             shape((8, width), F32),
+            shape((deep, units), F32),
+            shape((deep, inner), F32),
         ),
         [
             pltpu.VMEM((3, own, width), BF16),
             pltpu.VMEM((3, own, width), BF16),
-            DMA((3,)), DMA((3,)), DMA((3,)), DMA((3,)),
+            pltpu.VMEM((nf, nc, deep, columns), BF16),
+            pltpu.VMEM((nf - 1, nc, deep, columns), BF16),
+            pltpu.VMEM((nc - 1, deep, units), BF16),
+            pltpu.VMEM((nc - 1, deep, inner), BF16),
+            DMA((3,)), DMA((3,)), DMA((nf,)), DMA((nf,)),
+            DMA((nc,)), DMA((nc,)), DMA((nc,)), DMA((nc,)),
         ],
         6,
-        36,
-    )(joint_grad, weight_t, hidden, tok, mid_grad, mod)
-
-
-def tally_body(nf, nc, pieces, gathered, land, total, asend, arecv, bsend, brecv):
+        30,
+    )(joint_grad, weight_t, hidden, tok, mid_grad, mod, expand_parts, output_parts)
+
+
+def settle_body(
+    nf, nc, part, joint_parts, own_tokens, stats_first, stats_second, gate_grad, hidden_stats,
+    head_bias, shrink_sum, expand_sum, output_sum, modw, low,
+    tokens_grad, joint_sum, modulate_sum, bias_rows, done,
+    jland, pieces, land, total, gathered, fland, ftotal,
+    jsend, jrecv, gsend, grecv, asend, arecv, bsend, brecv, csend, crecv, dsend, drecv,
+):
     f, c, t = lax.axis_index("fsdp"), lax.axis_index("ctx"), lax.axis_index("tp")
-    inner = nc * 4
-    group = nf * nc
-    here = c * 4 + t
-    mine = f * nc + c
-    peers = []
+    mine, partner, cross, far = tp_places()
+    inner, group = nc * 4, nf * nc
+    here, slot = c * 4 + t, f * nc + c
+    width = stats_first.shape[1]
+    deep = joint_sum.shape[0]
+    slim = part // nc // 128
+    share = 2 * width // nc // 128
+    hshare = hidden_stats.shape[1] // nc // 128
+    tokens_grad[mine] = own_tokens[...]
+    rows = [
+        stats_first[0:1, :], stats_first[1:2, :], stats_second[2:3, :],
+        stats_second[0:1, :], stats_second[1:2, :], gate_grad[...],
+    ]
+
+    def strip(k):
+        at = k * 128
+        return rows[at // width][:, at % width : at % width + 128]
+
+    residual = [stats_second[4:5, :], stats_second[3:4, :]]
+    pieces[...] = jnp.zeros_like(pieces)
+    for cc in range(nc):
+        for tt in range(4):
+            k = cc * 4 + tt
+            for n in range(slim):
+                pieces[k, n : n + 1, :] = strip((tt * part // 128) + cc * slim + n)
+            for n in range(share):
+                at = (cc * share + n) * 128
+                pieces[k, slim + n : slim + n + 1, :] = residual[at // width][
+                    :, at % width : at % width + 128
+                ]
+        for n in range(hshare):
+            at = (cc * hshare + n) * 128
+            pieces[cc * 4 + t, slim + share + n : slim + share + n + 1, :] = hidden_stats[
+                :, at : at + 128
+            ]
+    last = slim + share + hshare
+    pieces[here, last : last + 1, :] = head_bias[...].T[0:1, :]
+    greet(
+        [
+            {"ctx": lax.rem(here + o, inner) // 4, "tp": lax.rem(lax.rem(here + o, inner), 4)}
+            for o in range(1, inner)
+        ]
+        + weight_peers(nf, nc)
+    )
+    first = []
     for o in range(1, inner):
         other = lax.rem(here + o, inner)
-        peers.append({"ctx": other // 4, "tp": lax.rem(other, 4)})
-    outer = []
-    for o in range(1, group):
-        other = lax.rem(mine + o, group)
-        outer.append({"fsdp": other // nc, "ctx": lax.rem(other, nc)})
-    greet(peers + outer)
-    copies = []
-    for o in range(1, inner):
-        other = lax.rem(here + o, inner)
-        copy = remote(pieces.at[other], land.at[here], asend.at[o], arecv.at[o], peers[o - 1])
+        copy = remote(
+            pieces.at[other], land.at[here], asend.at[o], arecv.at[o],
+            {"ctx": other // 4, "tp": lax.rem(other, 4)},
+        )
         copy.start()
-        copies.append(copy)
+        first.append(copy)
+    deals = deal_copies(joint_parts, jland, nc, jsend, jrecv)
+    for copy in deals:
+        copy.start()
+    gathers = gather_start(tokens_grad, mine, partner, cross, gsend, grecv)
     land[here] = pieces[here]
-    for copy in copies:
+    for copy in first:
         copy.wait_recv()
     acc = land[0]
     for k in range(1, inner):
         acc = acc + land[k]
     total[...] = acc
-    gathered[mine] = acc
+    gathered[slot] = acc
     second = []
-    for o in range(1, group):
-        copy = remote(total, gathered.at[mine], bsend.at[o], brecv.at[o], outer[o - 1])
+    for o, peer in zip(range(1, group), weight_peers(nf, nc)):
+        copy = remote(total, gathered.at[slot], bsend.at[o], brecv.at[o], peer)
         copy.start()
         second.append(copy)
+    squares = (
+        jnp.sum(shrink_sum[...] * shrink_sum[...])
+        + jnp.sum(expand_sum[...] * expand_sum[...])
+        + jnp.sum(output_sum[...] * output_sum[...])
+    )
     for copy in second:
         copy.wait_recv()
-    for copy in copies + second:
+    grads = []
+    for latent in range(nf):
+        strips = []
+        for cc in range(nc):
+            for n in range(slim):
+                strips.append(gathered[latent * nc + cc, n : n + 1, :])
+        grads.append(jnp.concatenate(strips, axis=1))
+    condition_bias = grads[0]
+    for latent in range(1, nf):
+        condition_bias = condition_bias + grads[latent]
+    bias_rows[...] = jnp.zeros_like(bias_rows)
+    bias_rows[0:1, 0:part] = condition_bias
+    factors = low[...].T
+    wide = modw[...].astype(BF16).astype(F32)
+    outer = None
+    ftotal[...] = jnp.zeros_like(ftotal)
+    for latent in range(nf):
+        term = factors[:, latent : latent + 1] * grads[latent]
+        outer = term if outer is None else outer + term
+        column = jnp.sum(wide * grads[latent], axis=1, keepdims=True)
+        ftotal[latent : latent + 1, 0:deep] = jnp.broadcast_to(column, (deep, 128)).T[0:1, :]
+    modulate_sum[...] = outer
+    squares = squares + jnp.sum(outer * outer)
+
+    def over(at, count, step):
+        found = []
+        for cc in range(nc):
+            value = None
+            for latent in range(nf):
+                block = gathered[latent * nc + cc, at : at + count, :]
+                value = block if value is None else value + block
+            for n in range(count):
+                found.append(value[n : n + 1, :])
+        return jnp.concatenate(found, axis=1)
+
+    residual_sum = over(slim, share, 0)
+    hidden_sum = over(slim + share, hshare, 0)
+    head_sum = over(last, 1, 0)
+    bias_rows[1:2, 0 : hidden_sum.shape[1]] = hidden_sum
+    bias_rows[2:3, 0 : head_sum.shape[1]] = head_sum
+    bias_rows[3:4, 0:width] = residual_sum[:, 0:width]
+    bias_rows[4:5, 0:width] = residual_sum[:, width : 2 * width]
+    lead = (slot == 0).astype(F32)
+    tensor_lead = (t == 0).astype(F32)
+    squares = squares + lead * (
+        jnp.sum(condition_bias * condition_bias)
+        + jnp.sum(hidden_sum * hidden_sum)
+        + jnp.sum(head_sum * head_sum)
+        + tensor_lead * jnp.sum(residual_sum * residual_sum)
+    )
+    for copy in deals:
+        copy.wait_recv()
+    joint = deal_sum(joint_parts, jland, nc)
+    joint_sum[...] = joint
+    squares = squares + jnp.sum(joint * joint)
+    ftotal[nf : nf + 1, :] = jnp.full((1, 128), squares)
+    third = []
+    for o, peer in zip(range(1, 4), ring_peers("tp", 4)):
+        copy = remote(ftotal, fland.at[t], csend.at[o], crecv.at[o], peer)
+        copy.start()
+        third.append(copy)
+    fland[t] = ftotal[...]
+    for copy in third:
+        copy.wait_recv()
+    acc = fland[0] + fland[1] + fland[2] + fland[3]
+    done[slot] = acc
+    fourth = []
+    for o, peer in zip(range(1, group), weight_peers(nf, nc)):
+        copy = remote(done.at[slot], done.at[slot], dsend.at[o], drecv.at[o], peer)
+        copy.start()
+        fourth.append(copy)
+    gather_end(tokens_grad, gathers, mine, partner, cross, gsend, grecv)
+    for copy in fourth:
+        copy.wait_recv()
+    for copy in first + deals + second + third + fourth:
         copy.wait_send()
 
 
-def tally(nf, nc, pieces):
-    inner, high, lanes = pieces.shape
-    group = nf * nc
+def settle(
+    nf, nc, part, joint_parts, own_tokens, stats_first, stats_second, gate_grad, hidden_stats,
+    head_bias, shrink_sum, expand_sum, output_sum, modw, low,
+):
+    own, width = own_tokens.shape
+    deep, columns = joint_parts.shape[1:]
+    inner, group = nc * 4, nf * nc
+    high = -(-(part // nc + 2 * width // nc + hidden_stats.shape[1] // nc + 128) // 1024) * 8
+    tall = -(-(nf + 1) // 8) * 8
     return call(
-        partial(tally_body, nf, nc),
-        "tally",
-        (shape((group, high, lanes), F32),),
+        partial(settle_body, nf, nc, part),
+        "settle",
+        (
+            shape((4, own, width), BF16),
+            shape((deep, columns), F32),
+            shape((deep, part), F32),
+            shape((8, max(part, width, hidden_stats.shape[1])), F32),
+            shape((group, tall, 128), F32),
+        ),
         [
-            pltpu.VMEM((inner, high, lanes), F32),
-            pltpu.VMEM((high, lanes), F32),
+            pltpu.VMEM((nc - 1, deep, columns), BF16),
+            pltpu.VMEM((inner, high, 128), F32),
+            pltpu.VMEM((inner, high, 128), F32),
+            pltpu.VMEM((high, 128), F32),
+            pltpu.VMEM((group, high, 128), F32),
+            pltpu.VMEM((4, tall, 128), F32),
+            pltpu.VMEM((tall, 128), F32),
+            DMA((nc,)), DMA((nc,)), DMA((3,)), DMA((3,)),
             DMA((inner,)), DMA((inner,)), DMA((group,)), DMA((group,)),
+            DMA((4,)), DMA((4,)), DMA((group,)), DMA((group,)),
         ],
         7,
-        12,
-    )(pieces)[0]
-
-
-def finish_body(nf, nc, piece, gathered, land, total, asend, arecv, bsend, brecv):
-    f, c, t = lax.axis_index("fsdp"), lax.axis_index("ctx"), lax.axis_index("tp")
-    group = nf * nc
-    mine = f * nc + c
-    peers = [{"tp": lax.rem(t + o, 4)} for o in range(1, 4)]
-    outer = []
-    for o in range(1, group):
-        other = lax.rem(mine + o, group)
-        outer.append({"fsdp": other // nc, "ctx": lax.rem(other, nc)})
-    greet(peers + outer)
-    copies = []
-    for o in range(1, 4):
-        copy = remote(piece, land.at[t], asend.at[o], arecv.at[o], peers[o - 1])
-        copy.start()
-        copies.append(copy)
-    land[t] = piece[...]
-    for copy in copies:
-        copy.wait_recv()
-    acc = land[0] + land[1] + land[2] + land[3]
-    total[...] = acc
-    gathered[mine] = acc
-    second = []
-    for o in range(1, group):
-        copy = remote(total, gathered.at[mine], bsend.at[o], brecv.at[o], outer[o - 1])
-        copy.start()
-        second.append(copy)
-    for copy in second:
-        copy.wait_recv()
-    for copy in copies + second:
-        copy.wait_send()
-
-
-def finish(nf, nc, piece):
-    high, lanes = piece.shape
-    group = nf * nc
-    return call(
-        partial(finish_body, nf, nc),
-        "finish",
-        (shape((group, high, lanes), F32),),
-        [
-            pltpu.VMEM((4, high, lanes), F32),
-            pltpu.VMEM((high, lanes), F32),
-            DMA((4,)), DMA((4,)), DMA((group,)), DMA((group,)),
-        ],
-        8,
-        10,
-    )(piece)[0]
-
-
-def adam_step(master, moments, gradient, clip_factor, decay_rate):
-    scaled = clip_factor * gradient
-    first_moment = first_decay * moments[0] + (1.0 - first_decay) * scaled
-    second_moment = second_decay * moments[1] * moments[1] + (1.0 - second_decay) * scaled * scaled
-    first_hat = first_moment / (1.0 - first_decay**ADAM_STEP)
-    second_hat = second_moment / (1.0 - second_decay**ADAM_STEP)
+        30,
+    )(
+        joint_parts, own_tokens, stats_first, stats_second, gate_grad, hidden_stats,
+        head_bias, shrink_sum, expand_sum, output_sum, modw, low,
+    )
+
+
+def update(master, first, root, gradient, clip, decay_rate):
+    scaled = clip * gradient
+    first_moment = first_decay * first + (1.0 - first_decay) * scaled
+    second_moment = second_decay * root * root + (1.0 - second_decay) * scaled * scaled
+    new_root = jnp.sqrt(second_moment)
+    first_hat = first_moment * (1.0 / (1.0 - first_decay**ADAM_STEP))
+    second_hat = second_moment * (1.0 / (1.0 - second_decay**ADAM_STEP))
     updated = master - learning_rate * (
         first_hat / (jnp.sqrt(second_hat) + adam_epsilon) + decay_rate * master
     )
-    return (updated, jnp.stack([first_moment, jnp.sqrt(second_moment)]))
+    return updated, first_moment, new_root
+
+
+def adam_body(count, nf, nc, done, condition, bias_rows, *refs):
+    grads = refs[:count]
+    masters = refs[count : 2 * count]
+    moments = refs[2 * count : 3 * count]
+    smalls = refs[3 * count : 3 * count + 8]
+    outs = refs[3 * count + 8 :]
+    news = outs[:count]
+    averages = outs[count : 2 * count]
+    small_outs = outs[2 * count : 2 * count + 8]
+    condition_grad, norm = outs[2 * count + 8 : 2 * count + 10]
+    scratch = outs[2 * count + 10 :]
+    wbufs = scratch[:count]
+    mbufs = scratch[count : 2 * count]
+    gbufs = scratch[2 * count : 3 * count]
+    isem, osem = scratch[3 * count :]
+    group = nf * nc
+    f = lax.axis_index("fsdp")
+    loads, stores = [], []
+    for k in range(count):
+        loads.append(
+            (
+                pltpu.make_async_copy(masters[k], wbufs[k], isem.at[0, k]),
+                pltpu.make_async_copy(moments[k], mbufs[k], isem.at[1, k]),
+                pltpu.make_async_copy(grads[k], gbufs[k], isem.at[2, k]),
+            )
+        )
+        stores.append(
+            (
+                pltpu.make_async_copy(wbufs[k], news[k], osem.at[0, k]),
+                pltpu.make_async_copy(mbufs[k], averages[k], osem.at[1, k]),
+            )
+        )
+    for trio in loads:
+        for copy in trio:
+            copy.start()
+    squares = done[0, nf : nf + 1, 0:1]
+    for k in range(1, group):
+        squares = squares + done[k, nf : nf + 1, 0:1]
+    grad_norm = jnp.sqrt(squares)
+    norm[...] = grad_norm
+    clip = jnp.minimum(1.0, clip_limit / (grad_norm + 1e-06))
+    deep = condition.shape[1] // group
+    found = [done[k, pl.ds(f, 1), 0:deep] for k in range(group)]
+    v = condition[pl.ds(f, 1), :]
+    gate = 1.0 / (1.0 + jnp.exp(-v))
+    condition_grad[...] = jnp.concatenate(found, axis=1) * (gate * (1.0 + v * (1.0 - gate)))
+    for k in range(4):
+        master, moment = smalls[2 * k], smalls[2 * k + 1]
+        if k < 3:
+            row = (2, 1, 0)[k]
+            grad = bias_rows[row : row + 1, 0 : master.shape[1]]
+            new, first, root = update(master[...], moment[0:1, :], moment[1:2, :], grad, clip, 0.0)
+            small_outs[2 * k][...] = new
+            small_outs[2 * k + 1][0:1, :] = first
+            small_outs[2 * k + 1][1:2, :] = root
+        else:
+            grad = bias_rows[3:5, 0 : master.shape[1]]
+            new, first, root = update(master[...], moment[0], moment[1], grad, clip, 0.0)
+            small_outs[2 * k][...] = new
+            small_outs[2 * k + 1][0] = first
+            small_outs[2 * k + 1][1] = root
+    for k in range(count):
+        for copy in loads[k]:
+            copy.wait()
+        deep_k = wbufs[k].shape[0]
+        step = min(16, deep_k)
+
+        def rows(i, carry, k=k, step=step):
+            at = pl.ds(pl.multiple_of(i * step, step), step)
+            new, first, root = update(
+                wbufs[k][at, :], mbufs[k][0, at, :], mbufs[k][1, at, :], gbufs[k][at, :],
+                clip, weight_decay,
+            )
+            wbufs[k][at, :] = new
+            mbufs[k][0, at, :] = first
+            mbufs[k][1, at, :] = root
+            return carry
+
+        lax.fori_loop(0, deep_k // step, rows, 0)
+        for copy in stores[k]:
+            copy.start()
+    for pair in stores:
+        for copy in pair:
+            copy.wait()
+
+
+def adam(nf, nc, done, condition, bias_rows, grads, masters, moments, smalls):
+    count = len(grads)
+    anywhere = pl.BlockSpec(memory_space=pl.ANY)
+    small_shapes = tuple(shape(a.shape, F32) for a in smalls)
+    outs = (
+        tuple(shape(m.shape, F32) for m in masters)
+        + tuple(shape(m.shape, F32) for m in moments)
+        + small_shapes
+        + (shape((1, condition.shape[1]), F32), shape((1, 1), F32))
+    )
+    return pl.pallas_call(
+        partial(adam_body, count, nf, nc),
+        out_shape=outs,
+        in_specs=vmem(3) + [anywhere] * (3 * count) + vmem(8),
+        out_specs=[anywhere] * (2 * count) + vmem(10),
+        scratch_shapes=[pltpu.VMEM(m.shape, F32) for m in masters]
+        + [pltpu.VMEM(m.shape, F32) for m in moments]
+        + [pltpu.VMEM(m.shape, F32) for m in masters]
+        + [DMA((3, count)), DMA((2, count))],
+        compiler_params=pltpu.CompilerParams(vmem_limit_bytes=40000000),
+        cost_estimate=cost(10),
+        name="adam",
+    )(done, condition, bias_rows, *grads, *masters, *moments, *smalls)
 
 
 def local(
@@ -914,17 +1299,8 @@
     units = expand_weight.shape[1]
     tok, cot = tokens[0], cotangent[0]
 
-    def gather(weight):
-        return lax.all_gather(weight.astype(BF16), ("fsdp", "ctx"), axis=0, tiled=True)
-
-    output_full, expand_full, shrink_full = (
-        gather(output_weight), gather(expand_weight), gather(shrink_weight)
-    )
-
-    condition_act, silu_pull = jax.vjp(jax.nn.silu, condition)
-    condition_low = condition_act.astype(BF16)
+    condition_low = jax.nn.silu(condition).astype(BF16)
     condition_here = lax.dynamic_slice_in_dim(condition_low, mine * deep, deep, 1)
-    condition_pad = jnp.pad(condition_here, ((0, 16 - nf), (0, 0)))
     strips = part // 128
     high = -(-strips // 8) * 8
     bias_strips = jnp.pad(condition_bias.reshape(strips, 128), ((0, high - strips), (0, 0)))
@@ -932,162 +1308,57 @@
     offset = jnp.stack(
         [bias_pairs[:, 0], jnp.zeros_like(bias_pairs[:, 0]), bias_pairs[:, 1]], axis=1
     ).reshape(-1, 1)
-    joint_t, hidden_first, joint_full_t, mod = entry(
-        nf, nc, tok, joint_weight, condition_pad, modulate_weight, bias_strips, offset
-    )
-    mod = mod[:, :strips]
-    att_t, qkv, out, lse = attend(nc, joint_t)
-    value, middle, hidden_second = project(att_t, output_full, tok, mod, residual_bias)
+    condition_pad = jnp.pad(condition_here, ((0, 16 - nf), (0, 0)))
+    joint_t, hidden_first, joint_full_t, mod, output_full = entry(
+        nf, nc, tok, joint_weight, condition_pad, modulate_weight, bias_strips, offset,
+        output_weight,
+    )
+    output_full = output_full.reshape(width, -1)
+    half = units // 2
+    att_t, qkv, out, lse, expand_early = attend(nf, nc, joint_t, expand_weight[:, :half])
+    value, middle, hidden_second, expand_full, shrink_full = project(
+        nf, nc, part, att_t, output_full, tok, mod, residual_bias,
+        expand_early, expand_weight[:, half:], shrink_weight,
+    )
     (
         attn_low, mid_grad, shrink_grad, expand_grad, stats_second, hidden_stats, sh_cross, sh_own,
     ) = branch(
-        hidden_second, cot, expand_full, shrink_full, hidden_bias[None, :], mod, middle, value
-    )
-
-    def scatter(grad):
-        return lax.psum_scatter(
-            grad, ("fsdp", "ctx"), scatter_dimension=0, tiled=True
-        ).astype(F32)
-
-    shrink_sum, expand_sum = scatter(shrink_grad), scatter(expand_grad)
-    joint_grad, output_grad, head_bias, mixed, gate_second_grad = retreat(
-        nc, attn_low, output_full, att_t, qkv, out, lse, sh_cross, sh_own, middle, cot, mod,
-        residual_bias,
-    )
-    output_sum = scatter(output_grad)
-    joint_weight_grad, tokens_grad, stats_first = leave(
-        joint_grad, joint_full_t, hidden_first, tok, mid_grad, mod
-    )
-    joint_sum = scatter(joint_weight_grad)
-
-    stats = jnp.stack(
-        [
-            stats_first[0], stats_first[1], stats_second[2],
-            stats_second[0], stats_second[1], gate_second_grad[0],
-        ]
-    ).reshape(4, nc, part // nc // 128, 128)
-    stats = stats.transpose(1, 0, 2, 3).reshape(nc * 4, -1, 128)
-    residual = jnp.stack([stats_second[4], stats_second[3]]).reshape(nc, -1, 128)
-    residual = jnp.repeat(residual, 4, axis=0)
-    same = (jnp.arange(4) == t).astype(F32)[None, :, None, None]
-    hidden_piece = (hidden_stats.reshape(nc, 1, -1, 128) * same).reshape(nc * 4, -1, 128)
-    exact = (jnp.arange(nc * 4) == c * 4 + t).astype(F32)[:, None, None]
-    head_piece = head_bias[:, 0].reshape(1, -1, 128) * exact
-    pieces = jnp.concatenate([stats, residual, hidden_piece, head_piece], axis=1)
-    counts = [stats.shape[1], residual.shape[1], hidden_piece.shape[1], head_piece.shape[1]]
-    used = sum(counts)
-    pieces = jnp.pad(pieces, ((0, 0), (0, -(-used // 8) * 8 - used), (0, 0)))
-    sums = tally(nf, nc, pieces).reshape(nf, nc, -1, 128)
-    edge = [0]
-    for count in counts:
-        edge.append(edge[-1] + count)
-    modulation_grad = sums[:, :, edge[0] : edge[1]].reshape(nf, part)
-    residual_sum = jnp.sum(sums[:, :, edge[1] : edge[2]], axis=0).reshape(2, width)
-    hidden_sum = jnp.sum(sums[:, :, edge[2] : edge[3]], axis=0).reshape(units)
-    attention_sum = jnp.sum(sums[:, :, edge[3] : edge[4]], axis=0).reshape(-1)
-    condition_bias_sum = jnp.sum(modulation_grad, axis=0)
-    low_rows = condition_here.astype(F32)
-    if nf <= 4:
-        modulate_sum = sum(
-            low_rows[k][:, None] * modulation_grad[k][None, :] for k in range(nf)
-        )
-        wide = modulate_weight.astype(BF16).astype(F32)
-        condition_part = jnp.stack(
-            [jnp.sum(wide * modulation_grad[k][None, :], axis=1) for k in range(nf)]
-        )
-    else:
-        modulate_sum = lax.dot_general(
-            low_rows, modulation_grad, (((0,), (0,)), ((), ())),
-            precision=lax.Precision.HIGHEST, preferred_element_type=F32,
-        )
-        condition_part = lax.dot_general(
-            modulation_grad, modulate_weight.astype(BF16).astype(F32), (((1,), (1,)), ((), ())),
-            precision=lax.Precision.HIGHEST, preferred_element_type=F32,
-        )
-    lead_flag = (mine == 0).astype(F32)
-    tensor_lead = (t == 0).astype(F32)
-    weight_squares = (
-        jnp.sum(joint_sum * joint_sum)
-        + jnp.sum(output_sum * output_sum)
-        + jnp.sum(expand_sum * expand_sum)
-        + jnp.sum(shrink_sum * shrink_sum)
-        + jnp.sum(modulate_sum * modulate_sum)
-    )
-    bias_squares = (
-        jnp.sum(attention_sum * attention_sum)
-        + jnp.sum(hidden_sum * hidden_sum)
-        + jnp.sum(condition_bias_sum * condition_bias_sum)
-        + tensor_lead * jnp.sum(residual_sum * residual_sum)
-    )
-    squares_part = weight_squares + lead_flag * bias_squares
-    tall = -(-(nf + 1) // 8) * 8
-    lanes = max(128, deep)
-    piece = jnp.concatenate(
-        [
-            jnp.pad(condition_part, ((0, 0), (0, lanes - deep))),
-            jnp.full((1, lanes), squares_part),
-            jnp.zeros((tall - nf - 1, lanes), F32),
-        ]
-    )
-    done = finish(nf, nc, piece)
-    squares = jnp.sum(done[:, nf, 0])
-    grad_norm = jnp.sqrt(squares)
-    clip_factor = jnp.minimum(1.0, clip_limit / (grad_norm + 1e-06))
-    condition_act_grad = lax.dynamic_slice_in_dim(done, f, 1, 1)[:, 0, :deep].reshape(1, -1)
-    condition_all = jnp.broadcast_to(condition_act_grad, condition.shape)
-    condition_grad = lax.dynamic_slice_in_dim(silu_pull(condition_all)[0], f, 1, 0)
-
-    joint_updated, joint_averages = adam_step(
-        joint_weight, joint_moments, joint_sum, clip_factor, weight_decay
-    )
-    output_updated, output_averages = adam_step(
-        output_weight, output_moments, output_sum, clip_factor, weight_decay
-    )
-    expand_updated, expand_averages = adam_step(
-        expand_weight, expand_moments, expand_sum, clip_factor, weight_decay
-    )
-    shrink_updated, shrink_averages = adam_step(
-        shrink_weight, shrink_moments, shrink_sum, clip_factor, weight_decay
-    )
-    modulate_updated, modulate_averages = adam_step(
-        modulate_weight, modulate_moments, modulate_sum, clip_factor, weight_decay
-    )
-    attention_updated, attention_averages = adam_step(
-        attention_bias, attention_moments, attention_sum, clip_factor, 0.0
-    )
-    hidden_updated, hidden_averages = adam_step(
-        hidden_bias, hidden_moments, hidden_sum, clip_factor, 0.0
-    )
-    condition_updated, condition_averages = adam_step(
-        condition_bias, condition_moments, condition_bias_sum, clip_factor, 0.0
-    )
-    residual_updated, residual_averages = adam_step(
-        residual_bias, residual_moments, residual_sum, clip_factor, 0.0
-    )
+        part, hidden_second, cot, expand_full.reshape(width, units),
+        shrink_full.reshape(width, units), hidden_bias[None, :], mod, middle, value,
+    )
+    joint_grad, head_bias, mixed, gate_second_grad, shrink_sum, expand_parts, output_parts = retreat(
+        nf, nc, part, attn_low, output_full, att_t, qkv, out, lse, sh_cross, sh_own, middle, cot,
+        mod, residual_bias, shrink_grad, expand_grad,
+    )
+    joint_parts, own_tokens, stats_first, expand_sum, output_sum = leave(
+        nf, nc, part, joint_grad, joint_full_t, hidden_first, tok, mid_grad, mod,
+        expand_parts, output_parts,
+    )
+    tokens_grad, joint_sum, modulate_sum, bias_rows, done = settle(
+        nf, nc, part, joint_parts, own_tokens, stats_first, stats_second, gate_second_grad,
+        hidden_stats, head_bias, shrink_sum, expand_sum, output_sum, modulate_weight,
+        condition_pad.astype(F32),
+    )
+    weights = (joint_weight, output_weight, expand_weight, shrink_weight, modulate_weight)
+    moments = (joint_moments, output_moments, expand_moments, shrink_moments, modulate_moments)
+    grads = (joint_sum, output_sum, expand_sum, shrink_sum, modulate_sum)
+    smalls = (
+        attention_bias[None, :], attention_moments, hidden_bias[None, :], hidden_moments,
+        condition_bias[None, :], condition_moments, residual_bias, residual_moments,
+    )
+    results = adam(nf, nc, done, condition, bias_rows, grads, weights, moments, smalls)
+    updated = []
+    for k in range(5):
+        updated += [results[k], results[5 + k]]
+    for k in range(4):
+        new = results[10 + 2 * k]
+        updated += [new[0] if k < 3 else new, results[11 + 2 * k]]
     return (
         mixed.reshape(1, rows, width),
         tokens_grad.reshape(1, rows, width).astype(F32),
-        condition_grad,
-        grad_norm,
-        joint_updated,
-        joint_averages,
-        output_updated,
-        output_averages,
-        expand_updated,
-        expand_averages,
-        shrink_updated,
-        shrink_averages,
-        modulate_updated,
-        modulate_averages,
-        attention_updated,
-        attention_averages,
-        hidden_updated,
-        hidden_averages,
-        condition_updated,
-        condition_averages,
-        residual_updated,
-        residual_averages,
-    )
+        results[18],
+        results[19][0, 0],
+    ) + tuple(updated)
 
 
 def solution(mesh):

time: 662 us -> 431 us (0.65)
  waiting for transfers between devices: 196 us -> 0 us
  Pallas kernels: 355 us -> 403 us
  blocking collectives: 34.6 us -> 0 us
  other arithmetic: 40.3 us -> 6.22 us
  between operations: 22.8 us -> 1.47 us
  local copies, waits for them, and re-layouts: 6.79 us -> 14.2 us
    reduce_scatter x4 -> x0, waiting for transfers between devices: 194 us -> none  [scatter(): lax.psum_scatter(grad, ('fsdp', 'ctx'), scatter_dimension=0, tiled=True)]
    pallas_call x8 -> x7, Pallas kernels: 355 us -> 397 us  [run(): pl.pallas_call(body, out_shape=outs, in_specs=vmem(len(args)), out_specs=...]
    all_gather x1 -> x0, blocking collectives: 34.6 us -> none  [gather(): lax.all_gather(weight.astype(BF16), ('fsdp', 'ctx'), axis=0, tiled=True)]
    reduce_sum x14 -> x0, other arithmetic: 14.4 us -> none  [the longest x1 1.69 us: local(): jnp.sum(shrink_sum * shrink_sum)]
    another operation x14 -> x0, other arithmetic: 11.6 us -> none  [the longest x12 11.5 us: adam_step(): return (updated, jnp.stack([first_moment, jnp.sqrt(second_moment)]))]
    unnamed x57 -> x55, local copies, waits for them, and re-layouts: 1.45 us -> 10.1 us
  transfers between devices with their start and end apart: 6 -> 0, of which waited for: 3 -> 0; matrix products, arithmetic and copies ran while one was open for 3% -> 0% of each run, Pallas kernels for 34% -> 0%
where the time goes in v2:
time: 431 us; the launch traced here: 425 us
  Pallas kernels  403 us (94%)
  local copies, waits for them, and re-layouts  14.2 us (3%)
  other arithmetic  6.22 us (1%)
    pallas_call x7, Pallas kernels, run(): pl.pallas_call(body, out_shape=outs, in_specs=vmem(len(args)), out_specs=...  397 us
    unnamed x55, local copies, waits for them, and re-layouts  10.1 us

profile of v2, /device:TPU:0, one launch (start us, length us, event | category | flops | bytes accessed | tf_op | source)
XLA Modules:
  0.0 424.9 jit_solution(5506746950503471575)
XLA Ops:
  0.7 0.7 fusion
  2.0 0.8 reshape.87
  2.9 1.1 reshape.96.offset
  4.0 1.3 pad.9.cbias
  5.3 41.9 %entry.1 = (bf16[768,1024]{1,0:T(8,128)(2,1)}, bf16[1024,1024]{1,0:T(8,128)(2,1)}, bf16[768,1024]{1,0:T(8,128)(2,1)}, f32[4,16,128]{2,1,0:T(8,128)}, bf16[8,128,256]{2,1,0:T(8,128)(2,1)}) custom-call(bf16[1024,1024]{1,0:T(8,128)(2,1)} %bitcast.22, f32[128,768]{1,0:T(8,128)} %refs_5_.1, bf16[16,128]{1,0:T(8,128)(2,1)} %get-tuple-element.147.cond, ...), custom_call_target="tpu_custom_call" | custom-call | bytes 90000000 | tf_op jit(solution)/shard_map/entry/pallas_call | solution.py:68
  47.2 0.8 fusion.1
  48.1 67.4 %attend.1 = (bf16[256,1024]{1,0:T(8,128)(2,1)}, bf16[192,4096]{1,0:T(8,128)(2,1)}, f32[64,4096]{1,0:T(8,128)}, f32[1,4096]{1,0:T(1,128)}, bf16[8,128,512]{2,1,0:T(8,128)(2,1)}) custom-call(bf16[768,1024]{1,0:T(8,128)(2,1)} %get-tuple-element.82.x, f32[128,512]{1,0:T(8,128)} %get-tuple-element.143.extra), custom_call_target="tpu_custom_call" | custom-call | bytes 210000000 | tf_op jit(solution)/shard_map/attend/pallas_call | solution.py:68
  115.5 69.2 %project.1 = (f32[256,1024]{1,0:T(8,128)}, f32[256,1024]{1,0:T(8,128)}, bf16[4,256,1024]{2,1,0:T(8,128)(2,1)}, bf16[8,128,1024]{2,1,0:T(8,128)(2,1)}, bf16[8,128,1024]{2,1,0:T(8,128)(2,1)}) custom-call(bf16[256,1024]{1,0:T(8,128)(2,1)} %get-tuple-element.83.att, bf16[1024,256]{1,0:T(8,128)(2,1)} %bitcast.30, bf16[1024,1024]{1,0:T(8,128)(2,1)} %bitcast.23, ...), custom_call_target="tpu_custom_call" | custom-call | bytes 108000000 | tf_op jit(solution)/shard_map/project/pallas_call | solution.py:68
  184.7 45.7 %branch.1 = (bf16[4,256,1024]{2,1,0:T(8,128)(2,1)}, f32[256,1024]{1,0:T(8,128)}, bf16[1024,1024]{1,0:T(8,128)(2,1)}, bf16[1024,1024]{1,0:T(8,128)(2,1)}, f32[8,1...) custom-call(bf16[4,256,1024]{2,1,0:T(8,128)(2,1)} %get-tuple-element.87.hidden, ...), custom_call_target="tpu_custom_call" | custom-call | bytes 135000000 | tf_op jit(solution)/shard_map/branch/pallas_call | solution.py:68
  230.4 94.7 %retreat.1 = (bf16[4,192,1024]{2,1,0:T(8,128)(2,1)}, f32[128,128]{1,0:T(8,128)}, bf16[4,256,1024]{2,1,0:T(8,128)(2,1)}, f32[1,1024]{1,0:T(1,128)}, f32[128,1024]...) custom-call(bf16[4,256,1024]{2,1,0:T(8,128)(2,1)} %get-tuple-element.92.attn_low, ...), custom_call_target="tpu_custom_call" | custom-call | bytes 300000000 | tf_op jit(solution)/shard_map/retreat/pallas_call | solution.py:68
  325.2 38.7 %leave.1 = (bf16[4,128,768]{2,1,0:T(8,128)(2,1)}, bf16[256,1024]{1,0:T(8,128)(2,1)}, f32[8,1024]{1,0:T(8,128)}, f32[128,1024]{1,0:T(8,128)}, f32[128,256]{1,0:T(8,128)}) custom-call(bf16[4,192,1024]{2,1,0:T(8,128)(2,1)} %get-tuple-element.101.joint_grad, bf16[768,1024]{1,0:T(8,128)(2,1)} %get-tuple-element.102.weight_t, ...), custom_call_target="tpu_custom_call" | custom-call | bytes 90000000 | tf_op jit(solution)/shard_map/leave/pallas_call | solution.py:68
  364.1 38.8 %settle.1 = (bf16[4,256,1024]{2,1,0:T(8,128)(2,1)}, f32[128,768]{1,0:T(8,128)}, f32[128,1536]{1,0:T(8,128)}, f32[8,1536]{1,0:T(8,128)}, f32[8,8,128]{2,1,0:T(8,128)}) custom-call(bf16[4,128,768]{2,1,0:T(8,128)(2,1)} %get-tuple-element.107.joint_parts, bf16[256,1024]{1,0:T(8,128)(2,1)} %get-tuple-element.108.own_tokens, ...), custom_call_target="tpu_custom_call" | custom-call | bytes 90000000 | tf_op jit(solution)/shard_map/settle/pallas_call | solution.py:68
  403.2 1.4 copy-done.6
  404.6 1.2 copy-done.7
  405.8 1.2 copy-done.8
  407.0 1.1 copy-done.9
  408.1 1.1 copy-done.10
  409.3 1.0 copy-done.13
  410.3 0.8 copy-done.16
  411.1 0.8 copy-done.17
  411.8 6.4 %adam.1 = (f32[128,768]{1,0:T(8,128)}, f32[128,256]{1,0:T(8,128)}, f32[128,1024]{1,0:T(8,128)}, f32[128,1024]{1,0:T(8,128)}, f32[128,1536]{1,0:T(8,128)}, /*inde...) custom-call(f32[8,8,128]{2,1,0:T(8,128)S(1)} %copy-done.17, ...), custom_call_target="tpu_custom_call" | custom-call | bytes 30000000 | tf_op jit(solution)/shard_map/adam/pallas_call | solution.py:1253
  418.3 0.6 reduce
  418.9 4.2 bitcast_convert_fusion
  423.1 1.3 copy.45
  (51 shorter events, 0.9 us)
Async XLA Ops:
  2.9 44.3 %copy-start.2 = (f32[128,1024]{1,0:T(8,128)S(1)}, f32[128,1024]{1,0:T(8,128)}, u32[]{:S(2)}) copy-start(f32[128,1024]{1,0:T(8,128)} %refs_7_.1) | copy-start | bytes 1572868
  363.9 39.0 %copy-start.26 = (f32[1536]{0:T(1024)S(1)}, f32[1536]{0:T(1024)}, u32[]{:S(2)}) copy-start(f32[1536]{0:T(1024)} %param.38) | copy-start | bytes 18436
  363.9 39.1 %copy-start = (f32[128,1536]{1,0:T(8,128)S(1)}, f32[128,1536]{1,0:T(8,128)}, u32[]{:S(2)}) copy-start(f32[128,1536]{1,0:T(8,128)} %refs_9_.1) | copy-start | bytes 2359300
  363.9 39.1 %copy-start.1 = (f32[128,1024]{1,0:T(8,128)S(1)}, f32[128,1024]{1,0:T(8,128)}, u32[]{:S(2)}) copy-start(f32[128,1024]{1,0:T(8,128)} %refs_8_.1) | copy-start | bytes 1572868
  364.0 39.1 %copy-start.3 = (f32[128,1024]{1,0:T(8,128)S(1)}, f32[128,1024]{1,0:T(8,128)}, u32[]{:S(2)}) copy-start(f32[128,1024]{1,0:T(8,128)} %get-tuple-element.114.shrink_sum.refs_3_) | copy-start | bytes 1572868
  364.0 39.1 %copy-start.4 = (f32[128,1024]{1,0:T(8,128)S(1)}, f32[128,1024]{1,0:T(8,128)}, u32[]{:S(2)}) copy-start(f32[128,1024]{1,0:T(8,128)} %get-tuple-element.115.expand_sum.refs_2_) | copy-start | bytes 1572868
  364.0 39.1 %copy-start.5 = (f32[128,768]{1,0:T(8,128)S(1)}, f32[128,768]{1,0:T(8,128)}, u32[]{:S(2)}) copy-start(f32[128,768]{1,0:T(8,128)} %refs_5_.1) | copy-start | bytes 1179652
  364.0 39.0 %copy-start.11 = (f32[128,256]{1,0:T(8,128)S(1)}, f32[128,256]{1,0:T(8,128)}, u32[]{:S(2)}) copy-start(f32[128,256]{1,0:T(8,128)} %refs_6_.1) | copy-start | bytes 393220
  364.0 39.0 %copy-start.12 = (f32[128,256]{1,0:T(8,128)S(1)}, f32[128,256]{1,0:T(8,128)}, u32[]{:S(2)}) copy-start(f32[128,256]{1,0:T(8,128)} %get-tuple-element.116.output_sum.refs_1_) | copy-start | bytes 393220
  364.0 39.0 %copy-start.14 = (f32[2,128,256]{2,1,0:T(8,128)S(1)}, f32[2,128,256]{2,1,0:T(8,128)}, u32[]{:S(2)}) copy-start(f32[2,128,256]{2,1,0:T(8,128)} %refs_11_.1) | copy-start | bytes 786436
  364.0 39.0 %copy-start.15 = (f32[2,1024]{1,0:T(2,128)S(1)}, f32[2,1024]{1,0:T(2,128)}, u32[]{:S(2)}) copy-start(f32[2,1024]{1,0:T(2,128)} %refs_21_.1) | copy-start | bytes 24580
  364.0 39.0 %copy-start.18 = (f32[2,2,1024]{2,1,0:T(2,128)S(1)}, f32[2,2,1024]{2,1,0:T(2,128)}, u32[]{:S(2)}) copy-start(f32[2,2,1024]{2,1,0:T(2,128)} %refs_22_.1) | copy-start | bytes 49156
  364.0 39.0 %copy-start.19 = (f32[1024]{0:T(1024)S(1)}, f32[1024]{0:T(1024)}, u32[]{:S(2)}) copy-start(f32[1024]{0:T(1024)} %param.36) | copy-start | bytes 12292
  364.1 39.0 %copy-start.20 = (f32[2,1536]{1,0:T(2,128)S(1)}, f32[2,1536]{1,0:T(2,128)}, u32[]{:S(2)}) copy-start(f32[2,1536]{1,0:T(2,128)} %refs_20_.1) | copy-start | bytes 36868
  364.1 39.0 %copy-start.21 = (f32[2,1024]{1,0:T(2,128)S(1)}, f32[2,1024]{1,0:T(2,128)}, u32[]{:S(2)}) copy-start(f32[2,1024]{1,0:T(2,128)} %condition.1) | copy-start | bytes 24580
  364.1 39.0 %copy-start.22 = (f32[512]{0:T(512)S(1)}, f32[512]{0:T(512)}, u32[]{:S(2)}) copy-start(f32[512]{0:T(512)} %param.34) | copy-start | bytes 6148
  364.1 39.0 %copy-start.23 = (f32[2,1024]{1,0:T(2,128)S(1)}, f32[2,1024]{1,0:T(2,128)}, u32[]{:S(2)}) copy-start(f32[2,1024]{1,0:T(2,128)} %refs_18_.1) | copy-start | bytes 24580
  364.1 39.0 %copy-start.24 = (f32[2,512]{1,0:T(2,128)S(1)}, f32[2,512]{1,0:T(2,128)}, u32[]{:S(2)}) copy-start(f32[2,512]{1,0:T(2,128)} %refs_16_.1) | copy-start | bytes 12292
  403.1 1.4 copy-start.6
  404.6 1.2 copy-start.7
  405.8 1.2 copy-start.8
  407.0 1.1 copy-start.9
  408.1 1.1 copy-start.10
  418.9 4.2 copy-start.25
  (3 other events, 2.6 us)

commit v3 on v2

v3 whole, which is shorter than its diff:
```python
from functools import partial

import jax
import jax.numpy as jnp
from jax import lax
from jax.experimental import pallas as pl
from jax.experimental.pallas import tpu as pltpu
from jax.sharding import PartitionSpec as P

HEAD_DIM = 64
ADAM_STEP = 10
F32 = jnp.float32
BF16 = jnp.bfloat16
MESH = pl.DeviceIdType.MESH
DMA = pltpu.SemaphoreType.DMA

norm_epsilon = 1e-06
first_decay = 0.9
second_decay = 0.999
adam_epsilon = 1e-08
learning_rate = 0.05
weight_decay = 0.1
clip_limit = 1.0
GELU_SCALE = 0.7978845608028654
GELU_CUBE = 0.044715


def dot(a, b, ca, cb):
    return lax.dot_general(a, b, (((ca,), (cb,)), ((), ())), preferred_element_type=F32)


def aligned(start, size):
    return pl.ds(pl.multiple_of(start, size), size)


def greet(peers):
    barrier = pltpu.get_barrier_semaphore()
    for peer in peers:
        pl.semaphore_signal(barrier, inc=1, device_id=peer, device_id_type=MESH)
    pl.semaphore_wait(barrier, len(peers))


def remote(source, target, send_sem, recv_sem, peer):
    return pltpu.make_async_remote_copy(
        src_ref=source,
        dst_ref=target,
        send_sem=send_sem,
        recv_sem=recv_sem,
        device_id=peer,
        device_id_type=MESH,
    )


def vmem(count):
    return [pl.BlockSpec(memory_space=pltpu.VMEM)] * count


def shape(dims, dtype):
    return jax.ShapeDtypeStruct(dims, dtype)


def cost(micros, flops=0):
    return pl.CostEstimate(flops=flops, bytes_accessed=int(micros * 3.0e6), transcendentals=0)


def call(body, name, outs, scratch, ident, micros, megabytes):
    def run(*args):
        return pl.pallas_call(
            body,
            out_shape=outs,
            in_specs=vmem(len(args)),
            out_specs=vmem(len(outs)),
            scratch_shapes=scratch,
            compiler_params=pltpu.CompilerParams(
                collective_id=ident, has_side_effects=True, vmem_limit_bytes=megabytes << 20
            ),
            cost_estimate=cost(micros),
            name=name,
        )(*args)

    return run


def transposed(block):
    return block.astype(F32).T.astype(BF16)


def row_of(mod, start, width, part):
    pieces = []
    for at in range(start, start + width, 128):
        pieces.append(mod[at // part, pl.ds((at % part) // 128, 1), :])
    return jnp.concatenate(pieces, axis=1)


def centred(values):
    center = values - jnp.mean(values, axis=-1, keepdims=True)
    inverse = lax.rsqrt(jnp.mean(center * center, axis=-1, keepdims=True) + norm_epsilon)
    return center * inverse, inverse


def normal_back(grad, normed, inverse):
    return inverse * (
        grad
        - jnp.mean(grad, axis=-1, keepdims=True)
        - normed * jnp.mean(grad * normed, axis=-1, keepdims=True)
    )


class Gather:
    def __init__(self, buf, nf, nc, sems, parts):
        self.buf, self.nf, self.nc, self.sems, self.parts = buf, nf, nc, sems, parts
        self.columns = buf.shape[2] // parts

    def view(self, ctx, part):
        slot = lax.axis_index("fsdp") * self.nc + ctx
        return self.buf.at[slot, :, pl.ds(part * self.columns, self.columns)]

    def along(self, o, part):
        c = lax.axis_index("ctx")
        zs, zr = self.sems[4 * part : 4 * part + 2]
        view = self.view(c, part)
        return remote(view, view, zs.at[o], zr.at[o], {"ctx": lax.rem(c + o, self.nc)})

    def onward(self, part):
        c = lax.axis_index("ctx")
        zs, zr = self.sems[4 * part : 4 * part + 2]
        view = self.view(lax.rem(c + 2, self.nc), part)
        up = remote(view, view, zs.at[0], zr.at[3], {"ctx": lax.rem(c + 1, self.nc)})
        down = remote(view, view, zs.at[0], zr.at[1], {"ctx": lax.rem(c + 3, self.nc)})
        return up, down

    def across(self, o, part):
        f, c = lax.axis_index("fsdp"), lax.axis_index("ctx")
        xs, xr = self.sems[4 * part + 2 : 4 * part + 4]
        view = self.view(lax.rem(c - o + self.nc, self.nc), part)
        return [
            remote(view, view, xs.at[fo, o], xr.at[fo, o], {"fsdp": lax.rem(f + fo, self.nf)})
            for fo in range(1, self.nf)
        ]

    def start(self):
        c = lax.axis_index("ctx")
        for part in range(self.parts):
            self.along(2, part).start()
            pl.when(c != 3)(self.along(1, part).start)
            pl.when(c != 0)(self.along(3, part).start)
            for copy in self.across(0, part):
                copy.start()

    def relay_middle(self, part):
        c = lax.axis_index("ctx")
        self.along(2, part).wait_recv()
        up, down = self.onward(part)
        pl.when(c == 2)(up.start)
        pl.when(c == 1)(down.start)
        for copy in self.across(2, part):
            copy.start()

    def relay_rest(self, part):
        for o in (1, 3):
            self.along(o, part).wait_recv()
            for copy in self.across(o, part):
                copy.start()

    def relay(self):
        for part in range(self.parts):
            self.relay_middle(part)
        for part in range(self.parts):
            self.relay_rest(part)

    def arrive(self):
        for part in range(self.parts):
            for o in range(self.nc):
                for copy in self.across(o, part):
                    copy.wait_recv()

    def drain(self):
        c = lax.axis_index("ctx")
        for part in range(self.parts):
            for o in range(self.nc):
                for copy in self.across(o, part):
                    copy.wait_send()
            up, down = self.onward(part)
            self.along(2, part).wait_send()
            pl.when(c != 3)(self.along(1, part).wait_send)
            pl.when(c != 0)(self.along(3, part).wait_send)
            pl.when(c == 2)(up.wait_send)
            pl.when(c == 1)(down.wait_send)


def gather_sems(nf, nc, parts):
    return [DMA((nc,)), DMA((nc,)), DMA((nf, nc)), DMA((nf, nc))] * parts


class Sum:
    def __init__(self, sbuf, rbuf, send, recv):
        self.sbuf, self.rbuf, self.send, self.recv = sbuf, rbuf, send, recv
        self.places = tp_places()

    def copy(self, k):
        mine, partner, cross, far = self.places
        peer = cross if k == 2 else partner
        return remote(
            self.sbuf.at[k], self.rbuf.at[k], self.send.at[k], self.recv.at[k], {"tp": peer}
        )

    def give(self, k, value):
        self.sbuf[k] = value.astype(BF16)
        self.copy(k).start()

    def pass_on(self, value):
        self.copy(0).wait_recv()
        self.give(2, value + self.rbuf[0].astype(F32))

    def near(self, value):
        self.copy(1).wait_recv()
        return value + self.rbuf[1].astype(F32)

    def total(self, value):
        self.copy(2).wait_recv()
        return value + self.rbuf[2].astype(F32)

    def drain(self):
        for k in range(3):
            self.copy(k).wait_send()


class Share:
    def __init__(self, slots, send, recv):
        self.slots, self.send, self.recv = slots, send, recv
        self.places = tp_places()

    def copy(self, k):
        mine, partner, cross, far = self.places
        slot, peer = ((mine, cross), (mine, partner), (cross, partner))[k]
        view = self.slots.at[slot]
        return remote(view, view, self.send.at[k], self.recv.at[k], {"tp": peer})

    def start(self):
        self.copy(0).start()
        self.copy(1).start()

    def relay(self):
        self.copy(0).wait_recv()
        self.copy(2).start()

    def finish(self):
        self.copy(1).wait_recv()
        self.copy(2).wait_recv()
        for k in range(3):
            self.copy(k).wait_send()


def share_sems():
    return [DMA((3,)), DMA((3,))]


def swap_copies(grad, land, nf, send, recv):
    f = lax.axis_index("fsdp")
    return [
        remote(
            grad.at[lax.rem(f + fo, nf)], land.at[fo - 1], send.at[fo], recv.at[fo],
            {"fsdp": lax.rem(f + fo, nf)},
        )
        for fo in range(1, nf)
    ]


def swap_sum(grad, land, out, nf):
    f = lax.axis_index("fsdp")
    for k in range(out.shape[0]):
        total = grad[f, k].astype(F32)
        for fo in range(1, nf):
            total = total + land[fo - 1, k].astype(F32)
        out[k] = total.astype(BF16)


def deal_copies(parts, land, nc, send, recv):
    c = lax.axis_index("ctx")
    return [
        remote(
            parts.at[lax.rem(c + o, nc)], land.at[o - 1], send.at[o], recv.at[o],
            {"ctx": lax.rem(c + o, nc)},
        )
        for o in (1, 3, 2)
    ]


def deal_sum(parts, land, nc):
    total = parts[lax.axis_index("ctx")].astype(F32)
    for o in range(1, nc):
        total = total + land[o - 1].astype(F32)
    return total


def ring_peers(axis, size):
    here = lax.axis_index(axis)
    return [{axis: lax.rem(here + o, size)} for o in range(1, size)]


def weight_peers(nf, nc):
    f, c = lax.axis_index("fsdp"), lax.axis_index("ctx")
    peers = []
    for o in range(1, nf * nc):
        other = lax.rem(f * nc + c + o, nf * nc)
        peers.append({"fsdp": other // nc, "ctx": lax.rem(other, nc)})
    return peers


def tp_places():
    mine = lax.axis_index("tp")
    partner = mine + 1 - 2 * lax.rem(mine, 2)
    cross = lax.rem(mine + 2, 4)
    far = lax.rem(partner + 2, 4)
    return mine, partner, cross, far


def forward_body(
    nf, nc, part, tok, jweight, cond, modw, cbias, offset, oweight, eweight, sweight, bias,
    hidden, weight_t, mod, obuf, qkv, out, lse, land, ebuf, value, middle, hidden_two, sgat,
    wbuf, pbuf, pland, normed, joint, stage, keys, scores, sbuf, rbuf,
    psend, precv, msend, mrecv, send, recv, osend, orecv, tsend, trecv, gsend, grecv, *gsems,
):
    f, c, t = lax.axis_index("fsdp"), lax.axis_index("ctx"), lax.axis_index("tp")
    mine, partner, cross, far = tp_places()
    group = nf * nc
    slot = f * nc + c
    rows, width = tok.shape
    strips = part // 128
    hd = HEAD_DIM
    step = 256
    partial_mod = dot(cond[...], modw[...].astype(BF16), 1, 0)
    for latent in range(nf):
        for k in range(strips):
            pbuf[latent, pl.ds(k, 1), :] = partial_mod[latent : latent + 1, 128 * k : 128 * k + 128]
    joint_gather = Gather(wbuf, nf, nc, gsems[0:8], 2)
    output_gather = Gather(obuf, nf, nc, gsems[8:12], 1)
    expand_gather = Gather(ebuf, nf, nc, gsems[12:20], 2)
    shrink_gather = Gather(sgat, nf, nc, gsems[20:28], 2)
    wbuf[slot] = jweight[...].astype(BF16)
    greet(weight_peers(nf, nc) + ring_peers("tp", 4))
    pcopies = []
    for o, peer in zip(range(1, group), weight_peers(nf, nc)):
        copy = remote(pbuf.at[peer["fsdp"]], pland.at[slot], psend.at[o], precv.at[o], peer)
        copy.start()
        pcopies.append(copy)
    joint_gather.start()
    pland[slot] = pbuf[f]
    obuf[slot] = oweight[...].astype(BF16)
    ebuf[slot] = eweight[...].astype(BF16)
    sgat[slot] = sweight[...].astype(BF16)
    half = rows // 2
    for at in range(0, half, step):
        normed[at : at + step, :] = centred(tok[at : at + step, :].astype(F32))[0]
    joint_gather.relay_middle(0)
    for at in range(half, rows, step):
        normed[at : at + step, :] = centred(tok[at : at + step, :].astype(F32))[0]
    joint_gather.relay_middle(1)
    for copy in pcopies:
        copy.wait_recv()
    total_mod = pland[0]
    for k in range(1, group):
        total_mod = total_mod + pland[k]
    mod[t] = total_mod + cbias[...]
    mcopies = []
    for o, peer in zip(range(1, 4), ring_peers("tp", 4)):
        copy = remote(mod.at[t], mod.at[t], msend.at[o], mrecv.at[o], peer)
        copy.start()
        mcopies.append(copy)
    joint_gather.relay_rest(0)
    for copy in mcopies:
        copy.wait_recv()
    shift = row_of(mod, 0, width, part)
    scale = row_of(mod, width, width, part)
    for at in range(0, rows, step):
        hidden[at : at + step, :] = (
            normed[at : at + step, :] * (1.0 + scale) + shift
        ).astype(BF16)
    joint_gather.relay_rest(1)
    output_gather.start()
    joint_gather.arrive()
    deep = jweight.shape[0]
    for k in range(group):
        weight_t[:, k * deep : (k + 1) * deep] = transposed(wbuf[k])

    total = rows * nc
    bq, bk = scores.shape[1], 512
    per = rows // bq
    copies = []
    for o in (2, 1, 3, 0):
        dst = lax.rem(c + o, nc)
        where = aligned(dst * 3 * hd, 3 * hd)
        head = (dot(weight_t[where, :], hidden[...], 1, 1) + offset[where, :]).astype(BF16)
        if o == 0:
            qkv[:, aligned(c * rows, rows)] = head
        else:
            joint[where, :] = head
            copy = remote(
                joint.at[where, :], qkv.at[:, aligned(c * rows, rows)],
                send.at[o], recv.at[o], {"ctx": dst},
            )
            copy.start()
            copies.append(copy)
    output_gather.relay()
    for copy in copies:
        copy.wait_recv()
    expand_gather.start()
    for at in range(0, total, 1024):
        keys[at : at + 1024, :] = transposed(qkv[hd : 2 * hd, at : at + 1024])

    def back(o, owner):
        return remote(stage.at[owner], land.at[c], osend.at[o], orecv.at[o], {"ctx": owner})

    def block(i, carry):
        o = 1 + i // per
        owner = lax.rem(c + o, nc)
        sub = lax.rem(i, per)
        where = aligned(owner * rows + sub * bq, bq)
        query = qkv[0:hd, where] * BF16(hd**-0.5)
        peak = None
        for at in range(0, total, bk):
            s = dot(keys[at : at + bk, :], query, 1, 0)
            scores[at : at + bk, :] = s
            high = jnp.max(s.reshape(bk // 8, 8, bq), axis=0)
            peak = high if peak is None else jnp.maximum(peak, high)
        peak = jnp.max(peak, axis=0, keepdims=True)
        acc, mass = None, None
        for at in range(0, total, bk):
            p = jnp.exp(scores[at : at + bk, :] - peak)
            low = jnp.sum(p.reshape(bk // 8, 8, bq), axis=0)
            mass = low if mass is None else mass + low
            term = dot(qkv[2 * hd : 3 * hd, at : at + bk], p.astype(BF16), 1, 0)
            acc = term if acc is None else acc + term
        mass = jnp.sum(mass, axis=0, keepdims=True)
        acc = acc * (1.0 / mass)
        out[:, where] = acc
        lse[:, where] = peak + jnp.log(mass)
        stage[owner, :, aligned(sub * bq, bq)] = acc.astype(BF16)

        @pl.when(jnp.logical_and(sub == per - 1, o < nc))
        def _():
            back(o, owner).start()

        @pl.when(i == 2)
        def _():
            expand_gather.relay_middle(0)
            expand_gather.relay_middle(1)

        @pl.when(i == per * nc - 3)
        def _():
            expand_gather.relay_rest(0)

        @pl.when(i == per * nc - 2)
        def _():
            expand_gather.relay_rest(1)
            shrink_gather.start()

        return carry

    lax.fori_loop(0, per * nc, block, 0)
    land[c] = stage[c]
    for o in range(1, nc):
        back(o, lax.rem(c + o, nc)).wait_recv()

    own = value.shape[0]
    deep_out = obuf.shape[1]
    output_gather.arrive()

    def piece(at):
        block_ = land[:, :, aligned(at * own, own)].reshape(nc * hd, own)
        weight = obuf[...].reshape(group * deep_out, nc * hd)
        return dot(block_.astype(F32).T.astype(BF16), weight, 1, 1)

    summing = Sum(sbuf, rbuf, tsend, trecv)
    summing.give(0, piece(far))
    summing.give(1, piece(partner))
    summing.pass_on(piece(cross))
    held = summing.near(piece(mine)) + bias[0:1, :]
    shrink_gather.relay_middle(0)
    shrink_gather.relay_middle(1)
    held = summing.total(held)
    value[...] = held
    gate = row_of(mod, 2 * width, width, part)
    shift = row_of(mod, 3 * width, width, part)
    scale = row_of(mod, 4 * width, width, part)
    mid = tok[aligned(mine * own, own), :].astype(F32) + gate * held
    middle[...] = mid
    hidden_two[mine] = (centred(mid)[0] * (1.0 + scale) + shift).astype(BF16)
    sharing = Share(hidden_two, gsend, grecv)
    sharing.start()
    shrink_gather.relay_rest(0)
    shrink_gather.relay_rest(1)
    sharing.relay()
    for o in range(1, nc):
        back(o, lax.rem(c + o, nc)).wait_send()
    for copy in pcopies + mcopies + copies:
        copy.wait_send()
    expand_gather.arrive()
    shrink_gather.arrive()
    for gather in (joint_gather, output_gather, expand_gather, shrink_gather):
        gather.drain()
    summing.drain()
    sharing.finish()


def forward(nf, nc, part, tok, jweight, cond, modw, cbias, offset, oweight, eweight, sweight, bias):
    rows, width = tok.shape
    deep, columns = jweight.shape
    group = nf * nc
    own = rows // 4
    total = rows * nc
    hd = HEAD_DIM
    bq = min(512, rows)
    return call(
        partial(forward_body, nf, nc, part),
        "forward",
        (
            shape((rows, width), BF16),
            shape((columns, width), BF16),
            shape((4,) + cbias.shape, F32),
            shape((group,) + oweight.shape, BF16),
            shape((3 * hd, total), BF16),
            shape((hd, total), F32),
            shape((1, total), F32),
            shape((nc, hd, rows), BF16),
            shape((group,) + eweight.shape, BF16),
            shape((own, width), F32),
            shape((own, width), F32),
            shape((4, own, width), BF16),
            shape((group,) + sweight.shape, BF16),
        ),
        [
            pltpu.VMEM((group, deep, columns), BF16),
            pltpu.VMEM((nf,) + cbias.shape, F32),
            pltpu.VMEM((group,) + cbias.shape, F32),
            pltpu.VMEM((rows, width), F32),
            pltpu.VMEM((columns, rows), BF16),
            pltpu.VMEM((nc, hd, rows), BF16),
            pltpu.VMEM((total, hd), BF16),
            pltpu.VMEM((total, bq), F32),
            pltpu.VMEM((3, own, width), BF16),
            pltpu.VMEM((3, own, width), BF16),
            DMA((group,)), DMA((group,)), DMA((4,)), DMA((4,)),
            DMA((nc,)), DMA((nc,)), DMA((nc,)), DMA((nc,)),
        ]
        + share_sems() * 2
        + gather_sems(nf, nc, 7),
        1,
        150,
        50,
    )(tok, jweight, cond, modw, cbias, offset, oweight, eweight, sweight, bias)


def branch_body(
    nf, nc, part, hidden, cot, expand, shrink, hbias, mod, middle, value,
    attn_low, mid_grad, shrink_parts, expand_grad, stats, hstats, sh_cross, sh_own,
    gbuf, abuf, ebuf, slopes, shrink_grad, sland, sbuf, rbuf, shold,
    tsend, trecv, send, recv, gsend, grecv, ssend, srecv,
):
    mine, partner, cross, far = tp_places()
    own, width = middle.shape
    deep = shrink_parts.shape[1]
    gate_first = row_of(mod, 2 * width, width, part)
    scale_second = row_of(mod, 4 * width, width, part)
    gate_second = row_of(mod, 5 * width, width, part)
    greet(ring_peers("tp", 4) + ring_peers("fsdp", nf))
    for at in range(4):
        where = pl.ds(at * own, own)
        grad = gate_second * cot[where, :].astype(F32)
        gbuf[where, :] = grad.astype(BF16)
        u = dot(hidden[at], expand[...], 1, 0) + hbias[...]
        squared = u * u
        th = jnp.tanh(GELU_SCALE * (u + GELU_CUBE * squared * u))
        abuf[where, :] = (0.5 * u * (1.0 + th)).astype(BF16)
        slopes[where, :] = 0.5 * (1.0 + th) + 0.5 * u * (1.0 - th * th) * (
            GELU_SCALE * (1.0 + 3.0 * GELU_CUBE * squared)
        )
    step = 256
    for at in range(0, width, step):
        block = dot(gbuf[:, at : at + step], abuf[...], 0, 0).astype(BF16)
        for k in range(at // deep, (at + step) // deep):
            shrink_grad[k // nc, k % nc] = block[k * deep - at : (k + 1) * deep - at, :]
    swaps = swap_copies(shrink_grad, sland, nf, ssend, srecv)
    for copy in swaps:
        copy.start()
    column = None
    copies = []
    summing = Sum(sbuf, rbuf, send, recv)
    held = None
    for turn, at in enumerate((far, partner, cross, mine)):
        where = aligned(at * own, own)
        pull = dot(gbuf[where, :], shrink[...], 1, 0) * slopes[where, :]
        tally = jnp.sum(pull, axis=0, keepdims=True)
        column = tally if column is None else column + tally
        pull = pull.astype(BF16)
        ebuf[where, :] = pull
        back = dot(pull, expand[...], 1, 1)
        if turn < 2:
            summing.give(turn, back)
        elif turn == 2:
            summing.pass_on(back)
        else:
            held = summing.near(back)
    hstats[...] = column
    for turn, at in enumerate((far, partner, cross, mine)):
        forth = dot(abuf[aligned(at * own, own), :], shrink[...], 1, 1)
        if turn < 2:
            shold[turn] = forth.astype(BF16)
            copy = remote(
                shold.at[turn], shold.at[2 + turn], tsend.at[turn], trecv.at[turn], {"tp": partner}
            )
            copy.start()
            copies.append(copy)
        elif turn == 2:
            copies[0].wait_recv()
            sh_cross[...] = (forth + shold[2].astype(F32)).astype(BF16)
        else:
            copies[1].wait_recv()
            sh_own[...] = forth + shold[3].astype(F32)
    mine_rows = cot[aligned(mine * own, own), :].astype(F32)
    stats[3:4, :] = jnp.sum(gate_second * mine_rows, axis=0, keepdims=True)
    normed, inverse = centred(middle[...])
    grad_in = summing.total(held)
    stats[0:1, :] = jnp.sum(grad_in, axis=0, keepdims=True)
    stats[1:2, :] = jnp.sum(grad_in * normed, axis=0, keepdims=True)
    mgrad = mine_rows + normal_back(grad_in * (1.0 + scale_second), normed, inverse)
    mid_grad[...] = mgrad
    agrad = gate_first * mgrad
    attn_low[mine] = agrad.astype(BF16)
    sharing = Share(attn_low, gsend, grecv)
    sharing.start()
    stats[2:3, :] = jnp.sum(mgrad * value[...], axis=0, keepdims=True)
    stats[4:5, :] = jnp.sum(agrad, axis=0, keepdims=True)
    stats[5:8, :] = jnp.zeros((3, width), F32)
    flat = hidden.shape[0] * own
    for at in range(0, width, step):
        expand_grad[at : at + step, :] = dot(
            hidden[:, :, at : at + step].reshape(flat, step), ebuf[...], 0, 0
        ).astype(BF16)
    sharing.relay()
    for copy in swaps:
        copy.wait_recv()
    swap_sum(shrink_grad, sland, shrink_parts, nf)
    sharing.finish()
    summing.drain()
    for copy in copies + swaps:
        copy.wait_send()


def branch(nf, nc, part, hidden, cot, expand, shrink, hbias, mod, middle, value):
    rows, width = cot.shape
    own = rows // 4
    units = expand.shape[1]
    deep = width // (nf * nc)
    return call(
        partial(branch_body, nf, nc, part),
        "branch",
        (
            shape((4, own, width), BF16),
            shape((own, width), F32),
            shape((nc, deep, units), BF16),
            shape((width, units), BF16),
            shape((8, width), F32),
            shape((1, units), F32),
            shape((own, width), BF16),
            shape((own, width), F32),
        ),
        [
            pltpu.VMEM((rows, width), BF16),
            pltpu.VMEM((rows, units), BF16),
            pltpu.VMEM((rows, units), BF16),
            pltpu.VMEM((rows, units), F32),
            pltpu.VMEM((nf, nc, deep, units), BF16),
            pltpu.VMEM((nf - 1, nc, deep, units), BF16),
            pltpu.VMEM((3, own, width), BF16),
            pltpu.VMEM((3, own, width), BF16),
            pltpu.VMEM((4, own, width), BF16),
            DMA((2,)), DMA((2,)),
        ]
        + share_sems() * 2
        + [DMA((nf,))] * 2,
        2,
        40,
        50,
    )(hidden, cot, expand, shrink, hbias, mod, middle, value)


def backward_body(
    nf, nc, part, attn_low, obuf, att, qkv, out, lse, sh_cross, sh_own, middle, cot, mod, bias,
    shrink_parts, expand_grad, weight_t, hidden, tok, mid_grad, stats_second, hidden_stats,
    modw, low,
    mixed, tokens_grad, shrink_sum, expand_sum, output_sum, joint_sum, modulate_sum,
    bias_rows, done,
    dout, dost, keys, vals, dq, stage, rland, wt, delta, output_grad, eland, oland,
    expand_parts, output_parts, sdeal, edeal, odeal, joint_grad, sbuf, rbuf, jgrad, jland,
    joint_parts, jdeal, pieces, land, total_piece, gathered, fland, ftotal, gate_row,
    send, recv, jsend, jrecv, csend, crecv, gsend, grecv, tsend, trecv, hsend, hrecv,
    esend, erecv, osend, orecv, nsend, nrecv,
    d1s, d1r, d2s, d2r, d3s, d3r, d4s, d4r, asend, arecv, bsend, brecv, f1s, f1r, f2s, f2r,
):
    f, c, t = lax.axis_index("fsdp"), lax.axis_index("ctx"), lax.axis_index("tp")
    mine, partner, cross, far = tp_places()
    own, width = middle.shape
    rows = cot.shape[0]
    total = rows * nc
    hd = HEAD_DIM
    inner, group = nc * 4, nf * nc
    here, slot = c * 4 + t, f * nc + c
    bk = bq = 512
    per = rows // bk
    deep = joint_sum.shape[0]
    heads_wide = nc * hd
    expand_swap = swap_copies(expand_grad, eland, nf, esend, erecv)
    output_swap = swap_copies(output_grad, oland, nf, osend, orecv)
    joint_swap = swap_copies(jgrad, jland, nf, nsend, nrecv)
    shrink_deal = deal_copies(shrink_parts, sdeal, nc, d1s, d1r)
    expand_deal = deal_copies(expand_parts, edeal, nc, d2s, d2r)
    output_deal = deal_copies(output_parts, odeal, nc, d3s, d3r)
    joint_deal = deal_copies(joint_parts, jdeal, nc, d4s, d4r)
    wt[...] = transposed(obuf[...].reshape(width, heads_wide))
    low_grad = attn_low[...].reshape(rows, width)
    dost[...] = dot(wt[...], low_grad, 1, 1).astype(BF16)
    greet(
        [
            {"ctx": lax.rem(here + o, inner) // 4, "tp": lax.rem(lax.rem(here + o, inner), 4)}
            for o in range(1, inner)
        ]
        + weight_peers(nf, nc)
    )
    copies = []
    for o in (2, 1, 3):
        dst = lax.rem(c + o, nc)
        copy = remote(
            dost.at[aligned(dst * hd, hd), :], dout.at[:, aligned(c * rows, rows)],
            send.at[o], recv.at[o], {"ctx": dst},
        )
        copy.start()
        copies.append(copy)
    for copy in expand_swap:
        copy.start()
    crossing = remote(sh_cross, rland, csend, crecv, {"tp": cross})
    crossing.start()
    for copy in shrink_deal:
        copy.start()
    dout[:, aligned(c * rows, rows)] = dost[aligned(c * hd, hd), :]
    flat = dot(att[...].reshape(heads_wide, rows), low_grad, 1, 0).T.astype(BF16)
    output_grad[...] = flat.reshape(output_grad.shape)
    for copy in output_swap:
        copy.start()
    for at in range(0, total, 1024):
        keys[at : at + 1024, :] = transposed(qkv[hd : 2 * hd, at : at + 1024])
        vals[at : at + 1024, :] = transposed(qkv[2 * hd : 3 * hd, at : at + 1024])
    dq[...] = jnp.zeros_like(dq)
    for copy in copies:
        copy.wait_recv()
    for at in range(0, total, 1024):
        delta[:, at : at + 1024] = jnp.sum(
            dout[:, at : at + 1024].astype(F32) * out[:, at : at + 1024], axis=0, keepdims=True
        )
    sharing = Share(mixed, gsend, grecv)

    def kv_back(o, owner):
        return remote(
            stage.at[owner, pl.ds(hd, 2 * hd), :], joint_grad.at[c, pl.ds(hd, 2 * hd), :],
            jsend.at[0, o], jrecv.at[0, o], {"ctx": owner},
        )

    def q_back(o, owner):
        return remote(
            stage.at[owner, pl.ds(0, hd), :], joint_grad.at[c, pl.ds(0, hd), :],
            jsend.at[1, o], jrecv.at[1, o], {"ctx": owner},
        )

    def block(i, vsum):
        o = 1 + i // per
        owner = lax.rem(c + o, nc)
        sub = lax.rem(i, per)
        where = aligned(owner * rows + sub * bk, bk)
        key, val, key_t = keys[where, :], vals[where, :], qkv[hd : 2 * hd, where]
        dk, dv = None, None
        for at in range(0, total, bq):
            query = qkv[0:hd, at : at + bq] * BF16(hd**-0.5)
            grad = dout[:, at : at + bq]
            p = jnp.exp(dot(key, query, 1, 0) - lse[:, at : at + bq])
            ds = (p * (dot(val, grad, 1, 0) - delta[:, at : at + bq])).astype(BF16)
            tv = dot(grad, p.astype(BF16), 1, 1)
            tk = dot(query, ds, 1, 1)
            dv = tv if dv is None else dv + tv
            dk = tk if dk is None else dk + tk
            dq[:, at : at + bq] += dot(key_t, ds, 1, 0)
        put = aligned(sub * bk, bk)
        stage[owner, hd : 2 * hd, put] = dk.astype(BF16)
        stage[owner, 2 * hd : 3 * hd, put] = dv.astype(BF16)

        @pl.when(jnp.logical_and(sub == per - 1, o < nc))
        def _():
            kv_back(o, owner).start()

        @pl.when(i == 2)
        def _():
            crossing.wait_recv()
            value = sh_own[...] + rland[...].astype(F32) + bias[1:2, :]
            gate = row_of(mod, 5 * width, width, part)
            mixed[mine] = (middle[...] + gate * value).astype(BF16)
            sharing.start()
            gate_row[...] = jnp.sum(
                cot[aligned(mine * own, own), :].astype(F32) * value, axis=0, keepdims=True
            )

        @pl.when(i == 5)
        def _():
            for copy in expand_swap + output_swap:
                copy.wait_recv()
            swap_sum(expand_grad, eland, expand_parts, nf)
            swap_sum(output_grad, oland, output_parts, nf)
            sharing.relay()

        return vsum + jnp.sum(dv, axis=1, keepdims=True)

    vsum = lax.fori_loop(0, per * nc, block, jnp.zeros((hd, 1), F32))
    qsum = jnp.zeros((hd, 1), F32)
    for o in (2, 1, 3, 0):
        owner = lax.rem(c + o, nc)
        piece = dq[:, aligned(owner * rows, rows)] * (hd**-0.5)
        qsum = qsum + jnp.sum(piece, axis=1, keepdims=True)
        stage[owner, 0:hd, :] = piece.astype(BF16)
        if o > 0:
            q_back(o, owner).start()
    for copy in output_deal + expand_deal:
        copy.start()
    joint_grad[c] = stage[c]
    bias_column = jnp.concatenate([qsum, vsum], axis=0)
    for copy in shrink_deal:
        copy.wait_recv()
    shrink_total = deal_sum(shrink_parts, sdeal, nc)
    shrink_sum[...] = shrink_total
    squares = jnp.sum(shrink_total * shrink_total)
    for o in range(1, nc):
        owner = lax.rem(c + o, nc)
        kv_back(o, owner).wait_recv()
        q_back(o, owner).wait_recv()

    columns = weight_t.shape[0]
    flat_grad = joint_grad[...].reshape(columns, rows)
    rows_f = width // nf
    step = max(128, min(256, rows_f))
    for o in range(1, nf + 1):
        member = lax.rem(f + o, nf)
        for at in range(0, rows_f, step):
            lanes = aligned(member * rows_f + at, step) if step % 128 == 0 else None
            block_ = dot(flat_grad, hidden[:, lanes], 1, 0).T.astype(BF16)
            for k in range(at // deep, (at + step) // deep):
                jgrad[member, k] = block_[k * deep - at : (k + 1) * deep - at, :]
        if o < nf:
            joint_swap[o - 1].start()

    def piece_of(at):
        block_ = joint_grad[:, :, aligned(at * own, own)].reshape(columns, own)
        return dot(block_.astype(F32).T.astype(BF16), weight_t[...], 1, 0)

    summing = Sum(sbuf, rbuf, tsend, trecv)
    summing.give(0, piece_of(far))
    summing.give(1, piece_of(partner))
    summing.pass_on(piece_of(cross))
    held = summing.near(piece_of(mine))
    normed, inverse = centred(tok[aligned(mine * own, own), :].astype(F32))
    for copy in output_deal:
        copy.wait_recv()
    output_total = deal_sum(output_parts, odeal, nc)
    output_sum[...] = output_total
    squares = squares + jnp.sum(output_total * output_total)
    grad_in = summing.total(held)
    scale = row_of(mod, width, width, part)
    shift_row = jnp.sum(grad_in, axis=0, keepdims=True)
    scale_row = jnp.sum(grad_in * normed, axis=0, keepdims=True)

    slim = part // nc // 128
    share = 2 * width // nc // 128
    hshare = hidden_stats.shape[1] // nc // 128
    last = slim + share + hshare
    vectors = [
        shift_row, scale_row, stats_second[2:3, :],
        stats_second[0:1, :], stats_second[1:2, :], gate_row[...],
    ]
    residual = [stats_second[4:5, :], stats_second[3:4, :]]
    pieces[...] = jnp.zeros_like(pieces)
    for cc in range(nc):
        for tt in range(4):
            k = cc * 4 + tt
            for n in range(slim):
                at = ((tt * part // 128) + cc * slim + n) * 128
                pieces[k, n : n + 1, :] = vectors[at // width][:, at % width : at % width + 128]
            for n in range(share):
                at = (cc * share + n) * 128
                pieces[k, slim + n : slim + n + 1, :] = residual[at // width][
                    :, at % width : at % width + 128
                ]
        for n in range(hshare):
            at = (cc * hshare + n) * 128
            pieces[cc * 4 + t, slim + share + n : slim + share + n + 1, :] = hidden_stats[
                :, at : at + 128
            ]
    pieces[here, last : last + 1, :] = jnp.broadcast_to(bias_column, (2 * hd, 128)).T[0:1, :]
    first = []
    for o in range(1, inner):
        other = lax.rem(here + o, inner)
        copy = remote(
            pieces.at[other], land.at[here], asend.at[o], arecv.at[o],
            {"ctx": other // 4, "tp": lax.rem(other, 4)},
        )
        copy.start()
        first.append(copy)
    tokens_grad[mine] = (
        mid_grad[...] + normal_back(grad_in * (1.0 + scale), normed, inverse)
    ).astype(BF16)
    token_share = Share(tokens_grad, hsend, hrecv)
    token_share.start()
    for copy in joint_swap:
        copy.wait_recv()
    swap_sum(jgrad, jland, joint_parts, nf)
    for copy in joint_deal:
        copy.start()
    land[here] = pieces[here]
    for copy in first:
        copy.wait_recv()
    acc = land[0]
    for k in range(1, inner):
        acc = acc + land[k]
    total_piece[...] = acc
    gathered[slot] = acc
    second = []
    for o, peer in zip(range(1, group), weight_peers(nf, nc)):
        copy = remote(total_piece, gathered.at[slot], bsend.at[o], brecv.at[o], peer)
        copy.start()
        second.append(copy)
    for copy in expand_deal:
        copy.wait_recv()
    expand_total = deal_sum(expand_parts, edeal, nc)
    expand_sum[...] = expand_total
    squares = squares + jnp.sum(expand_total * expand_total)
    for copy in second:
        copy.wait_recv()

    grads = []
    for latent in range(nf):
        strips = []
        for cc in range(nc):
            for n in range(slim):
                strips.append(gathered[latent * nc + cc, n : n + 1, :])
        grads.append(jnp.concatenate(strips, axis=1))
    condition_bias = grads[0]
    for latent in range(1, nf):
        condition_bias = condition_bias + grads[latent]
    bias_rows[...] = jnp.zeros_like(bias_rows)
    bias_rows[0:1, 0:part] = condition_bias
    factors = low[...].T
    wide = modw[...].astype(BF16).astype(F32)
    outer = None
    ftotal[...] = jnp.zeros_like(ftotal)
    for latent in range(nf):
        term = factors[:, latent : latent + 1] * grads[latent]
        outer = term if outer is None else outer + term
        column = jnp.sum(wide * grads[latent], axis=1, keepdims=True)
        ftotal[latent : latent + 1, 0:deep] = jnp.broadcast_to(column, (deep, 128)).T[0:1, :]
    modulate_sum[...] = outer
    squares = squares + jnp.sum(outer * outer)

    def over(at, count):
        found = []
        for cc in range(nc):
            value = None
            for latent in range(nf):
                block_ = gathered[latent * nc + cc, at : at + count, :]
                value = block_ if value is None else value + block_
            for n in range(count):
                found.append(value[n : n + 1, :])
        return jnp.concatenate(found, axis=1)

    residual_sum = over(slim, share)
    hidden_sum = over(slim + share, hshare)
    head_sum = over(last, 1)
    bias_rows[1:2, 0 : hidden_sum.shape[1]] = hidden_sum
    bias_rows[2:3, 0 : head_sum.shape[1]] = head_sum
    bias_rows[3:4, 0:width] = residual_sum[:, 0:width]
    bias_rows[4:5, 0:width] = residual_sum[:, width : 2 * width]
    lead = (slot == 0).astype(F32)
    tensor_lead = (t == 0).astype(F32)
    squares = squares + lead * (
        jnp.sum(condition_bias * condition_bias)
        + jnp.sum(hidden_sum * hidden_sum)
        + jnp.sum(head_sum * head_sum)
        + tensor_lead * jnp.sum(residual_sum * residual_sum)
    )
    token_share.relay()
    for copy in joint_deal:
        copy.wait_recv()
    joint = deal_sum(joint_parts, jdeal, nc)
    joint_sum[...] = joint
    squares = squares + jnp.sum(joint * joint)
    ftotal[nf : nf + 1, :] = jnp.full((1, 128), squares)
    third = []
    for o, peer in zip(range(1, 4), ring_peers("tp", 4)):
        copy = remote(ftotal, fland.at[t], f1s.at[o], f1r.at[o], peer)
        copy.start()
        third.append(copy)
    fland[t] = ftotal[...]
    for copy in third:
        copy.wait_recv()
    done[slot] = fland[0] + fland[1] + fland[2] + fland[3]
    fourth = []
    for o, peer in zip(range(1, group), weight_peers(nf, nc)):
        copy = remote(done.at[slot], done.at[slot], f2s.at[o], f2r.at[o], peer)
        copy.start()
        fourth.append(copy)
    sharing.finish()
    token_share.finish()
    summing.drain()
    for o in range(1, nc):
        owner = lax.rem(c + o, nc)
        kv_back(o, owner).wait_send()
        q_back(o, owner).wait_send()
    deals = shrink_deal + expand_deal + output_deal + joint_deal
    for copy in copies + [crossing] + expand_swap + output_swap + joint_swap + deals:
        copy.wait_send()
    for copy in fourth:
        copy.wait_recv()
    for copy in first + second + third + fourth:
        copy.wait_send()


def backward(
    nf, nc, part, attn_low, obuf, att, qkv, out, lse, sh_cross, sh_own, middle, cot, mod, bias,
    shrink_parts, expand_grad, weight_t, hidden, tok, mid_grad, stats_second, hidden_stats,
    modw, low,
):
    rows, width = cot.shape
    own = rows // 4
    total = rows * nc
    hd = HEAD_DIM
    inner, group = nc * 4, nf * nc
    deep = width // group
    units = expand_grad.shape[1]
    columns = weight_t.shape[0]
    heads_wide = nc * hd
    expand_grad = expand_grad.reshape(nf, nc, deep, units)
    high = -(-(part // nc + 2 * width // nc + hidden_stats.shape[1] // nc + 128) // 1024) * 8
    tall = -(-(nf + 1) // 8) * 8
    return call(
        partial(backward_body, nf, nc, part),
        "backward",
        (
            shape((4, own, width), BF16),
            shape((4, own, width), BF16),
            shape((deep, units), F32),
            shape((deep, units), F32),
            shape((deep, heads_wide), F32),
            shape((deep, columns), F32),
            shape((deep, part), F32),
            shape((8, max(part, width, hidden_stats.shape[1])), F32),
            shape((group, tall, 128), F32),
        ),
        [
            pltpu.VMEM((hd, total), BF16),
            pltpu.VMEM((heads_wide, rows), BF16),
            pltpu.VMEM((total, hd), BF16),
            pltpu.VMEM((total, hd), BF16),
            pltpu.VMEM((hd, total), F32),
            pltpu.VMEM((nc, 3 * hd, rows), BF16),
            pltpu.VMEM((own, width), BF16),
            pltpu.VMEM((heads_wide, width), BF16),
            pltpu.VMEM((1, total), F32),
            pltpu.VMEM((nf, nc, deep, heads_wide), BF16),
            pltpu.VMEM((nf - 1, nc, deep, units), BF16),
            pltpu.VMEM((nf - 1, nc, deep, heads_wide), BF16),
            pltpu.VMEM((nc, deep, units), BF16),
            pltpu.VMEM((nc, deep, heads_wide), BF16),
            pltpu.VMEM((nc - 1, deep, units), BF16),
            pltpu.VMEM((nc - 1, deep, units), BF16),
            pltpu.VMEM((nc - 1, deep, heads_wide), BF16),
            pltpu.VMEM((nc, 3 * hd, rows), BF16),
            pltpu.VMEM((3, own, width), BF16),
            pltpu.VMEM((3, own, width), BF16),
            pltpu.VMEM((nf, nc, deep, columns), BF16),
            pltpu.VMEM((nf - 1, nc, deep, columns), BF16),
            pltpu.VMEM((nc, deep, columns), BF16),
            pltpu.VMEM((nc - 1, deep, columns), BF16),
            pltpu.VMEM((inner, high, 128), F32),
            pltpu.VMEM((inner, high, 128), F32),
            pltpu.VMEM((high, 128), F32),
            pltpu.VMEM((group, high, 128), F32),
            pltpu.VMEM((4, tall, 128), F32),
            pltpu.VMEM((tall, 128), F32),
            pltpu.VMEM((1, width), F32),
            DMA((nc,)), DMA((nc,)), DMA((2, nc)), DMA((2, nc)),
            DMA, DMA,
        ]
        + share_sems() * 3
        + [DMA((nf,))] * 6
        + [DMA((nc,))] * 8
        + [DMA((inner,))] * 2
        + [DMA((group,))] * 2
        + [DMA((4,))] * 2
        + [DMA((group,))] * 2,
        3,
        150,
        56,
    )(
        attn_low, obuf, att, qkv, out, lse, sh_cross, sh_own, middle, cot, mod, bias,
        shrink_parts, expand_grad, weight_t, hidden, tok, mid_grad, stats_second, hidden_stats,
        modw, low,
    )


def update(master, first, root, gradient, clip, decay_rate):
    scaled = clip * gradient
    first_moment = first_decay * first + (1.0 - first_decay) * scaled
    second_moment = second_decay * root * root + (1.0 - second_decay) * scaled * scaled
    new_root = jnp.sqrt(second_moment)
    first_hat = first_moment * (1.0 / (1.0 - first_decay**ADAM_STEP))
    second_hat = second_moment * (1.0 / (1.0 - second_decay**ADAM_STEP))
    updated = master - learning_rate * (
        first_hat / (jnp.sqrt(second_hat) + adam_epsilon) + decay_rate * master
    )
    return updated, first_moment, new_root


def adam_body(count, nf, nc, done, condition, bias_rows, *refs):
    grads = refs[:count]
    masters = refs[count : 2 * count]
    moments = refs[2 * count : 3 * count]
    smalls = refs[3 * count : 3 * count + 8]
    outs = refs[3 * count + 8 :]
    news = outs[:count]
    averages = outs[count : 2 * count]
    small_outs = outs[2 * count : 2 * count + 8]
    condition_grad, norm = outs[2 * count + 8 : 2 * count + 10]
    scratch = outs[2 * count + 10 :]
    wbufs = scratch[:count]
    mbufs = scratch[count : 2 * count]
    gbufs = scratch[2 * count : 3 * count]
    isem, osem = scratch[3 * count :]
    group = nf * nc
    f = lax.axis_index("fsdp")
    loads, stores = [], []
    for k in range(count):
        loads.append(
            (
                pltpu.make_async_copy(masters[k], wbufs[k], isem.at[0, k]),
                pltpu.make_async_copy(moments[k], mbufs[k], isem.at[1, k]),
                pltpu.make_async_copy(grads[k], gbufs[k], isem.at[2, k]),
            )
        )
        stores.append(
            (
                pltpu.make_async_copy(wbufs[k], news[k], osem.at[0, k]),
                pltpu.make_async_copy(mbufs[k], averages[k], osem.at[1, k]),
            )
        )
    for trio in loads:
        for copy in trio:
            copy.start()
    squares = done[0, nf : nf + 1, 0:1]
    for k in range(1, group):
        squares = squares + done[k, nf : nf + 1, 0:1]
    grad_norm = jnp.sqrt(squares)
    norm[...] = grad_norm
    clip = jnp.minimum(1.0, clip_limit / (grad_norm + 1e-06))
    deep = condition.shape[1] // group
    found = [done[k, pl.ds(f, 1), 0:deep] for k in range(group)]
    v = condition[pl.ds(f, 1), :]
    gate = 1.0 / (1.0 + jnp.exp(-v))
    condition_grad[...] = jnp.concatenate(found, axis=1) * (gate * (1.0 + v * (1.0 - gate)))
    for k in range(4):
        master, moment = smalls[2 * k], smalls[2 * k + 1]
        if k < 3:
            row = (2, 1, 0)[k]
            grad = bias_rows[row : row + 1, 0 : master.shape[1]]
            new, first, root = update(master[...], moment[0:1, :], moment[1:2, :], grad, clip, 0.0)
            small_outs[2 * k][...] = new
            small_outs[2 * k + 1][0:1, :] = first
            small_outs[2 * k + 1][1:2, :] = root
        else:
            grad = bias_rows[3:5, 0 : master.shape[1]]
            new, first, root = update(master[...], moment[0], moment[1], grad, clip, 0.0)
            small_outs[2 * k][...] = new
            small_outs[2 * k + 1][0] = first
            small_outs[2 * k + 1][1] = root
    for k in range(count):
        for copy in loads[k]:
            copy.wait()
        deep_k = wbufs[k].shape[0]
        step = min(16, deep_k)

        def rows(i, carry, k=k, step=step):
            at = pl.ds(pl.multiple_of(i * step, step), step)
            new, first, root = update(
                wbufs[k][at, :], mbufs[k][0, at, :], mbufs[k][1, at, :], gbufs[k][at, :],
                clip, weight_decay,
            )
            wbufs[k][at, :] = new
            mbufs[k][0, at, :] = first
            mbufs[k][1, at, :] = root
            return carry

        lax.fori_loop(0, deep_k // step, rows, 0)
        for copy in stores[k]:
            copy.start()
    for pair in stores:
        for copy in pair:
            copy.wait()


def adam(nf, nc, done, condition, bias_rows, grads, masters, moments, smalls):
    count = len(grads)
    anywhere = pl.BlockSpec(memory_space=pl.ANY)
    small_shapes = tuple(shape(a.shape, F32) for a in smalls)
    outs = (
        tuple(shape(m.shape, F32) for m in masters)
        + tuple(shape(m.shape, F32) for m in moments)
        + small_shapes
        + (shape((1, condition.shape[1]), F32), shape((1, 1), F32))
    )
    return pl.pallas_call(
        partial(adam_body, count, nf, nc),
        out_shape=outs,
        in_specs=vmem(3) + [anywhere] * (3 * count) + vmem(8),
        out_specs=[anywhere] * (2 * count) + vmem(10),
        scratch_shapes=[pltpu.VMEM(m.shape, F32) for m in masters]
        + [pltpu.VMEM(m.shape, F32) for m in moments]
        + [pltpu.VMEM(m.shape, F32) for m in masters]
        + [DMA((3, count)), DMA((2, count))],
        compiler_params=pltpu.CompilerParams(vmem_limit_bytes=32 << 20),
        cost_estimate=cost(10),
        name="adam",
    )(done, condition, bias_rows, *grads, *masters, *moments, *smalls)


def local(
    nf,
    nc,
    tokens,
    condition,
    cotangent,
    joint_weight,
    joint_moments,
    output_weight,
    output_moments,
    expand_weight,
    expand_moments,
    shrink_weight,
    shrink_moments,
    modulate_weight,
    modulate_moments,
    attention_bias,
    attention_moments,
    hidden_bias,
    hidden_moments,
    condition_bias,
    condition_moments,
    residual_bias,
    residual_moments,
):
    latent_count, rows, width = tokens.shape
    heads = joint_weight.shape[1] // (3 * HEAD_DIM)
    assert latent_count == 1 and heads == nc and lax.axis_size("tp") == 4
    f, c, t = lax.axis_index("fsdp"), lax.axis_index("ctx"), lax.axis_index("tp")
    mine = f * nc + c
    deep, part = modulate_weight.shape
    units = expand_weight.shape[1]
    tok, cot = tokens[0], cotangent[0]

    condition_low = jax.nn.silu(condition).astype(BF16)
    condition_here = lax.dynamic_slice_in_dim(condition_low, mine * deep, deep, 1)
    strips = part // 128
    high = -(-strips // 8) * 8
    bias_strips = jnp.pad(condition_bias.reshape(strips, 128), ((0, high - strips), (0, 0)))
    bias_pairs = attention_bias.reshape(heads, 2, HEAD_DIM)
    offset = jnp.stack(
        [bias_pairs[:, 0], jnp.zeros_like(bias_pairs[:, 0]), bias_pairs[:, 1]], axis=1
    ).reshape(-1, 1)
    condition_pad = jnp.pad(condition_here, ((0, 16 - nf), (0, 0)))
    (
        hidden_first, joint_full_t, mod, output_full, qkv, out, lse, att, expand_full,
        value, middle, hidden_second, shrink_full,
    ) = forward(
        nf, nc, part, tok, joint_weight, condition_pad, modulate_weight, bias_strips, offset,
        output_weight, expand_weight, shrink_weight, residual_bias,
    )
    (
        attn_low, mid_grad, shrink_parts, expand_grad, stats_second, hidden_stats,
        sh_cross, sh_own,
    ) = branch(
        nf, nc, part, hidden_second, cot, expand_full.reshape(width, units),
        shrink_full.reshape(width, units), hidden_bias[None, :], mod, middle, value,
    )
    (
        mixed, tokens_grad, shrink_sum, expand_sum, output_sum, joint_sum, modulate_sum,
        bias_rows, done,
    ) = backward(
        nf, nc, part, attn_low, output_full, att, qkv, out, lse, sh_cross, sh_own, middle, cot,
        mod, residual_bias, shrink_parts, expand_grad, joint_full_t, hidden_first, tok, mid_grad,
        stats_second, hidden_stats, modulate_weight, condition_pad.astype(F32),
    )
    weights = (joint_weight, output_weight, expand_weight, shrink_weight, modulate_weight)
    moments = (joint_moments, output_moments, expand_moments, shrink_moments, modulate_moments)
    grads = (joint_sum, output_sum, expand_sum, shrink_sum, modulate_sum)
    smalls = (
        attention_bias[None, :], attention_moments, hidden_bias[None, :], hidden_moments,
        condition_bias[None, :], condition_moments, residual_bias, residual_moments,
    )
    results = adam(nf, nc, done, condition, bias_rows, grads, weights, moments, smalls)
    updated = []
    for k in range(5):
        updated += [results[k], results[5 + k]]
    for k in range(4):
        new = results[10 + 2 * k]
        updated += [new[0] if k < 3 else new, results[11 + 2 * k]]
    return (
        mixed.reshape(1, rows, width),
        tokens_grad.reshape(1, rows, width).astype(F32),
        results[18],
        results[19][0, 0],
    ) + tuple(updated)


def solution(mesh):
    rows = P(("fsdp", "ctx"), "tp")
    pair = P(None, ("fsdp", "ctx"), "tp")
    tokens = P("fsdp", "ctx", None)
    small = (P("tp"), P(None, "tp"))
    return jax.shard_map(
        partial(local, mesh.shape["fsdp"], mesh.shape["ctx"]),
        mesh=mesh,
        in_specs=(tokens, P(), tokens) + (rows, pair) * 5 + small * 3 + (P(), P()),
        out_specs=(tokens, tokens, P("fsdp", None), P())
        + (rows, pair) * 5
        + small * 3
        + (P(), P()),
        check_vma=False,
    )
```

time: 431 us -> 375 us (0.87)
  Pallas kernels: 403 us -> 338 us
  local copies, waits for them, and re-layouts: 14.2 us -> 22.9 us
    pallas_call x7 -> x3, Pallas kernels: 397 us -> 331 us  [run(): pl.pallas_call(body, out_shape=outs, in_specs=vmem(len(args)), out_specs=...]
    unnamed x55 -> x87, local copies, waits for them, and re-layouts: 10.1 us -> 21 us
where the time goes in v3:
time: 375 us; the launch traced here: 368 us
  Pallas kernels  338 us (90%)
  local copies, waits for them, and re-layouts  22.9 us (6%)
  other arithmetic  6.22 us (2%)
    pallas_call x3, Pallas kernels, run(): pl.pallas_call(body, out_shape=outs, in_specs=vmem(len(args)), out_specs=...  331 us
    unnamed x87, local copies, waits for them, and re-layouts  21 us

profile of v3, /device:TPU:0, one launch (start us, length us, event | category | flops | bytes accessed | tf_op | source)
XLA Modules:
  0.0 368.4 jit_solution(15744837894876613575)
XLA Ops:
  2.0 0.8 reshape.81
  3.9 1.1 copy-done
  5.1 1.0 copy-done.2
  6.1 1.0 copy-done.4
  7.2 1.0 copy-done.6
  8.2 0.9 copy-done.16
  9.8 139.6 %forward.1 = (bf16[1024,1024]{1,0:T(8,128)(2,1)}, bf16[768,1024]{1,0:T(8,128)(2,1)}, f32[4,16,128]{2,1,0:T(8,128)S(1)}, bf16[8,128,256]{2,1,0:T(8,128)(2,1)S(1)}...) custom-call(bf16[1024,1024]{1,0:T(8,128)(2,1)} %bitcast.22, ...), custom_call_target="tpu_custom_call" | custom-call | bytes 450000000 | tf_op jit(solution)/shard_map/forward/pallas_call | solution.py:68
  149.4 0.8 copy-done.20
  150.2 0.8 copy-done.21
  151.6 47.1 %branch.1 = (bf16[4,256,1024]{2,1,0:T(8,128)(2,1)}, f32[256,1024]{1,0:T(8,128)S(1)}, bf16[4,128,1024]{2,1,0:T(8,128)(2,1)S(1)}, bf16[1024,1024]{1,0:T(8,128)(2,1...) custom-call(bf16[4,256,1024]{2,1,0:T(8,128)(2,1)} %get-tuple-element, ...), custom_call_target="tpu_custom_call" | custom-call | bytes 120000000 | tf_op jit(solution)/shard_map/branch/pallas_call | solution.py:68
  198.7 1.0 copy-done.11
  199.6 1.0 copy-done.12
  200.6 1.0 copy-done.13
  201.6 0.8 copy-done.22
  203.7 144.7 %backward.1 = (bf16[4,256,1024]{2,1,0:T(8,128)(2,1)}, bf16[4,256,1024]{2,1,0:T(8,128)(2,1)}, f32[128,1024]{1,0:T(8,128)}, f32[128,1024]{1,0:T(8,128)}, f32[128,2...) custom-call(bf16[4,256,1024]{2,1,0:T(8,128)(2,1)} %get-tuple-element.78.a, ...), custom_call_target="tpu_custom_call" | custom-call | bytes 450000000 | tf_op jit(solution)/shard_map/backward/pallas_call | solution.py:68
  348.7 1.1 copy-done.15
  349.8 1.0 copy-done.18
  350.8 1.0 copy-done.19
  351.9 1.0 copy-done.23
  352.9 0.9 copy-done.25
  353.8 0.8 copy-done.29
  355.3 6.4 %adam.1 = (f32[128,768]{1,0:T(8,128)}, f32[128,256]{1,0:T(8,128)}, f32[128,1024]{1,0:T(8,128)}, f32[128,1024]{1,0:T(8,128)}, f32[128,1536]{1,0:T(8,128)}, /*inde...) custom-call(f32[8,8,128]{2,1,0:T(8,128)S(1)} %copy-done.30, ...), custom_call_target="tpu_custom_call" | custom-call | bytes 30000000 | tf_op jit(solution)/shard_map/adam/pallas_call | solution.py:1223
  362.4 4.2 %bitcast_convert_fusion = f32[1,1024,1024]{2,1,0:T(8,128)} fusion(bf16[1,1024,1024]{2,1,0:T(8,128)(2,1)} %bitcast.24), kind=kLoop, calls=%fused_computation | loop fusion | flops 1048576 | bytes 6291456 | tf_op jit(solution)/shard_map/convert_element_type | solution.py:1320
  366.6 1.3 copy.45
  (78 shorter events, 6.5 us)
Async XLA Ops:
  3.9 1.1 copy-start
  5.1 1.0 copy-start.2
  9.8 141.8 %copy-start.33 = (f32[1024]{0:T(1024)S(1)}, f32[1024]{0:T(1024)}, u32[]{:S(2)}) copy-start(f32[1024]{0:T(1024)} %param.36) | copy-start | bytes 12292
  151.6 47.1 %copy-start.26 = (f32[4,16,128]{2,1,0:T(8,128)}, f32[4,16,128]{2,1,0:T(8,128)S(1)}, u32[]{:S(2)}) copy-start(f32[4,16,128]{2,1,0:T(8,128)S(1)} %get-tuple-element.75.mod) | copy-start | bytes 98308
  203.6 144.9 %copy-start.42 = (f32[1536]{0:T(1024)S(1)}, f32[1536]{0:T(1024)}, u32[]{:S(2)}) copy-start(f32[1536]{0:T(1024)} %param.38) | copy-start | bytes 18436
  203.6 144.9 %copy-start.1 = (f32[128,1536]{1,0:T(8,128)S(1)}, f32[128,1536]{1,0:T(8,128)}, u32[]{:S(2)}) copy-start(f32[128,1536]{1,0:T(8,128)} %refs_9_.1) | copy-start | bytes 2359300
  203.6 144.9 %copy-start.3 = (f32[128,1024]{1,0:T(8,128)S(1)}, f32[128,1024]{1,0:T(8,128)}, u32[]{:S(2)}) copy-start(f32[128,1024]{1,0:T(8,128)} %refs_7_.1) | copy-start | bytes 1572868
  203.6 144.9 %copy-start.5 = (f32[128,1024]{1,0:T(8,128)S(1)}, f32[128,1024]{1,0:T(8,128)}, u32[]{:S(2)}) copy-start(f32[128,1024]{1,0:T(8,128)} %refs_8_.1) | copy-start | bytes 1572868
  203.6 144.9 %copy-start.7 = (f32[128,768]{1,0:T(8,128)S(1)}, f32[128,768]{1,0:T(8,128)}, u32[]{:S(2)}) copy-start(f32[128,768]{1,0:T(8,128)} %refs_5_.1) | copy-start | bytes 1179652
  203.6 144.9 %copy-start.8 = (f32[2,128,1536]{2,1,0:T(8,128)S(1)}, f32[2,128,1536]{2,1,0:T(8,128)}, u32[]{:S(2)}) copy-start(f32[2,128,1536]{2,1,0:T(8,128)} %refs_14_.1) | copy-start | bytes 4718596
  203.6 144.9 %copy-start.9 = (f32[2,128,1024]{2,1,0:T(8,128)S(1)}, f32[2,128,1024]{2,1,0:T(8,128)}, u32[]{:S(2)}) copy-start(f32[2,128,1024]{2,1,0:T(8,128)} %refs_12_.1) | copy-start | bytes 3145732
  203.6 144.9 %copy-start.10 = (f32[2,128,1024]{2,1,0:T(8,128)S(1)}, f32[2,128,1024]{2,1,0:T(8,128)}, u32[]{:S(2)}) copy-start(f32[2,128,1024]{2,1,0:T(8,128)} %refs_13_.1) | copy-start | bytes 3145732
  203.6 144.9 %copy-start.14 = (f32[2,128,768]{2,1,0:T(8,128)S(1)}, f32[2,128,768]{2,1,0:T(8,128)}, u32[]{:S(2)}) copy-start(f32[2,128,768]{2,1,0:T(8,128)} %refs_10_.1) | copy-start | bytes 2359300
  203.6 144.9 %copy-start.17 = (f32[128,256]{1,0:T(8,128)S(1)}, f32[128,256]{1,0:T(8,128)}, u32[]{:S(2)}) copy-start(f32[128,256]{1,0:T(8,128)} %refs_6_.1) | copy-start | bytes 393220
  203.6 144.9 %copy-start.24 = (f32[2,128,256]{2,1,0:T(8,128)S(1)}, f32[2,128,256]{2,1,0:T(8,128)}, u32[]{:S(2)}) copy-start(f32[2,128,256]{2,1,0:T(8,128)} %refs_11_.1) | copy-start | bytes 786436
  203.7 144.9 %copy-start.28 = (f32[2,1024]{1,0:T(2,128)S(1)}, f32[2,1024]{1,0:T(2,128)}, u32[]{:S(2)}) copy-start(f32[2,1024]{1,0:T(2,128)} %refs_21_.1) | copy-start | bytes 24580
  203.7 144.9 %copy-start.32 = (f32[2,2,1024]{2,1,0:T(2,128)S(1)}, f32[2,2,1024]{2,1,0:T(2,128)}, u32[]{:S(2)}) copy-start(f32[2,2,1024]{2,1,0:T(2,128)} %refs_22_.1) | copy-start | bytes 49156
  203.7 144.9 %copy-start.35 = (f32[2,1536]{1,0:T(2,128)S(1)}, f32[2,1536]{1,0:T(2,128)}, u32[]{:S(2)}) copy-start(f32[2,1536]{1,0:T(2,128)} %refs_20_.1) | copy-start | bytes 36868
  203.7 144.9 %copy-start.36 = (f32[2,1024]{1,0:T(2,128)S(1)}, f32[2,1024]{1,0:T(2,128)}, u32[]{:S(2)}) copy-start(f32[2,1024]{1,0:T(2,128)} %condition.1) | copy-start | bytes 24580
  203.7 144.9 %copy-start.37 = (f32[512]{0:T(512)S(1)}, f32[512]{0:T(512)}, u32[]{:S(2)}) copy-start(f32[512]{0:T(512)} %param.34) | copy-start | bytes 6148
  203.7 144.9 %copy-start.38 = (f32[2,1024]{1,0:T(2,128)S(1)}, f32[2,1024]{1,0:T(2,128)}, u32[]{:S(2)}) copy-start(f32[2,1024]{1,0:T(2,128)} %refs_18_.1) | copy-start | bytes 24580
  203.7 144.9 %copy-start.39 = (f32[2,512]{1,0:T(2,128)S(1)}, f32[2,512]{1,0:T(2,128)}, u32[]{:S(2)}) copy-start(f32[2,512]{1,0:T(2,128)} %refs_16_.1) | copy-start | bytes 12292
  348.7 1.1 copy-start.15
  362.4 4.2 %copy-start.41 = (bf16[4,256,1024]{2,1,0:T(8,128)(2,1)S(1)}, bf16[4,256,1024]{2,1,0:T(8,128)(2,1)}, u32[]{:S(2)}) copy-start(bf16[4,256,1024]{2,1,0:T(8,128)(2,1)} %get-tuple-element.93) | copy-start | bytes 6291460
  (19 other events, 16.3 us)

commit v4 on v3

v4 whole, which is shorter than its diff:
```python
from functools import partial

import jax
import jax.numpy as jnp
from jax import lax
from jax.experimental import pallas as pl
from jax.experimental.pallas import tpu as pltpu
from jax.sharding import PartitionSpec as P

HEAD_DIM = 64
ADAM_STEP = 10
F32 = jnp.float32
BF16 = jnp.bfloat16
MESH = pl.DeviceIdType.MESH
DMA = pltpu.SemaphoreType.DMA

norm_epsilon = 1e-06
first_decay = 0.9
second_decay = 0.999
adam_epsilon = 1e-08
learning_rate = 0.05
weight_decay = 0.1
clip_limit = 1.0
GELU_SCALE = 0.7978845608028654
GELU_CUBE = 0.044715


def dot(a, b, ca, cb):
    return lax.dot_general(a, b, (((ca,), (cb,)), ((), ())), preferred_element_type=F32)


def aligned(start, size):
    return pl.ds(pl.multiple_of(start, size), size)


def greet(peers):
    barrier = pltpu.get_barrier_semaphore()
    for peer in peers:
        pl.semaphore_signal(barrier, inc=1, device_id=peer, device_id_type=MESH)
    pl.semaphore_wait(barrier, len(peers))


def remote(source, target, send_sem, recv_sem, peer):
    return pltpu.make_async_remote_copy(
        src_ref=source,
        dst_ref=target,
        send_sem=send_sem,
        recv_sem=recv_sem,
        device_id=peer,
        device_id_type=MESH,
    )


def vmem(count):
    return [pl.BlockSpec(memory_space=pltpu.VMEM)] * count


def shape(dims, dtype):
    return jax.ShapeDtypeStruct(dims, dtype)


def cost(micros, flops=0):
    return pl.CostEstimate(flops=flops, bytes_accessed=int(micros * 3.0e6), transcendentals=0)


def call(body, name, outs, scratch, ident, micros, megabytes, ins=(), to=()):
    def run(*args):
        return pl.pallas_call(
            body,
            out_shape=outs,
            in_specs=[pl.BlockSpec(memory_space=pltpu.HBM if k in ins else pltpu.VMEM) for k in range(len(args))],
            out_specs=[pl.BlockSpec(memory_space=pltpu.HBM if k in to else pltpu.VMEM) for k in range(len(outs))],
            scratch_shapes=scratch,
            compiler_params=pltpu.CompilerParams(
                collective_id=ident, has_side_effects=True, vmem_limit_bytes=megabytes << 20
            ),
            cost_estimate=cost(micros),
            name=name,
        )(*args)

    return run


def transposed(block):
    return block.astype(F32).T.astype(BF16)


def row_of(mod, start, width, part):
    pieces = []
    for at in range(start, start + width, 128):
        pieces.append(mod[at // part, pl.ds((at % part) // 128, 1), :])
    return jnp.concatenate(pieces, axis=1)


def centred(values):
    center = values - jnp.mean(values, axis=-1, keepdims=True)
    inverse = lax.rsqrt(jnp.mean(center * center, axis=-1, keepdims=True) + norm_epsilon)
    return center * inverse, inverse


def normal_back(grad, normed, inverse):
    return inverse * (
        grad
        - jnp.mean(grad, axis=-1, keepdims=True)
        - normed * jnp.mean(grad * normed, axis=-1, keepdims=True)
    )


class Gather:
    def __init__(self, buf, nf, nc, sems, parts, first=0):
        self.buf, self.nf, self.nc, self.sems = buf, nf, nc, sems
        self.first, self.parts = first, range(first, parts)
        self.columns = buf.shape[2] // parts

    def sem(self, part, kind):
        return self.sems[4 * (part - self.first) + kind]

    def view(self, ctx, part):
        slot = lax.axis_index("fsdp") * self.nc + ctx
        return self.buf.at[slot, :, pl.ds(part * self.columns, self.columns)]

    def along(self, o, part):
        c = lax.axis_index("ctx")
        zs, zr = self.sem(part, 0), self.sem(part, 1)
        view = self.view(c, part)
        return remote(view, view, zs.at[o], zr.at[o], {"ctx": lax.rem(c + o, self.nc)})

    def onward(self, part):
        c = lax.axis_index("ctx")
        zs, zr = self.sem(part, 0), self.sem(part, 1)
        view = self.view(lax.rem(c + 2, self.nc), part)
        up = remote(view, view, zs.at[0], zr.at[3], {"ctx": lax.rem(c + 1, self.nc)})
        down = remote(view, view, zs.at[0], zr.at[1], {"ctx": lax.rem(c + 3, self.nc)})
        return up, down

    def across(self, o, part):
        f, c = lax.axis_index("fsdp"), lax.axis_index("ctx")
        xs, xr = self.sem(part, 2), self.sem(part, 3)
        view = self.view(lax.rem(c - o + self.nc, self.nc), part)
        return [
            remote(view, view, xs.at[fo, o], xr.at[fo, o], {"fsdp": lax.rem(f + fo, self.nf)})
            for fo in range(1, self.nf)
        ]

    def start(self):
        c = lax.axis_index("ctx")
        for part in self.parts:
            self.along(2, part).start()
            pl.when(c != 3)(self.along(1, part).start)
            pl.when(c != 0)(self.along(3, part).start)
            for copy in self.across(0, part):
                copy.start()

    def relay_middle(self, part):
        c = lax.axis_index("ctx")
        self.along(2, part).wait_recv()
        up, down = self.onward(part)
        pl.when(c == 2)(up.start)
        pl.when(c == 1)(down.start)
        for copy in self.across(2, part):
            copy.start()

    def relay_rest(self, part):
        for o in (1, 3):
            self.along(o, part).wait_recv()
            for copy in self.across(o, part):
                copy.start()

    def relay(self):
        for part in self.parts:
            self.relay_middle(part)
        for part in self.parts:
            self.relay_rest(part)

    def arrive(self):
        for part in self.parts:
            for o in range(self.nc):
                for copy in self.across(o, part):
                    copy.wait_recv()

    def drain(self):
        c = lax.axis_index("ctx")
        for part in self.parts:
            for o in range(self.nc):
                for copy in self.across(o, part):
                    copy.wait_send()
            up, down = self.onward(part)
            self.along(2, part).wait_send()
            pl.when(c != 3)(self.along(1, part).wait_send)
            pl.when(c != 0)(self.along(3, part).wait_send)
            pl.when(c == 2)(up.wait_send)
            pl.when(c == 1)(down.wait_send)


def gather_sems(nf, nc, parts):
    return [DMA((nc,)), DMA((nc,)), DMA((nf, nc)), DMA((nf, nc))] * parts


class Sum:
    def __init__(self, sbuf, rbuf, send, recv):
        self.sbuf, self.rbuf, self.send, self.recv = sbuf, rbuf, send, recv
        self.places = tp_places()

    def copy(self, k):
        mine, partner, cross, far = self.places
        peer = cross if k == 2 else partner
        return remote(
            self.sbuf.at[k], self.rbuf.at[k], self.send.at[k], self.recv.at[k], {"tp": peer}
        )

    def give(self, k, value):
        self.sbuf[k] = value.astype(BF16)
        self.copy(k).start()

    def pass_on(self, value):
        self.copy(0).wait_recv()
        self.give(2, value + self.rbuf[0].astype(F32))

    def near(self, value):
        self.copy(1).wait_recv()
        return value + self.rbuf[1].astype(F32)

    def total(self, value):
        self.copy(2).wait_recv()
        return value + self.rbuf[2].astype(F32)

    def drain(self):
        for k in range(3):
            self.copy(k).wait_send()


class Share:
    def __init__(self, slots, send, recv):
        self.slots, self.send, self.recv = slots, send, recv
        self.places = tp_places()

    def copy(self, k):
        mine, partner, cross, far = self.places
        slot, peer = ((mine, cross), (mine, partner), (cross, partner))[k]
        view = self.slots.at[slot]
        return remote(view, view, self.send.at[k], self.recv.at[k], {"tp": peer})

    def start(self):
        self.copy(0).start()
        self.copy(1).start()

    def relay(self):
        self.copy(0).wait_recv()
        self.copy(2).start()

    def finish(self):
        self.copy(1).wait_recv()
        self.copy(2).wait_recv()
        for k in range(3):
            self.copy(k).wait_send()


def share_sems():
    return [DMA((3,)), DMA((3,))]


class Scatter:
    def __init__(self, nf, nc, grad, parts, xland, zland, xsend, xrecv, zsend, zrecv, lanes=None):
        f, c = lax.axis_index("fsdp"), lax.axis_index("ctx")
        self.nf, self.nc, self.grad, self.parts, self.xland, self.zland = (
            nf, nc, grad, parts, xland, zland,
        )
        self.lanes = slice(None) if lanes is None else pl.ds(*lanes)
        keep = self.lanes
        self.swaps, self.deals = [], []
        for fo in range(1, nf) if grad is not None else ():
            member = lax.rem(f + fo, nf)
            self.swaps.append(
                remote(
                    grad.at[member, :, :, keep], xland.at[fo - 1, :, :, keep],
                    xsend.at[fo], xrecv.at[fo], {"fsdp": member},
                )
            )
        for o in (2, 1, 3):
            member = lax.rem(c + o, nc)
            self.deals.append(
                remote(
                    parts.at[member, :, keep], zland.at[o - 1, :, keep], zsend.at[o], zrecv.at[o],
                    {"ctx": member},
                )
            )

    def swap(self):
        for copy in self.swaps:
            copy.start()

    def swapped(self):
        f = lax.axis_index("fsdp")
        for copy in self.swaps:
            copy.wait_recv()
        for k in range(self.nc):
            total = self.grad[f, k, :, self.lanes].astype(F32)
            for fo in range(1, self.nf):
                total = total + self.xland[fo - 1, k, :, self.lanes].astype(F32)
            self.parts[k, :, self.lanes] = total.astype(BF16)

    def deal(self):
        for copy in self.deals:
            copy.start()

    def dealt(self):
        for copy in self.deals:
            copy.wait_recv()
        total = self.parts[lax.axis_index("ctx"), :, self.lanes].astype(F32)
        for o in range(1, self.nc):
            total = total + self.zland[o - 1, :, self.lanes].astype(F32)
        return total

    def drain(self, swaps=True, deals=True):
        for copy in (self.swaps if swaps else []) + (self.deals if deals else []):
            copy.wait_send()


def ring_peers(axis, size):
    here = lax.axis_index(axis)
    return [{axis: lax.rem(here + o, size)} for o in range(1, size)]


def weight_peers(nf, nc):
    f, c = lax.axis_index("fsdp"), lax.axis_index("ctx")
    peers = []
    for o in range(1, nf * nc):
        other = lax.rem(f * nc + c + o, nf * nc)
        peers.append({"fsdp": other // nc, "ctx": lax.rem(other, nc)})
    return peers


def all_peers(nf, nc):
    f, c, t = lax.axis_index("fsdp"), lax.axis_index("ctx"), lax.axis_index("tp")
    count = nf * nc * 4
    peers = []
    for o in range(1, count):
        other = lax.rem((f * nc + c) * 4 + t + o, count)
        peers.append(
            {"fsdp": other // (nc * 4), "ctx": lax.rem(other // 4, nc), "tp": lax.rem(other, 4)}
        )
    return peers


def turned(mine, turn):
    high = lax.rem(mine // 2 + turn // 2, 2)
    return high * 2 + lax.rem(mine + turn, 2)


def tp_places():
    mine = lax.axis_index("tp")
    partner = mine + 1 - 2 * lax.rem(mine, 2)
    cross = lax.rem(mine + 2, 4)
    far = lax.rem(partner + 2, 4)
    return mine, partner, cross, far


def load_all(pairs, sems):
    copies = []
    for k, (source, target) in enumerate(pairs):
        copy = pltpu.make_async_copy(source, target, sems.at[k])
        copy.start()
        copies.append(copy)
    return copies


def head_peers(nc):
    c, t = lax.axis_index("ctx"), lax.axis_index("tp")
    inner = nc * 4
    peers = []
    for o in range(1, inner):
        other = lax.rem(c * 4 + t + o, inner)
        peers.append({"ctx": other // 4, "tp": lax.rem(other, 4)})
    return peers


def forward_body(
    nf, nc, part, tok_hbm, jw_hbm, cond, modw_hbm, cbias, offset, ow_hbm, ew_hbm, bias, sw_hbm,
    hidden_hbm, weight_hbm, mod, out_t_hbm, qkv_hbm, out_hbm, lse, land_hbm, ebuf_hbm,
    value, middle, hidden_two_hbm, sbuf_hbm,
    sweight, sbuf, tok, jweight, modw, oweight, eweight, out_t, qkv, out, ebuf, hidden_two,
    hidden, weight_t, wbuf, obuf, oall, pbuf, pland, normed, joint, stage, land, keys, scores,
    lsem, ssem, psend, precv, msend, mrecv, send, recv, osend, orecv, hsend, hrecv, asend, arecv,
    *gsems,
):
    f, c, t = lax.axis_index("fsdp"), lax.axis_index("ctx"), lax.axis_index("tp")
    mine, partner, cross, far = tp_places()
    group = nf * nc
    slot = f * nc + c
    rows, width = tok.shape
    own = rows // 4
    strips = part // 128
    hd = HEAD_DIM
    step = 128
    loads = load_all(
        (
            (jw_hbm, jweight), (modw_hbm, modw), (tok_hbm, tok), (ow_hbm, oweight),
            (ew_hbm, eweight), (sw_hbm.at[:, pl.ds(0, sweight.shape[1])], sweight),
        ),
        lsem,
    )
    joint_gather = Gather(wbuf, nf, nc, gsems[0:8], 2)
    output_gather = Gather(obuf, nf, nc, gsems[8:12], 1)
    expand_gather = Gather(ebuf, nf, nc, gsems[12:20], 2)
    shrink_gather = Gather(sbuf, nf, nc, gsems[20:24], 1)
    loads[0].wait()
    wbuf[slot] = jweight[...].astype(BF16)
    greet(weight_peers(nf, nc) + head_peers(nc))
    joint_gather.start()
    loads[1].wait()
    partial_mod = dot(cond[...], modw[...].astype(BF16), 1, 0)
    for latent in range(nf):
        for k in range(strips):
            pbuf[latent, pl.ds(k, 1), :] = partial_mod[latent : latent + 1, 128 * k : 128 * k + 128]
    pcopies = []
    for o, peer in zip(range(1, group), weight_peers(nf, nc)):
        copy = remote(pbuf.at[peer["fsdp"]], pland.at[slot], psend.at[o], precv.at[o], peer)
        copy.start()
        pcopies.append(copy)
    pland[slot] = pbuf[f]
    loads[2].wait()

    def norm_rows(k, carry):
        at = aligned(k * step, step)
        normed[at, :] = centred(tok[at, :].astype(F32))[0]
        return carry

    lax.fori_loop(0, rows // 2 // step, norm_rows, 0)
    joint_gather.relay_middle(0)
    lax.fori_loop(rows // 2 // step, rows // step, norm_rows, 0)
    joint_gather.relay_middle(1)
    for copy in pcopies:
        copy.wait_recv()
    total_mod = pland[0]
    for k in range(1, group):
        total_mod = total_mod + pland[k]
    mod[t] = total_mod + cbias[...]
    mcopies = []
    for o, peer in zip(range(1, 4), ring_peers("tp", 4)):
        copy = remote(mod.at[t], mod.at[t], msend.at[o], mrecv.at[o], peer)
        copy.start()
        mcopies.append(copy)
    joint_gather.relay_rest(0)
    for copy in loads[3:]:
        copy.wait()
    obuf[slot] = oweight[...].astype(BF16)
    ebuf[slot] = eweight[...].astype(BF16)
    sbuf[slot] = sweight[...].astype(BF16)
    for copy in mcopies:
        copy.wait_recv()
    shift = row_of(mod, 0, width, part)
    scale = row_of(mod, width, width, part)

    def hide_rows(k, carry):
        at = aligned(k * step, step)
        hidden[at, :] = (normed[at, :] * (1.0 + scale) + shift).astype(BF16)
        return carry

    lax.fori_loop(0, rows // step, hide_rows, 0)
    joint_gather.relay_rest(1)
    output_gather.start()
    joint_gather.arrive()
    deep = jweight.shape[0]
    for k in range(group):
        weight_t[:, k * deep : (k + 1) * deep] = transposed(wbuf[k])

    total = rows * nc
    bq, bk = scores.shape[1], 512
    per = rows // bq

    def query_copy(o):
        dst = lax.rem(c + o, nc)
        return remote(
            joint.at[aligned(dst * 3 * hd, hd), :], qkv.at[pl.ds(0, hd), aligned(c * rows, rows)],
            send.at[1, o], recv.at[1, o], {"ctx": dst},
        )

    copies = []
    for o in (2, 1, 3, 0):
        dst = lax.rem(c + o, nc)
        where = aligned(dst * 3 * hd, 3 * hd)
        head = (dot(weight_t[where, :], hidden[...], 1, 1) + offset[where, :]).astype(BF16)
        if o == 0:
            qkv[:, aligned(c * rows, rows)] = head
        else:
            joint[where, :] = head
            copy = remote(
                joint.at[pl.ds(pl.multiple_of(dst * 3 * hd + hd, hd), 2 * hd), :],
                qkv.at[pl.ds(hd, 2 * hd), aligned(c * rows, rows)],
                send.at[0, o], recv.at[0, o], {"ctx": dst},
            )
            copy.start()
            copies.append(copy)
    for o in (2, 1, 3):
        query_copy(o).start()
    saves = [
        pltpu.make_async_copy(source, target, ssem.at[k])
        for k, (source, target) in enumerate(
            (
                (hidden, hidden_hbm), (weight_t, weight_hbm), (out_t, out_t_hbm), (qkv, qkv_hbm),
                (out, out_hbm), (land, land_hbm), (ebuf, ebuf_hbm), (sbuf, sbuf_hbm),
                (hidden_two, hidden_two_hbm),
            )
        )
    ]
    saves[0].start()
    saves[1].start()
    output_gather.relay()
    output_gather.arrive()
    oall[mine] = obuf[...].reshape(width, nc * hd)
    weights_share = Share(oall, asend, arecv)
    weights_share.start()
    for copy in copies:
        copy.wait_recv()
    expand_gather.start()
    for at in range(0, total, 1024):
        keys[at : at + 1024, :] = transposed(qkv[hd : 2 * hd, at : at + 1024])

    def given(o, k):
        owner, tt = lax.rem(c - o + nc, nc), lax.rem(t + k, 4)
        return remote(
            stage.at[owner, :, aligned(tt * own, own)], land.at[t, c],
            osend.at[o, k], orecv.at[o, k], {"ctx": owner, "tp": tt},
        )

    def block(i, carry):
        turn, sub = i // per, lax.rem(i, per)
        o = jnp.where(turn > 0, 1 + lax.rem(turn, 3), 0)
        owner = lax.rem(c - o + nc, nc)

        @pl.when(jnp.logical_and(sub == 0, turn > 0))
        def _():
            query_copy(o).wait_recv()

        @pl.when(i == 2 * per)
        def _():
            expand_gather.relay_middle(0)
            expand_gather.relay_middle(1)

        @pl.when(i == 3 * per)
        def _():
            expand_gather.relay_rest(0)
            expand_gather.relay_rest(1)
            shrink_gather.start()
            saves[3].start()

        where = aligned(owner * rows + sub * bq, bq)
        query = qkv[0:hd, where] * BF16(hd**-0.5)
        peak = None
        for at in range(0, total, bk):
            s = dot(keys[at : at + bk, :], query, 1, 0)
            scores[at : at + bk, :] = s
            high = jnp.max(s.reshape(bk // 8, 8, bq), axis=0)
            peak = high if peak is None else jnp.maximum(peak, high)
        peak = jnp.max(peak, axis=0, keepdims=True)
        acc, mass = None, None
        for at in range(0, total, bk):
            p = jnp.exp(scores[at : at + bk, :] - peak)
            low = jnp.sum(p.reshape(bk // 8, 8, bq), axis=0)
            mass = low if mass is None else mass + low
            term = dot(qkv[2 * hd : 3 * hd, at : at + bk], p.astype(BF16), 1, 0)
            acc = term if acc is None else acc + term
        mass = jnp.sum(mass, axis=0, keepdims=True)
        acc = acc * (1.0 / mass)
        out[:, where] = acc
        lse[:, where] = peak + jnp.log(mass)
        stage[owner, :, aligned(sub * bq, bq)] = acc.astype(BF16)

        @pl.when(sub == per - 1)
        def _():
            pl.when(turn > 0)(given(o, 0).start)
            for k in range(1, 4):
                given(o, k).start()

        @pl.when(i == per - 1)
        def _():
            weights_share.relay()

        @pl.when(i == 2 * per - 1)
        def _():
            weights_share.finish()
            for k in range(4):
                out_t[k] = transposed(oall[k])
            saves[2].start()

        return carry

    lax.fori_loop(0, per * nc, block, 0)
    land[t, c] = stage[c, :, aligned(t * own, own)]
    saves[4].start()
    expand_gather.arrive()
    saves[6].start()
    shrink_gather.relay_middle(0)

    order = [(o, k) for o in (0, 2, 3, 1) for k in range(4) if o or k]
    for o, k in order:
        given(o, k).wait_recv()
    held = bias[0:1, :]
    for k in range(4):
        block_ = land[k].reshape(nc * hd, own)
        held = held + dot(block_.astype(F32).T.astype(BF16), out_t[k], 1, 0)
    value[...] = held
    gate = row_of(mod, 2 * width, width, part)
    shift = row_of(mod, 3 * width, width, part)
    scale = row_of(mod, 4 * width, width, part)
    mid = tok[aligned(mine * own, own), :].astype(F32) + gate * held
    middle[...] = mid
    hidden_two[mine] = (centred(mid)[0] * (1.0 + scale) + shift).astype(BF16)
    sharing = Share(hidden_two, hsend, hrecv)
    sharing.start()
    saves[5].start()
    shrink_gather.relay_rest(0)
    for o, k in order:
        given(o, k).wait_send()
    for o in (2, 1, 3):
        query_copy(o).wait_send()
    for copy in pcopies + mcopies + copies:
        copy.wait_send()
    shrink_gather.arrive()
    saves[7].start()
    sharing.relay()
    sharing.finish()
    saves[8].start()
    for copy in saves:
        copy.wait()
    for gather in (joint_gather, output_gather, expand_gather, shrink_gather):
        gather.drain()


def forward(nf, nc, part, tok, jweight, cond, modw, cbias, offset, oweight, eweight, bias, sweight):
    rows, width = tok.shape
    deep, columns = jweight.shape
    group = nf * nc
    own = rows // 4
    total = rows * nc
    hd = HEAD_DIM
    bq = min(512, rows)
    return call(
        partial(forward_body, nf, nc, part),
        "forward",
        (
            shape((rows, width), BF16),
            shape((columns, width), BF16),
            shape((4,) + cbias.shape, F32),
            shape((4, nc * hd, width), BF16),
            shape((3 * hd, total), BF16),
            shape((hd, total), F32),
            shape((1, total), F32),
            shape((4, nc, hd, own), BF16),
            shape((group,) + eweight.shape, BF16),
            shape((own, width), F32),
            shape((own, width), F32),
            shape((4, own, width), BF16),
            shape((group, deep, sweight.shape[1] // 2), BF16),
        ),
        [
            pltpu.VMEM((deep, sweight.shape[1] // 2), F32),
            pltpu.VMEM((group, deep, sweight.shape[1] // 2), BF16),
            pltpu.VMEM(tok.shape, BF16),
            pltpu.VMEM(jweight.shape, F32),
            pltpu.VMEM(modw.shape, F32),
            pltpu.VMEM(oweight.shape, F32),
            pltpu.VMEM(eweight.shape, F32),
            pltpu.VMEM((4, nc * hd, width), BF16),
            pltpu.VMEM((3 * hd, total), BF16),
            pltpu.VMEM((hd, total), F32),
            pltpu.VMEM((group,) + eweight.shape, BF16),
            pltpu.VMEM((4, own, width), BF16),
            pltpu.VMEM((rows, width), BF16),
            pltpu.VMEM((columns, width), BF16),
            pltpu.VMEM((group, deep, columns), BF16),
            pltpu.VMEM((group,) + oweight.shape, BF16),
            pltpu.VMEM((4, width, nc * hd), BF16),
            pltpu.VMEM((nf,) + cbias.shape, F32),
            pltpu.VMEM((group,) + cbias.shape, F32),
            pltpu.VMEM((rows, width), F32),
            pltpu.VMEM((columns, rows), BF16),
            pltpu.VMEM((nc, hd, rows), BF16),
            pltpu.VMEM((4, nc, hd, own), BF16),
            pltpu.VMEM((total, hd), BF16),
            pltpu.VMEM((total, bq), F32),
            DMA((6,)), DMA((9,)),
            DMA((group,)), DMA((group,)), DMA((4,)), DMA((4,)),
            DMA((2, nc)), DMA((2, nc)), DMA((nc, 4)), DMA((nc, 4)), DMA((3,)), DMA((3,)),
        ]
        + share_sems()
        + gather_sems(nf, nc, 6),
        1,
        150,
        60,
        ins=(0, 1, 3, 6, 7, 9),
        to=(0, 1, 3, 4, 5, 7, 8, 11, 12),
    )(tok, jweight, cond, modw, cbias, offset, oweight, eweight, bias, sweight)


def branch_body(
    nf, nc, part, hidden_hbm, cot_hbm, expand_hbm, sw_hbm, sbuf_hbm, hbias, mod, middle, value,
    attn_own, mid_grad, shrink_half, shrink_rest, expand_grad, stats, hstats, sh_cross, sh_own,
    cot, hidden, expand, sweight, sgat, gbuf, abuf, ebuf, slopes, held_buf,
    shrink_grad, shrink_parts, sland, dland, sbuf, rbuf, shold,
    lsem, tsend, trecv, send, recv, s1s, s1r, s2s, s2r, d1s, d1r, d2s, d2r, *gsems,
):
    mine, partner, cross, far = tp_places()
    own, width = middle.shape
    group = nf * nc
    deep, units = sweight.shape
    slot = lax.axis_index("fsdp") * nc + lax.axis_index("ctx")
    gate_first = row_of(mod, 2 * width, width, part)
    scale_second = row_of(mod, 4 * width, width, part)
    gate_second = row_of(mod, 5 * width, width, part)
    split = units // 2
    loads = load_all(
        (
            (sw_hbm, sweight), (hidden_hbm, hidden), (expand_hbm, expand), (cot_hbm, cot),
            (sbuf_hbm, sgat.at[:, :, pl.ds(0, split)]),
        ),
        lsem,
    )
    loads[0].wait()
    sgat[slot, :, split:units] = sweight[:, split:units].astype(BF16)
    greet(ring_peers("tp", 4) + weight_peers(nf, nc))
    gather = Gather(sgat, nf, nc, gsems, 2, 1)
    gather.start()
    for copy in loads[1:]:
        copy.wait()
    tile = 32

    def ahead(turn, carry):
        at = turned(mine, turn)

        @pl.when(turn == 2)
        def _():
            gather.relay_middle(1)


        where = aligned(at * own, own)
        weight = expand[...].reshape(width, units)
        slopes[where, :] = dot(hidden[at], weight, 1, 0) + hbias[...]

        def curve(k, carry_):
            row = pl.ds(pl.multiple_of(at * own + k * tile, tile), tile)
            u = slopes[row, :]
            squared = u * u
            th = jnp.tanh(GELU_SCALE * (u + GELU_CUBE * squared * u))
            abuf[row, :] = (0.5 * u * (1.0 + th)).astype(BF16)
            slopes[row, :] = 0.5 * (1.0 + th) + 0.5 * u * (1.0 - th * th) * (
                GELU_SCALE * (1.0 + 3.0 * GELU_CUBE * squared)
            )
            gbuf[row, :] = (gate_second * cot[row, :].astype(F32)).astype(BF16)
            return carry_

        lax.fori_loop(0, own // tile, curve, 0)
        return carry

    lax.fori_loop(0, 4, ahead, 0)
    gather.relay_rest(1)
    step = 256
    for at in range(0, width, step):
        block = dot(gbuf[:, at : at + step], abuf[...], 0, 0).astype(BF16)
        for k in range(at // deep, (at + step) // deep):
            shrink_grad[k // nc, k % nc] = block[k * deep - at : (k + 1) * deep - at, :]
    early = Scatter(
        nf, nc, shrink_grad, shrink_parts, sland, dland, s1s, s1r, d1s, d1r, (0, split)
    )
    late = Scatter(
        nf, nc, shrink_grad, shrink_parts, sland, dland, s2s, s2r, d2s, d2r, (split, split)
    )
    early.swap()
    late.swap()
    gather.arrive()
    hstats[...] = jnp.zeros_like(hstats)
    summing = Sum(sbuf, rbuf, send, recv)

    def back_turn(turn, carry):
        at = turned(mine, 3 - turn)
        where = aligned(at * own, own)
        weight = sgat[...].reshape(width, units)
        pull = dot(gbuf[where, :], weight, 1, 0) * slopes[where, :]
        hstats[...] += jnp.sum(pull, axis=0, keepdims=True)
        pull = pull.astype(BF16)
        ebuf[where, :] = pull
        held_buf[...] = dot(pull, expand[...].reshape(width, units), 1, 1)

        @pl.when(turn == 0)
        def _():
            summing.give(0, held_buf[...])

        @pl.when(turn == 1)
        def _():
            summing.pass_on(held_buf[...])

        @pl.when(turn == 2)
        def _():
            summing.give(1, held_buf[...])

        return carry

    lax.fori_loop(0, 4, back_turn, 0)
    copies = []
    for turn, at in enumerate((far, partner)):
        weight = sgat[...].reshape(width, units)
        shold[turn] = dot(abuf[aligned(at * own, own), :], weight, 1, 1).astype(BF16)
        copy = remote(
            shold.at[turn], shold.at[2 + turn], tsend.at[turn], trecv.at[turn], {"tp": partner}
        )
        copy.start()
        copies.append(copy)
    flat = hidden.shape[0] * own
    for at in range(0, width, step):
        expand_grad[at : at + step, :] = dot(
            hidden[:, :, at : at + step].reshape(flat, step), ebuf[...], 0, 0
        ).astype(BF16)
    early.swapped()
    early.deal()
    weight = sgat[...].reshape(width, units)
    forth = dot(abuf[aligned(cross * own, own), :], weight, 1, 1)
    copies[0].wait_recv()
    sh_cross[...] = (forth + shold[2].astype(F32)).astype(BF16)
    forth = dot(abuf[aligned(mine * own, own), :], weight, 1, 1)
    copies[1].wait_recv()
    sh_own[...] = forth + shold[3].astype(F32)
    mine_rows = cot[aligned(mine * own, own), :].astype(F32)
    stats[3:4, :] = jnp.sum(gate_second * mine_rows, axis=0, keepdims=True)
    normed, inverse = centred(middle[...])
    grad_in = summing.total(summing.near(held_buf[...]))
    stats[0:1, :] = jnp.sum(grad_in, axis=0, keepdims=True)
    stats[1:2, :] = jnp.sum(grad_in * normed, axis=0, keepdims=True)
    mgrad = mine_rows + normal_back(grad_in * (1.0 + scale_second), normed, inverse)
    mid_grad[...] = mgrad
    agrad = gate_first * mgrad
    attn_own[...] = agrad.astype(BF16)
    stats[2:3, :] = jnp.sum(mgrad * value[...], axis=0, keepdims=True)
    stats[4:5, :] = jnp.sum(agrad, axis=0, keepdims=True)
    stats[5:8, :] = jnp.zeros((3, width), F32)
    late.swapped()
    shrink_rest[...] = shrink_parts[:, :, split:units]
    shrink_half[...] = early.dealt()
    early.drain()
    late.drain(deals=False)
    summing.drain()
    gather.drain()
    for copy in copies:
        copy.wait_send()


def branch(nf, nc, part, hidden, cot, expand, sweight, sbuf, hbias, mod, middle, value):
    rows, width = cot.shape
    own = rows // 4
    deep, units = sweight.shape
    group = nf * nc
    return call(
        partial(branch_body, nf, nc, part),
        "branch",
        (
            shape((own, width), BF16),
            shape((own, width), F32),
            shape((deep, units // 2), F32),
            shape((nc, deep, units // 2), BF16),
            shape((width, units), BF16),
            shape((8, width), F32),
            shape((1, units), F32),
            shape((own, width), BF16),
            shape((own, width), F32),
        ),
        [
            pltpu.VMEM((rows, width), BF16),
            pltpu.VMEM((4, own, width), BF16),
            pltpu.VMEM((group, deep, units), BF16),
            pltpu.VMEM((deep, units), F32),
            pltpu.VMEM((group, deep, units), BF16),
            pltpu.VMEM((rows, width), BF16),
            pltpu.VMEM((rows, units), BF16),
            pltpu.VMEM((rows, units), BF16),
            pltpu.VMEM((rows, units), F32),
            pltpu.VMEM((own, width), F32),
            pltpu.VMEM((nf, nc, deep, units), BF16),
            pltpu.VMEM((nc, deep, units), BF16),
            pltpu.VMEM((nf - 1, nc, deep, units), BF16),
            pltpu.VMEM((nc - 1, deep, units), BF16),
            pltpu.VMEM((3, own, width), BF16),
            pltpu.VMEM((3, own, width), BF16),
            pltpu.VMEM((4, own, width), BF16),
            DMA((5,)), DMA((2,)), DMA((2,)),
        ]
        + share_sems()
        + [DMA((nf,))] * 4
        + [DMA((nc,))] * 4
        + gather_sems(nf, nc, 1),
        2,
        40,
        60,
        ins=(0, 1, 2, 3, 4),
    )(hidden, cot, expand, sweight, sbuf, hbias, mod, middle, value)


def backward_body(
    nf, nc, part, attn_own, out_t_hbm, heads_hbm, qkv_hbm, out_hbm, lse, sh_cross, sh_own, middle,
    cot_hbm, mod, bias, shrink_half, shrink_parts, expand_grad, weight_hbm, hidden_hbm, tok_hbm,
    mid_grad, stats_second, hidden_stats, modw_hbm, low,
    mixed, tokens_grad, shrink_sum, expand_sum, output_sum, joint_sum, modulate_sum,
    bias_rows, done,
    out_t, qkv, out, heads, att, cot_own, tok_own, weight_t, hidden, modw,
    attn_low, dout, dost, keys, vals, dq, stage, rland, delta, output_grad, eland, oland,
    expand_parts, output_parts, sdeal, edeal, odeal, joint_grad, sbuf, rbuf,
    kvgrad, kvland, kvparts, kvdeal, qgrad, qland, qparts, qdeal, pieces, land, total_piece, gathered, ftotal, gate_row,
    lsem, send, recv, jsend, jrecv, csend, crecv, gsend, grecv, tsend, trecv, hsend, hrecv,
    lowsend, lowrecv, hsend2, hrecv2, x1s, x1r, x2s, x2r, x3s, x3r, x4s, x4r, x5s, x5r,
    d1s, d1r, d2s, d2r, d3s, d3r, d4s, d4r, d5s, d5r, d6s, d6r, asend, arecv, bsend, brecv, f1s, f1r,
):
    f, c, t = lax.axis_index("fsdp"), lax.axis_index("ctx"), lax.axis_index("tp")
    mine, partner, cross, far = tp_places()
    own, width = middle.shape
    rows = 4 * own
    total = rows * nc
    hd = HEAD_DIM
    inner, group = nc * 4, nf * nc
    here, slot = c * 4 + t, f * nc + c
    bk = bq = 512
    per = rows // bk
    deep = joint_sum.shape[0]
    heads_wide = nc * hd
    units = expand_grad.shape[3]
    half = units // 2
    shrink = Scatter(nf, nc, None, shrink_parts, eland, sdeal, None, None, d1s, d1r)
    early = Scatter(
        nf, nc, expand_grad, expand_parts, eland, edeal, x1s, x1r, d2s, d2r, (0, half)
    )
    late = Scatter(
        nf, nc, expand_grad, expand_parts, eland, edeal, x2s, x2r, d3s, d3r, (half, half)
    )
    project = Scatter(nf, nc, output_grad, output_parts, oland, odeal, x3s, x3r, d4s, d4r)
    kv = Scatter(nf, nc, kvgrad, kvparts, kvland, kvdeal, x4s, x4r, d5s, d5r)
    query = Scatter(nf, nc, qgrad, qparts, qland, qdeal, x5s, x5r, d6s, d6r)
    own_rows = aligned(mine * own, own)
    loads = load_all(
        (
            (out_t_hbm, out_t), (qkv_hbm, qkv), (out_hbm, out), (heads_hbm, heads),
            (cot_hbm.at[own_rows, :], cot_own), (tok_hbm.at[own_rows, :], tok_own),
            (weight_hbm, weight_t), (hidden_hbm, hidden), (modw_hbm, modw),
        ),
        lsem,
    )
    attn_low[mine] = attn_own[...]
    loads[0].wait()
    for k in range(4):
        dost[k] = dot(out_t[k], attn_own[...], 1, 1).astype(BF16).reshape(nc, hd, own)
    greet(all_peers(nf, nc))
    where_own = aligned(c * rows + t * own, own)

    def send_out(o, k):
        cc, tt = lax.rem(c + o, nc), lax.rem(t + k, 4)
        return remote(
            dost.at[tt, cc], dout.at[:, where_own], send.at[o, k], recv.at[o, k],
            {"ctx": cc, "tp": tt},
        )

    order = [(o, k) for o in (2, 1, 3, 0) for k in range(4) if o or k]
    for o, k in order:
        send_out(o, k).start()
    low_share = Share(attn_low, lowsend, lowrecv)
    low_share.start()
    early.swap()
    late.swap()
    crossing = remote(sh_cross, rland, csend, crecv, {"tp": cross})
    crossing.start()
    shrink.deal()
    dout[:, where_own] = dost[t, c]
    for copy in loads[1:4]:
        copy.wait()
    for at in range(0, total, 1024):
        keys[at : at + 1024, :] = transposed(qkv[hd : 2 * hd, at : at + 1024])
        vals[at : at + 1024, :] = transposed(qkv[2 * hd : 3 * hd, at : at + 1024])
    dq[...] = jnp.zeros_like(dq)
    for o, k in order:
        send_out(o, k).wait_recv()
    for at in range(0, total, 1024):
        delta[:, at : at + 1024] = jnp.sum(
            dout[:, at : at + 1024].astype(F32) * out[:, at : at + 1024], axis=0, keepdims=True
        )
    sharing = Share(mixed, gsend, grecv)
    exchange = [
        remote(heads.at[peer["tp"]], att.at[:, :, own_rows], hsend2.at[k], hrecv2.at[k], peer)
        for k, peer in zip(range(1, 4), ring_peers("tp", 4))
    ]

    def kv_back(o, owner):
        return remote(
            stage.at[owner, pl.ds(hd, 2 * hd), :], joint_grad.at[c, pl.ds(hd, 2 * hd), :],
            jsend.at[0, o], jrecv.at[0, o], {"ctx": owner},
        )

    def q_back(o, owner):
        return remote(
            stage.at[owner, pl.ds(0, hd), :], joint_grad.at[c, pl.ds(0, hd), :],
            jsend.at[1, o], jrecv.at[1, o], {"ctx": owner},
        )

    def block(i, vsum):
        o = 1 + i // per
        owner = lax.rem(c + o, nc)
        sub = lax.rem(i, per)
        where = aligned(owner * rows + sub * bk, bk)
        key, val, key_t = keys[where, :], vals[where, :], qkv[hd : 2 * hd, where]
        dk, dv = None, None
        for at in range(0, total, bq):
            query = qkv[0:hd, at : at + bq] * BF16(hd**-0.5)
            grad = dout[:, at : at + bq]
            p = jnp.exp(dot(key, query, 1, 0) - lse[:, at : at + bq])
            ds = (p * (dot(val, grad, 1, 0) - delta[:, at : at + bq])).astype(BF16)
            tv = dot(grad, p.astype(BF16), 1, 1)
            tk = dot(query, ds, 1, 1)
            dv = tv if dv is None else dv + tv
            dk = tk if dk is None else dk + tk
            dq[:, at : at + bq] += dot(key_t, ds, 1, 0)
        put = aligned(sub * bk, bk)
        stage[owner, hd : 2 * hd, put] = dk.astype(BF16)
        stage[owner, 2 * hd : 3 * hd, put] = dv.astype(BF16)

        @pl.when(jnp.logical_and(sub == per - 1, o < nc))
        def _():
            kv_back(o, owner).start()

        @pl.when(i == 1)
        def _():
            low_share.relay()
            att[:, :, own_rows] = heads[t]
            for copy in exchange:
                copy.start()

        @pl.when(i == 3)
        def _():
            for k in (1, 2):
                low_share.copy(k).wait_recv()
            for copy in exchange:
                copy.wait_recv()
            flat = dot(
                att[...].reshape(heads_wide, rows), attn_low[...].reshape(rows, width), 1, 0
            ).T.astype(BF16)
            output_grad[...] = flat.reshape(output_grad.shape)
            project.swap()

        @pl.when(i == 2)
        def _():
            crossing.wait_recv()
            loads[4].wait()
            value = sh_own[...] + rland[...].astype(F32) + bias[1:2, :]
            gate = row_of(mod, 5 * width, width, part)
            mixed[mine] = (middle[...] + gate * value).astype(BF16)
            sharing.start()
            gate_row[...] = jnp.sum(
                cot_own[...].astype(F32) * value, axis=0, keepdims=True
            )

        @pl.when(i == 2)
        def _():
            early.swapped()
            early.deal()

        @pl.when(i == 4)
        def _():
            late.swapped()

        @pl.when(i == 6)
        def _():
            project.swapped()
            sharing.relay()

        return vsum + jnp.sum(dv, axis=1, keepdims=True)

    vsum = lax.fori_loop(0, per * nc, block, jnp.zeros((hd, 1), F32))
    qsum = jnp.zeros((hd, 1), F32)
    for o in (2, 1, 3, 0):
        owner = lax.rem(c + o, nc)
        piece = dq[:, aligned(owner * rows, rows)] * (hd**-0.5)
        qsum = qsum + jnp.sum(piece, axis=1, keepdims=True)
        stage[owner, 0:hd, :] = piece.astype(BF16)
        if o > 0:
            q_back(o, owner).start()
    late.deal()
    project.deal()
    joint_grad[c] = stage[c]
    bias_column = jnp.concatenate([qsum, vsum], axis=0)
    for copy in loads[5:]:
        copy.wait()
    rows_f = width // nf

    def weight_grad(scatter, source, into):
        flat_grad = source.reshape(-1, rows)

        def put(lanes, member, first, count):
            block_ = dot(flat_grad, hidden[:, lanes], 1, 0).T.astype(BF16)
            for k in range(count):
                row = (member, first + k) if member is not None else divmod(first + k, nc)
                into[row[0], row[1]] = block_[k * deep : (k + 1) * deep, :]

        if rows_f % 128:
            for at in range(0, width, 256):
                put(pl.ds(at, 256), None, at // deep, 256 // deep)
            scatter.swap()
            return
        wide_step = min(256, rows_f)
        for o in range(1, nf + 1):
            member = lax.rem(f + o, nf)
            for at in range(0, rows_f, wide_step):
                put(
                    aligned(member * rows_f + at, wide_step), member, at // deep, wide_step // deep
                )
            if o < nf:
                scatter.swaps[o - 1].start()

    for o in range(1, nc):
        kv_back(o, lax.rem(c + o, nc)).wait_recv()
    weight_grad(kv, joint_grad[:, hd : 3 * hd, :], kvgrad)
    shrink_total = shrink.dealt()
    shrink_sum[:, 0:half] = shrink_half[...]
    shrink_sum[:, half:units] = shrink_total
    squares = jnp.sum(shrink_total * shrink_total) + jnp.sum(shrink_half[...] * shrink_half[...])
    for o in range(1, nc):
        q_back(o, lax.rem(c + o, nc)).wait_recv()

    columns = weight_t.shape[0]

    def piece_of(at):
        block_ = joint_grad[:, :, aligned(at * own, own)].reshape(columns, own)
        return dot(block_.astype(F32).T.astype(BF16), weight_t[...], 1, 0)

    summing = Sum(sbuf, rbuf, tsend, trecv)
    summing.give(0, piece_of(far))
    summing.give(1, piece_of(partner))
    summing.pass_on(piece_of(cross))
    weight_grad(query, joint_grad[:, 0:hd, :], qgrad)
    held = summing.near(piece_of(mine))
    kv.swapped()
    kv.deal()
    normed, inverse = centred(tok_own[...].astype(F32))
    grad_in = summing.total(held)
    scale = row_of(mod, width, width, part)
    shift_row = jnp.sum(grad_in, axis=0, keepdims=True)
    scale_row = jnp.sum(grad_in * normed, axis=0, keepdims=True)

    slim = part // nc // 128
    share = 2 * width // nc // 128
    hshare = hidden_stats.shape[1] // nc // 128
    last = slim + share + hshare
    vectors = [
        shift_row, scale_row, stats_second[2:3, :],
        stats_second[0:1, :], stats_second[1:2, :], gate_row[...],
    ]
    residual = [stats_second[4:5, :], stats_second[3:4, :]]
    pieces[...] = jnp.zeros_like(pieces)
    for cc in range(nc):
        for tt in range(4):
            k = cc * 4 + tt
            for n in range(slim):
                at = ((tt * part // 128) + cc * slim + n) * 128
                pieces[k, n : n + 1, :] = vectors[at // width][:, at % width : at % width + 128]
            for n in range(share):
                at = (cc * share + n) * 128
                pieces[k, slim + n : slim + n + 1, :] = residual[at // width][
                    :, at % width : at % width + 128
                ]
        for n in range(hshare):
            at = (cc * hshare + n) * 128
            pieces[cc * 4 + t, slim + share + n : slim + share + n + 1, :] = hidden_stats[
                :, at : at + 128
            ]
    pieces[here, last : last + 1, :] = jnp.broadcast_to(bias_column, (2 * hd, 128)).T[0:1, :]
    first = []
    for o in range(1, inner):
        other = lax.rem(here + o, inner)
        copy = remote(
            pieces.at[other], land.at[here], asend.at[o], arecv.at[o],
            {"ctx": other // 4, "tp": lax.rem(other, 4)},
        )
        copy.start()
        first.append(copy)
    tokens_grad[mine] = (
        mid_grad[...] + normal_back(grad_in * (1.0 + scale), normed, inverse)
    ).astype(BF16)
    token_share = Share(tokens_grad, hsend, hrecv)
    token_share.start()
    query.swapped()
    query.deal()
    land[here] = pieces[here]
    for copy in first:
        copy.wait_recv()
    acc = land[0]
    for k in range(1, inner):
        acc = acc + land[k]
    total_piece[...] = acc
    gathered[slot] = acc
    second = []
    for o, peer in zip(range(1, group), weight_peers(nf, nc)):
        copy = remote(total_piece, gathered.at[slot], bsend.at[o], brecv.at[o], peer)
        copy.start()
        second.append(copy)
    expand_total = early.dealt()
    expand_sum[:, 0:half] = expand_total
    squares = squares + jnp.sum(expand_total * expand_total)
    expand_total = late.dealt()
    expand_sum[:, half:units] = expand_total
    squares = squares + jnp.sum(expand_total * expand_total)
    output_total = project.dealt()
    output_sum[...] = output_total
    squares = squares + jnp.sum(output_total * output_total)
    for copy in second:
        copy.wait_recv()

    grads = []
    for latent in range(nf):
        strips = []
        for cc in range(nc):
            for n in range(slim):
                strips.append(gathered[latent * nc + cc, n : n + 1, :])
        grads.append(jnp.concatenate(strips, axis=1))
    condition_bias = grads[0]
    for latent in range(1, nf):
        condition_bias = condition_bias + grads[latent]
    bias_rows[...] = jnp.zeros_like(bias_rows)
    bias_rows[0:1, 0:part] = condition_bias
    factors = low[...].T
    wide = modw[...].astype(BF16).astype(F32)
    outer = None
    ftotal[...] = jnp.zeros_like(ftotal)
    for latent in range(nf):
        term = factors[:, latent : latent + 1] * grads[latent]
        outer = term if outer is None else outer + term
        column = jnp.sum(wide * grads[latent], axis=1, keepdims=True)
        ftotal[latent : latent + 1, 0:deep] = jnp.broadcast_to(column, (deep, 128)).T[0:1, :]
    modulate_sum[...] = outer
    squares = squares + jnp.sum(outer * outer)

    def over(at, count):
        found = []
        for cc in range(nc):
            value = None
            for latent in range(nf):
                block_ = gathered[latent * nc + cc, at : at + count, :]
                value = block_ if value is None else value + block_
            for n in range(count):
                found.append(value[n : n + 1, :])
        return jnp.concatenate(found, axis=1)

    residual_sum = over(slim, share)
    hidden_sum = over(slim + share, hshare)
    head_sum = over(last, 1)
    bias_rows[1:2, 0 : hidden_sum.shape[1]] = hidden_sum
    bias_rows[2:3, 0 : head_sum.shape[1]] = head_sum
    bias_rows[3:4, 0:width] = residual_sum[:, 0:width]
    bias_rows[4:5, 0:width] = residual_sum[:, width : 2 * width]
    lead = (slot == 0).astype(F32)
    tensor_lead = (t == 0).astype(F32)
    squares = squares + lead * (
        jnp.sum(condition_bias * condition_bias)
        + jnp.sum(hidden_sum * hidden_sum)
        + jnp.sum(head_sum * head_sum)
        + tensor_lead * jnp.sum(residual_sum * residual_sum)
    )
    token_share.relay()
    kv_total, q_total = kv.dealt(), query.dealt()
    squares = squares + jnp.sum(kv_total * kv_total) + jnp.sum(q_total * q_total)
    ftotal[nf : nf + 1, :] = jnp.full((1, 128), squares)
    third = []
    for o, peer in zip(range(1, group * 4), all_peers(nf, nc)):
        copy = remote(ftotal, done.at[slot, t], f1s.at[o], f1r.at[o], peer)
        copy.start()
        third.append(copy)
    done[slot, t] = ftotal[...]
    kv_total, q_total = kv_total.T, q_total.T
    blocks = []
    for k in range(nc):
        blocks += [q_total[k * hd : (k + 1) * hd], kv_total[k * 2 * hd : (k + 1) * 2 * hd]]
    joint_sum[...] = jnp.concatenate(blocks, axis=0).T
    sharing.finish()
    token_share.finish()
    summing.drain()
    for o in range(1, nc):
        owner = lax.rem(c + o, nc)
        kv_back(o, owner).wait_send()
        q_back(o, owner).wait_send()
    for o, k in order:
        send_out(o, k).wait_send()
    for k in range(3):
        low_share.copy(k).wait_send()
    for copy in exchange:
        copy.wait_send()
    crossing.wait_send()
    shrink.drain(swaps=False)
    for scatter in (early, late, project, kv, query):
        scatter.drain()
    for copy in third:
        copy.wait_recv()
    for copy in first + second + third:
        copy.wait_send()


def backward(
    nf, nc, part, attn_own, out_t, att, qkv, out, lse, sh_cross, sh_own, middle, cot, mod, bias,
    shrink_half, shrink_parts, expand_grad, weight_t, hidden, tok, mid_grad, stats_second, hidden_stats,
    modw, low,
):
    rows, width = cot.shape
    own = rows // 4
    total = rows * nc
    hd = HEAD_DIM
    inner, group = nc * 4, nf * nc
    deep = width // group
    units = expand_grad.shape[1]
    columns = weight_t.shape[0]
    heads_wide = nc * hd
    expand_grad = expand_grad.reshape(nf, nc, deep, units)
    high = -(-(part // nc + 2 * width // nc + hidden_stats.shape[1] // nc + 128) // 1024) * 8
    tall = -(-(nf + 1) // 8) * 8
    return call(
        partial(backward_body, nf, nc, part),
        "backward",
        (
            shape((4, own, width), BF16),
            shape((4, own, width), BF16),
            shape((deep, units), F32),
            shape((deep, units), F32),
            shape((deep, heads_wide), F32),
            shape((deep, columns), F32),
            shape((deep, part), F32),
            shape((8, max(part, width, hidden_stats.shape[1])), F32),
            shape((group, 4, tall, 128), F32),
        ),
        [
            pltpu.VMEM(out_t.shape, BF16),
            pltpu.VMEM(qkv.shape, BF16),
            pltpu.VMEM(out.shape, F32),
            pltpu.VMEM(att.shape, BF16),
            pltpu.VMEM((nc, hd, rows), BF16),
            pltpu.VMEM((own, width), BF16),
            pltpu.VMEM((own, width), BF16),
            pltpu.VMEM(weight_t.shape, BF16),
            pltpu.VMEM(hidden.shape, BF16),
            pltpu.VMEM(modw.shape, F32),
            pltpu.VMEM((4, own, width), BF16),
            pltpu.VMEM((hd, total), BF16),
            pltpu.VMEM((4, nc, hd, own), BF16),
            pltpu.VMEM((total, hd), BF16),
            pltpu.VMEM((total, hd), BF16),
            pltpu.VMEM((hd, total), F32),
            pltpu.VMEM((nc, 3 * hd, rows), BF16),
            pltpu.VMEM((own, width), BF16),
            pltpu.VMEM((1, total), F32),
            pltpu.VMEM((nf, nc, deep, heads_wide), BF16),
            pltpu.VMEM((nf - 1, nc, deep, units), BF16),
            pltpu.VMEM((nf - 1, nc, deep, heads_wide), BF16),
            pltpu.VMEM((nc, deep, units), BF16),
            pltpu.VMEM((nc, deep, heads_wide), BF16),
            pltpu.VMEM((nc - 1, deep, units // 2), BF16),
            pltpu.VMEM((nc - 1, deep, units), BF16),
            pltpu.VMEM((nc - 1, deep, heads_wide), BF16),
            pltpu.VMEM((nc, 3 * hd, rows), BF16),
            pltpu.VMEM((3, own, width), BF16),
            pltpu.VMEM((3, own, width), BF16),
            pltpu.VMEM((nf, nc, deep, 2 * heads_wide), BF16),
            pltpu.VMEM((nf - 1, nc, deep, 2 * heads_wide), BF16),
            pltpu.VMEM((nc, deep, 2 * heads_wide), BF16),
            pltpu.VMEM((nc - 1, deep, 2 * heads_wide), BF16),
            pltpu.VMEM((nf, nc, deep, heads_wide), BF16),
            pltpu.VMEM((nf - 1, nc, deep, heads_wide), BF16),
            pltpu.VMEM((nc, deep, heads_wide), BF16),
            pltpu.VMEM((nc - 1, deep, heads_wide), BF16),
            pltpu.VMEM((inner, high, 128), F32),
            pltpu.VMEM((inner, high, 128), F32),
            pltpu.VMEM((high, 128), F32),
            pltpu.VMEM((group, high, 128), F32),
            pltpu.VMEM((tall, 128), F32),
            pltpu.VMEM((1, width), F32),
            DMA((9,)), DMA((nc, 4)), DMA((nc, 4)), DMA((2, nc)), DMA((2, nc)),
            DMA, DMA,
        ]
        + share_sems() * 4
        + [DMA((4,))] * 2
        + [DMA((nf,))] * 10
        + [DMA((nc,))] * 12
        + [DMA((inner,))] * 2
        + [DMA((group,))] * 2
        + [DMA((group * 4,))] * 2,
        3,
        150,
        60,
        ins=(1, 2, 3, 4, 9, 15, 16, 17, 21),
    )(
        attn_own, out_t, att, qkv, out, lse, sh_cross, sh_own, middle, cot, mod, bias,
        shrink_half, shrink_parts, expand_grad, weight_t, hidden, tok, mid_grad, stats_second,
        hidden_stats, modw, low,
    )


def update(master, first, root, gradient, clip, decay_rate):
    scaled = clip * gradient
    first_moment = first_decay * first + (1.0 - first_decay) * scaled
    second_moment = second_decay * root * root + (1.0 - second_decay) * scaled * scaled
    new_root = jnp.sqrt(second_moment)
    first_hat = first_moment * (1.0 / (1.0 - first_decay**ADAM_STEP))
    second_hat = second_moment * (1.0 / (1.0 - second_decay**ADAM_STEP))
    updated = master - learning_rate * (
        first_hat / (jnp.sqrt(second_hat) + adam_epsilon) + decay_rate * master
    )
    return updated, first_moment, new_root


def adam_body(count, nf, nc, done, condition, bias_rows, tokens_hbm, mixed_hbm, *refs):
    grads = refs[:count]
    masters = refs[count : 2 * count]
    moments = refs[2 * count : 3 * count]
    smalls = refs[3 * count : 3 * count + 8]
    outs = refs[3 * count + 8 :]
    news = outs[:count]
    averages = outs[count : 2 * count]
    small_outs = outs[2 * count : 2 * count + 8]
    condition_grad, norm, tokens_out, mixed_out = outs[2 * count + 8 : 2 * count + 12]
    scratch = outs[2 * count + 12 :]
    wbufs = scratch[:count]
    mbufs = scratch[count : 2 * count]
    gbufs = scratch[2 * count : 3 * count]
    tokens_low, mixed, wide, isem, osem, tsem = scratch[3 * count :]
    token_load = pltpu.make_async_copy(tokens_hbm, tokens_low, tsem.at[5])
    mixed_load = pltpu.make_async_copy(mixed_hbm, mixed, tsem.at[6])
    group = nf * nc
    f = lax.axis_index("fsdp")
    loads, stores = [], []
    for k in range(count):
        loads.append(
            (
                pltpu.make_async_copy(masters[k], wbufs[k], isem.at[0, k]),
                pltpu.make_async_copy(moments[k], mbufs[k], isem.at[1, k]),
                pltpu.make_async_copy(grads[k], gbufs[k], isem.at[2, k]),
            )
        )
        stores.append(
            (
                pltpu.make_async_copy(wbufs[k], news[k], osem.at[0, k]),
                pltpu.make_async_copy(mbufs[k], averages[k], osem.at[1, k]),
            )
        )
    for copy in loads[0]:
        copy.start()
    token_load.start()
    mixed_load.start()
    for group_ in loads[1:]:
        for copy in group_:
            copy.start()
    token_load.wait()
    mixed_load.wait()
    mixed_copy = pltpu.make_async_copy(mixed, mixed_out, tsem.at[4])
    mixed_copy.start()
    token_copies = []
    for k in range(4):

        def widen(i, carry, k=k):
            at = pl.ds(pl.multiple_of(i * 16, 16), 16)
            wide[k, at, :] = tokens_low[k, at, :].astype(F32)
            return carry

        lax.fori_loop(0, wide.shape[1] // 16, widen, 0)
        copy = pltpu.make_async_copy(wide.at[k], tokens_out.at[k], tsem.at[k])
        copy.start()
        token_copies.append(copy)
    folded = [done[k, 0] + done[k, 1] + done[k, 2] + done[k, 3] for k in range(group)]
    squares = folded[0][nf : nf + 1, 0:1]
    for k in range(1, group):
        squares = squares + folded[k][nf : nf + 1, 0:1]
    grad_norm = jnp.sqrt(squares)
    norm[...] = grad_norm
    clip = jnp.minimum(1.0, clip_limit / (grad_norm + 1e-06))
    deep = condition.shape[1] // group
    found = []
    for k in range(group):
        row = done[k, 0, pl.ds(f, 1), 0:deep]
        for tt in range(1, 4):
            row = row + done[k, tt, pl.ds(f, 1), 0:deep]
        found.append(row)
    v = condition[pl.ds(f, 1), :]
    gate = 1.0 / (1.0 + jnp.exp(-v))
    condition_grad[...] = jnp.concatenate(found, axis=1) * (gate * (1.0 + v * (1.0 - gate)))
    for k in range(4):
        master, moment = smalls[2 * k], smalls[2 * k + 1]
        if k < 3:
            row = (2, 1, 0)[k]
            grad = bias_rows[row : row + 1, 0 : master.shape[1]]
            new, first, root = update(master[...], moment[0:1, :], moment[1:2, :], grad, clip, 0.0)
            small_outs[2 * k][...] = new
            small_outs[2 * k + 1][0:1, :] = first
            small_outs[2 * k + 1][1:2, :] = root
        else:
            grad = bias_rows[3:5, 0 : master.shape[1]]
            new, first, root = update(master[...], moment[0], moment[1], grad, clip, 0.0)
            small_outs[2 * k][...] = new
            small_outs[2 * k + 1][0] = first
            small_outs[2 * k + 1][1] = root
    for k in range(count):
        for copy in loads[k]:
            copy.wait()
        deep_k = wbufs[k].shape[0]
        step = min(16, deep_k)

        def rows(i, carry, k=k, step=step):
            at = pl.ds(pl.multiple_of(i * step, step), step)
            new, first, root = update(
                wbufs[k][at, :], mbufs[k][0, at, :], mbufs[k][1, at, :], gbufs[k][at, :],
                clip, weight_decay,
            )
            wbufs[k][at, :] = new
            mbufs[k][0, at, :] = first
            mbufs[k][1, at, :] = root
            return carry

        lax.fori_loop(0, deep_k // step, rows, 0)
        for copy in stores[k]:
            copy.start()
    for pair in stores:
        for copy in pair:
            copy.wait()
    for copy in token_copies + [mixed_copy]:
        copy.wait()


def adam(nf, nc, done, condition, bias_rows, tokens_low, mixed, grads, masters, moments, smalls):
    count = len(grads)
    anywhere = pl.BlockSpec(memory_space=pltpu.HBM)
    small_shapes = tuple(shape(a.shape, F32) for a in smalls)
    outs = (
        tuple(shape(m.shape, F32) for m in masters)
        + tuple(shape(m.shape, F32) for m in moments)
        + small_shapes
        + (shape((1, condition.shape[1]), F32), shape((1, 1), F32))
        + (shape(tokens_low.shape, F32), shape(mixed.shape, BF16))
    )
    return pl.pallas_call(
        partial(adam_body, count, nf, nc),
        out_shape=outs,
        in_specs=vmem(3) + [anywhere] * (2 + 3 * count) + vmem(8),
        out_specs=[anywhere] * (2 * count) + vmem(10) + [anywhere] * 2,
        scratch_shapes=[pltpu.VMEM(m.shape, F32) for m in masters]
        + [pltpu.VMEM(m.shape, F32) for m in moments]
        + [pltpu.VMEM(m.shape, F32) for m in masters]
        + [
            pltpu.VMEM(tokens_low.shape, BF16), pltpu.VMEM(mixed.shape, BF16),
            pltpu.VMEM(tokens_low.shape, F32),
        ]
        + [DMA((3, count)), DMA((2, count)), DMA((7,))],
        compiler_params=pltpu.CompilerParams(vmem_limit_bytes=63 << 20),
        cost_estimate=cost(10),
        name="adam",
    )(done, condition, bias_rows, tokens_low, mixed, *grads, *masters, *moments, *smalls)


def local(
    nf,
    nc,
    tokens,
    condition,
    cotangent,
    joint_weight,
    joint_moments,
    output_weight,
    output_moments,
    expand_weight,
    expand_moments,
    shrink_weight,
    shrink_moments,
    modulate_weight,
    modulate_moments,
    attention_bias,
    attention_moments,
    hidden_bias,
    hidden_moments,
    condition_bias,
    condition_moments,
    residual_bias,
    residual_moments,
):
    latent_count, rows, width = tokens.shape
    heads = joint_weight.shape[1] // (3 * HEAD_DIM)
    assert latent_count == 1 and heads == nc and lax.axis_size("tp") == 4
    f, c, t = lax.axis_index("fsdp"), lax.axis_index("ctx"), lax.axis_index("tp")
    mine = f * nc + c
    deep, part = modulate_weight.shape
    units = expand_weight.shape[1]
    tok, cot = tokens[0], cotangent[0]

    condition_low = jax.nn.silu(condition).astype(BF16)
    condition_here = lax.dynamic_slice_in_dim(condition_low, mine * deep, deep, 1)
    strips = part // 128
    high = -(-strips // 8) * 8
    bias_strips = jnp.pad(condition_bias.reshape(strips, 128), ((0, high - strips), (0, 0)))
    bias_pairs = attention_bias.reshape(heads, 2, HEAD_DIM)
    offset = jnp.stack(
        [bias_pairs[:, 0], jnp.zeros_like(bias_pairs[:, 0]), bias_pairs[:, 1]], axis=1
    ).reshape(-1, 1)
    condition_pad = jnp.pad(condition_here, ((0, 16 - nf), (0, 0)))
    (
        hidden_first, joint_full_t, mod, out_t, qkv, out, lse, att, expand_full,
        value, middle, hidden_two, shrink_early,
    ) = forward(
        nf, nc, part, tok, joint_weight, condition_pad, modulate_weight, bias_strips, offset,
        output_weight, expand_weight, residual_bias, shrink_weight,
    )
    (
        attn_own, mid_grad, shrink_half, shrink_parts, expand_grad, stats_second, hidden_stats,
        sh_cross, sh_own,
    ) = branch(
        nf, nc, part, hidden_two, cot, expand_full, shrink_weight, shrink_early, hidden_bias[None, :], mod, middle, value,
    )
    (
        mixed, tokens_grad, shrink_sum, expand_sum, output_sum, joint_sum, modulate_sum,
        bias_rows, done,
    ) = backward(
        nf, nc, part, attn_own, out_t, att, qkv, out, lse, sh_cross, sh_own, middle, cot,
        mod, residual_bias, shrink_half, shrink_parts, expand_grad, joint_full_t, hidden_first,
        tok, mid_grad, stats_second, hidden_stats, modulate_weight, condition_pad.astype(F32),
    )
    weights = (joint_weight, output_weight, expand_weight, shrink_weight, modulate_weight)
    moments = (joint_moments, output_moments, expand_moments, shrink_moments, modulate_moments)
    grads = (joint_sum, output_sum, expand_sum, shrink_sum, modulate_sum)
    smalls = (
        attention_bias[None, :], attention_moments, hidden_bias[None, :], hidden_moments,
        condition_bias[None, :], condition_moments, residual_bias, residual_moments,
    )
    results = adam(nf, nc, done, condition, bias_rows, tokens_grad, mixed, grads, weights, moments, smalls)
    updated = []
    for k in range(5):
        updated += [results[k], results[5 + k]]
    for k in range(4):
        new = results[10 + 2 * k]
        updated += [new[0] if k < 3 else new, results[11 + 2 * k]]
    return (
        results[21].reshape(1, rows, width),
        results[20].reshape(1, rows, width),
        results[18],
        results[19][0, 0],
    ) + tuple(updated)


def solution(mesh):
    rows = P(("fsdp", "ctx"), "tp")
    pair = P(None, ("fsdp", "ctx"), "tp")
    tokens = P("fsdp", "ctx", None)
    small = (P("tp"), P(None, "tp"))
    return jax.shard_map(
        partial(local, mesh.shape["fsdp"], mesh.shape["ctx"]),
        mesh=mesh,
        in_specs=(tokens, P(), tokens) + (rows, pair) * 5 + small * 3 + (P(), P()),
        out_specs=(tokens, tokens, P("fsdp", None), P())
        + (rows, pair) * 5
        + small * 3
        + (P(), P()),
        check_vma=False,
    )
```

time: 375 us -> 354 us (0.944)
  local copies, waits for them, and re-layouts: 22.9 us -> 3.84 us
  Pallas kernels: 338 us -> 343 us
    unnamed x87 -> x2, local copies, waits for them, and re-layouts: 21 us -> 0.01 us
    pallas_call x1, Pallas kernels: 6.42 us -> 11.5 us  [adam(): pl.pallas_call(partial(adam_body, count, nf, nc), out_shape=outs, in_spec...]
    convert_element_type x1 -> x0, other arithmetic: 4.22 us -> none  [local(): tokens_grad.reshape(1, rows, width).astype(F32)]
where the time goes in v4:
time: 354 us; the launch traced here: 350 us
  Pallas kernels  343 us (97%)
  local copies, waits for them, and re-layouts  3.84 us (1%)
    pallas_call x3, Pallas kernels, run(): pl.pallas_call(body, out_shape=outs, in_specs=[pl.BlockSpec(memory_space=...  331 us
    pallas_call x1, Pallas kernels, adam(): pl.pallas_call(partial(adam_body, count, nf, nc), out_shape=outs, in_spec...  11.5 us

profile of v4, /device:TPU:0, one launch (start us, length us, event | category | flops | bytes accessed | tf_op | source)
XLA Modules:
  0.0 350.4 jit_solution(9570318824755424471)
XLA Ops:
  0.7 0.7 fusion
  1.4 0.6 pad_convert_fusion
  2.0 0.8 reshape.63
  2.7 0.1 pad.11.clone
  2.8 0.1 pad_maximum_fusion
  2.9 1.1 reshape.68.offset
  4.0 1.3 pad.9.cbias
  5.3 126.4 %forward.1 = (bf16[1024,1024]{1,0:T(8,128)(2,1)}, bf16[768,1024]{1,0:T(8,128)(2,1)}, f32[4,16,128]{2,1,0:T(8,128)}, bf16[4,256,1024]{2,1,0:T(8,128)(2,1)}, bf16[...) custom-call(bf16[1024,1024]{1,0:T(8,128)(2,1)} %bitcast.12, ...), custom_call_target="tpu_custom_call" | custom-call | bytes 450000000 | tf_op jit(solution)/shard_map/forward/pallas_call | solution.py:68
  131.7 61.9 %branch.1 = (bf16[256,1024]{1,0:T(8,128)(2,1)}, f32[256,1024]{1,0:T(8,128)}, f32[128,512]{1,0:T(8,128)}, bf16[4,128,512]{2,1,0:T(8,128)(2,1)}, bf16[1024,1024]{1...) custom-call(bf16[4,256,1024]{2,1,0:T(8,128)(2,1)} %get-tuple-element., ...), custom_call_target="tpu_custom_call" | custom-call | bytes 120000000 | tf_op jit(solution)/shard_map/branch/pallas_call | solution.py:68
  193.6 0.0 copy-start
  193.6 143.0 %backward.1 = (bf16[4,256,1024]{2,1,0:T(8,128)(2,1)}, bf16[4,256,1024]{2,1,0:T(8,128)(2,1)}, f32[128,1024]{1,0:T(8,128)}, f32[128,1024]{1,0:T(8,128)}, f32[128,2...) custom-call(bf16[256,1024]{1,0:T(8,128)(2,1)} %get-tuple-element.81.a, ...), custom_call_target="tpu_custom_call" | custom-call | bytes 450000000 | tf_op jit(solution)/shard_map/backward/pallas_call | solution.py:68
  336.6 0.0 copy-done
  336.6 0.6 broadcast_in_dim.12.refs_19_
  337.2 11.5 %adam.1 = (f32[128,768]{1,0:T(8,128)}, f32[128,256]{1,0:T(8,128)}, f32[128,1024]{1,0:T(8,128)}, f32[128,1024]{1,0:T(8,128)}, f32[128,1536]{1,0:T(8,128)}, /*inde...) custom-call(f32[8,4,8,128]{3,2,1,0:T(8,128)} %get-tuple-element.97.d, ...), custom_call_target="tpu_custom_call" | custom-call | bytes 30000000 | tf_op jit(solution)/shard_map/adam/pallas_call | solution.py:1534
  348.7 1.3 reduce
  (1 shorter events, 0.0 us)
Async XLA Ops:
  193.6 143.0 %copy-start = (f32[1536]{0:T(1024)S(1)}, f32[1536]{0:T(1024)}, u32[]{:S(2)}) copy-start(f32[1536]{0:T(1024)} %param.38) | copy-start | bytes 18436

commit v5 on v4

--- a/solution.py
+++ b/solution.py
@@ -142,9 +142,9 @@
             for fo in range(1, self.nf)
         ]
 
-    def start(self):
+    def start(self, only=None):
         c = lax.axis_index("ctx")
-        for part in self.parts:
+        for part in self.parts if only is None else (only,):
             self.along(2, part).start()
             pl.when(c != 3)(self.along(1, part).start)
             pl.when(c != 0)(self.along(3, part).start)
@@ -379,7 +379,7 @@
     hidden_hbm, weight_hbm, mod, out_t_hbm, qkv_hbm, out_hbm, lse, land_hbm, ebuf_hbm,
     value, middle, hidden_two_hbm, sbuf_hbm,
     sweight, sbuf, tok, jweight, modw, oweight, eweight, out_t, qkv, out, ebuf, hidden_two,
-    hidden, weight_t, wbuf, obuf, oall, pbuf, pland, normed, joint, stage, land, keys, scores,
+    hidden, weight_t, wbuf, obuf, oall, pbuf, pland, normed, joint, stage, land, keys, scores, columns,
     lsem, ssem, psend, precv, msend, mrecv, send, recv, osend, orecv, hsend, hrecv, asend, arecv,
     *gsems,
 ):
@@ -434,7 +434,8 @@
     total_mod = pland[0]
     for k in range(1, group):
         total_mod = total_mod + pland[k]
-    mod[t] = total_mod + cbias[...]
+    for k in range(strips):
+        mod[t, pl.ds(k, 1), :] = total_mod[k : k + 1, :] + cbias[:, 128 * k : 128 * k + 128]
     mcopies = []
     for o, peer in zip(range(1, 4), ring_peers("tp", 4)):
         copy = remote(mod.at[t], mod.at[t], msend.at[o], mrecv.at[o], peer)
@@ -458,7 +459,6 @@
 
     lax.fori_loop(0, rows // step, hide_rows, 0)
     joint_gather.relay_rest(1)
-    output_gather.start()
     joint_gather.arrive()
     deep = jweight.shape[0]
     for k in range(group):
@@ -476,10 +476,14 @@
         )
 
     copies = []
+    biases = offset.shape[1]
+    columns[...] = jnp.broadcast_to(offset[...], (128, biases)).T
     for o in (2, 1, 3, 0):
         dst = lax.rem(c + o, nc)
         where = aligned(dst * 3 * hd, 3 * hd)
-        head = (dot(weight_t[where, :], hidden[...], 1, 1) + offset[where, :]).astype(BF16)
+        pair = columns[aligned(dst * 2 * hd, 2 * hd), 0:1]
+        added = jnp.concatenate([pair[0:hd], jnp.zeros((hd, 1), F32), pair[hd : 2 * hd]], axis=0)
+        head = (dot(weight_t[where, :], hidden[...], 1, 1) + added).astype(BF16)
         if o == 0:
             qkv[:, aligned(c * rows, rows)] = head
         else:
@@ -491,6 +495,7 @@
             )
             copy.start()
             copies.append(copy)
+    output_gather.start()
     for o in (2, 1, 3):
         query_copy(o).start()
     saves = [
@@ -505,14 +510,10 @@
     ]
     saves[0].start()
     saves[1].start()
-    output_gather.relay()
-    output_gather.arrive()
-    oall[mine] = obuf[...].reshape(width, nc * hd)
     weights_share = Share(oall, asend, arecv)
-    weights_share.start()
     for copy in copies:
         copy.wait_recv()
-    expand_gather.start()
+    expand_gather.start(0)
     for at in range(0, total, 1024):
         keys[at : at + 1024, :] = transposed(qkv[hd : 2 * hd, at : at + 1024])
 
@@ -532,16 +533,23 @@
         def _():
             query_copy(o).wait_recv()
 
-        @pl.when(i == 2 * per)
+        @pl.when(i == per)
+        def _():
+            output_gather.relay()
+
+        @pl.when(i == per + 1)
+        def _():
+            output_gather.arrive()
+            oall[mine] = obuf[...].reshape(width, nc * hd)
+            weights_share.start()
+
+        @pl.when(i == per * nc - 1)
+        def _():
+            weights_share.relay()
+
+        @pl.when(i == 3 * per)
         def _():
             expand_gather.relay_middle(0)
-            expand_gather.relay_middle(1)
-
-        @pl.when(i == 3 * per)
-        def _():
-            expand_gather.relay_rest(0)
-            expand_gather.relay_rest(1)
-            shrink_gather.start()
             saves[3].start()
 
         where = aligned(owner * rows + sub * bq, bq)
@@ -572,25 +580,18 @@
             for k in range(1, 4):
                 given(o, k).start()
 
-        @pl.when(i == per - 1)
-        def _():
-            weights_share.relay()
-
-        @pl.when(i == 2 * per - 1)
-        def _():
-            weights_share.finish()
-            for k in range(4):
-                out_t[k] = transposed(oall[k])
-            saves[2].start()
-
         return carry
 
     lax.fori_loop(0, per * nc, block, 0)
+    expand_gather.start(1)
+    shrink_gather.start()
     land[t, c] = stage[c, :, aligned(t * own, own)]
+    expand_gather.relay_rest(0)
+    weights_share.finish()
+    for k in range(4):
+        out_t[k] = transposed(oall[k])
+    saves[2].start()
     saves[4].start()
-    expand_gather.arrive()
-    saves[6].start()
-    shrink_gather.relay_middle(0)
 
     order = [(o, k) for o in (0, 2, 3, 1) for k in range(4) if o or k]
     for o, k in order:
@@ -609,18 +610,23 @@
     sharing = Share(hidden_two, hsend, hrecv)
     sharing.start()
     saves[5].start()
+    expand_gather.relay_middle(1)
+    shrink_gather.relay_middle(0)
+    expand_gather.relay_rest(1)
     shrink_gather.relay_rest(0)
+    sharing.relay()
     for o, k in order:
         given(o, k).wait_send()
     for o in (2, 1, 3):
         query_copy(o).wait_send()
     for copy in pcopies + mcopies + copies:
         copy.wait_send()
+    expand_gather.arrive()
+    saves[6].start()
+    sharing.finish()
+    saves[8].start()
     shrink_gather.arrive()
     saves[7].start()
-    sharing.relay()
-    sharing.finish()
-    saves[8].start()
     for copy in saves:
         copy.wait()
     for gather in (joint_gather, output_gather, expand_gather, shrink_gather):
@@ -635,13 +641,14 @@
     total = rows * nc
     hd = HEAD_DIM
     bq = min(512, rows)
+    high = -(-part // 1024) * 8
     return call(
         partial(forward_body, nf, nc, part),
         "forward",
         (
             shape((rows, width), BF16),
             shape((columns, width), BF16),
-            shape((4,) + cbias.shape, F32),
+            shape((4, high, 128), F32),
             shape((4, nc * hd, width), BF16),
             shape((3 * hd, total), BF16),
             shape((hd, total), F32),
@@ -671,14 +678,15 @@
             pltpu.VMEM((group, deep, columns), BF16),
             pltpu.VMEM((group,) + oweight.shape, BF16),
             pltpu.VMEM((4, width, nc * hd), BF16),
-            pltpu.VMEM((nf,) + cbias.shape, F32),
-            pltpu.VMEM((group,) + cbias.shape, F32),
+            pltpu.VMEM((nf, high, 128), F32),
+            pltpu.VMEM((group, high, 128), F32),
             pltpu.VMEM((rows, width), F32),
             pltpu.VMEM((columns, rows), BF16),
             pltpu.VMEM((nc, hd, rows), BF16),
             pltpu.VMEM((4, nc, hd, own), BF16),
             pltpu.VMEM((total, hd), BF16),
             pltpu.VMEM((total, bq), F32),
+            pltpu.VMEM((offset.shape[1], 128), F32),
             DMA((6,)), DMA((9,)),
             DMA((group,)), DMA((group,)), DMA((4,)), DMA((4,)),
             DMA((2, nc)), DMA((2, nc)), DMA((nc, 4)), DMA((nc, 4)), DMA((3,)), DMA((3,)),
@@ -695,10 +703,10 @@
 
 def branch_body(
     nf, nc, part, hidden_hbm, cot_hbm, expand_hbm, sw_hbm, sbuf_hbm, hbias, mod, middle, value,
-    attn_own, mid_grad, shrink_half, shrink_rest, expand_grad, stats, hstats, sh_cross, sh_own,
+    attn_own, mid_grad, shrink_half, shrink_late, expand_grad, stats, hstats, sh_cross, sh_own,
     cot, hidden, expand, sweight, sgat, gbuf, abuf, ebuf, slopes, held_buf,
     shrink_grad, shrink_parts, sland, dland, sbuf, rbuf, shold,
-    lsem, tsend, trecv, send, recv, s1s, s1r, s2s, s2r, d1s, d1r, d2s, d2r, *gsems,
+    lsem, tsend, trecv, send, recv, s1s, s1r, d1s, d1r, *gsems,
 ):
     mine, partner, cross, far = tp_places()
     own, width = middle.shape
@@ -758,15 +766,11 @@
     for at in range(0, width, step):
         block = dot(gbuf[:, at : at + step], abuf[...], 0, 0).astype(BF16)
         for k in range(at // deep, (at + step) // deep):
-            shrink_grad[k // nc, k % nc] = block[k * deep - at : (k + 1) * deep - at, :]
-    early = Scatter(
-        nf, nc, shrink_grad, shrink_parts, sland, dland, s1s, s1r, d1s, d1r, (0, split)
-    )
-    late = Scatter(
-        nf, nc, shrink_grad, shrink_parts, sland, dland, s2s, s2r, d2s, d2r, (split, split)
-    )
+            rows_k = slice(k * deep - at, (k + 1) * deep - at)
+            shrink_grad[k // nc, k % nc] = block[rows_k, 0:split]
+            shrink_late[k // nc, k % nc] = block[rows_k, split:units]
+    early = Scatter(nf, nc, shrink_grad, shrink_parts, sland, dland, s1s, s1r, d1s, d1r)
     early.swap()
-    late.swap()
     gather.arrive()
     hstats[...] = jnp.zeros_like(hstats)
     summing = Sum(sbuf, rbuf, send, recv)
@@ -832,11 +836,8 @@
     stats[2:3, :] = jnp.sum(mgrad * value[...], axis=0, keepdims=True)
     stats[4:5, :] = jnp.sum(agrad, axis=0, keepdims=True)
     stats[5:8, :] = jnp.zeros((3, width), F32)
-    late.swapped()
-    shrink_rest[...] = shrink_parts[:, :, split:units]
     shrink_half[...] = early.dealt()
     early.drain()
-    late.drain(deals=False)
     summing.drain()
     gather.drain()
     for copy in copies:
@@ -855,7 +856,7 @@
             shape((own, width), BF16),
             shape((own, width), F32),
             shape((deep, units // 2), F32),
-            shape((nc, deep, units // 2), BF16),
+            shape((nf, nc, deep, units // 2), BF16),
             shape((width, units), BF16),
             shape((8, width), F32),
             shape((1, units), F32),
@@ -873,18 +874,18 @@
             pltpu.VMEM((rows, units), BF16),
             pltpu.VMEM((rows, units), F32),
             pltpu.VMEM((own, width), F32),
-            pltpu.VMEM((nf, nc, deep, units), BF16),
-            pltpu.VMEM((nc, deep, units), BF16),
-            pltpu.VMEM((nf - 1, nc, deep, units), BF16),
-            pltpu.VMEM((nc - 1, deep, units), BF16),
+            pltpu.VMEM((nf, nc, deep, units // 2), BF16),
+            pltpu.VMEM((nc, deep, units // 2), BF16),
+            pltpu.VMEM((nf - 1, nc, deep, units // 2), BF16),
+            pltpu.VMEM((nc - 1, deep, units // 2), BF16),
             pltpu.VMEM((3, own, width), BF16),
             pltpu.VMEM((3, own, width), BF16),
             pltpu.VMEM((4, own, width), BF16),
             DMA((5,)), DMA((2,)), DMA((2,)),
         ]
         + share_sems()
-        + [DMA((nf,))] * 4
-        + [DMA((nc,))] * 4
+        + [DMA((nf,))] * 2
+        + [DMA((nc,))] * 2
         + gather_sems(nf, nc, 1),
         2,
         40,
@@ -895,16 +896,16 @@
 
 def backward_body(
     nf, nc, part, attn_own, out_t_hbm, heads_hbm, qkv_hbm, out_hbm, lse, sh_cross, sh_own, middle,
-    cot_hbm, mod, bias, shrink_half, shrink_parts, expand_grad, weight_hbm, hidden_hbm, tok_hbm,
+    cot_hbm, mod, bias, shrink_half, shrink_grad, expand_grad, weight_hbm, hidden_hbm, tok_hbm,
     mid_grad, stats_second, hidden_stats, modw_hbm, low,
     mixed, tokens_grad, shrink_sum, expand_sum, output_sum, joint_sum, modulate_sum,
     bias_rows, done,
     out_t, qkv, out, heads, att, cot_own, tok_own, weight_t, hidden, modw,
-    attn_low, dout, dost, keys, vals, dq, stage, rland, delta, output_grad, eland, oland,
-    expand_parts, output_parts, sdeal, edeal, odeal, joint_grad, sbuf, rbuf,
+    attn_low, dout, dost, keys, vals, dq, dkv, stage, rland, delta, output_grad,
+    sland, shrink_parts, eland, oland, expand_parts, output_parts, sdeal, edeal, odeal, joint_grad, sbuf, rbuf,
     kvgrad, kvland, kvparts, kvdeal, qgrad, qland, qparts, qdeal, pieces, land, total_piece, gathered, ftotal, gate_row,
     lsem, send, recv, jsend, jrecv, csend, crecv, gsend, grecv, tsend, trecv, hsend, hrecv,
-    lowsend, lowrecv, hsend2, hrecv2, x1s, x1r, x2s, x2r, x3s, x3r, x4s, x4r, x5s, x5r,
+    lowsend, lowrecv, hsend2, hrecv2, x1s, x1r, x2s, x2r, x3s, x3r, x4s, x4r, x5s, x5r, x6s, x6r,
     d1s, d1r, d2s, d2r, d3s, d3r, d4s, d4r, d5s, d5r, d6s, d6r, asend, arecv, bsend, brecv, f1s, f1r,
 ):
     f, c, t = lax.axis_index("fsdp"), lax.axis_index("ctx"), lax.axis_index("tp")
@@ -921,7 +922,7 @@
     heads_wide = nc * hd
     units = expand_grad.shape[3]
     half = units // 2
-    shrink = Scatter(nf, nc, None, shrink_parts, eland, sdeal, None, None, d1s, d1r)
+    shrink = Scatter(nf, nc, shrink_grad, shrink_parts, sland, sdeal, x6s, x6r, d1s, d1r)
     early = Scatter(
         nf, nc, expand_grad, expand_parts, eland, edeal, x1s, x1r, d2s, d2r, (0, half)
     )
@@ -954,16 +955,14 @@
             {"ctx": cc, "tp": tt},
         )
 
-    order = [(o, k) for o in (2, 1, 3, 0) for k in range(4) if o or k]
+    order = [(o, k) for o in (0, 2, 1, 3) for k in range(4) if o or k]
+    shrink.swap()
     for o, k in order:
         send_out(o, k).start()
     low_share = Share(attn_low, lowsend, lowrecv)
     low_share.start()
+    crossing = remote(sh_cross, rland, csend, crecv, {"tp": cross})
     early.swap()
-    late.swap()
-    crossing = remote(sh_cross, rland, csend, crecv, {"tp": cross})
-    crossing.start()
-    shrink.deal()
     dout[:, where_own] = dost[t, c]
     for copy in loads[1:4]:
         copy.wait()
@@ -971,12 +970,7 @@
         keys[at : at + 1024, :] = transposed(qkv[hd : 2 * hd, at : at + 1024])
         vals[at : at + 1024, :] = transposed(qkv[2 * hd : 3 * hd, at : at + 1024])
     dq[...] = jnp.zeros_like(dq)
-    for o, k in order:
-        send_out(o, k).wait_recv()
-    for at in range(0, total, 1024):
-        delta[:, at : at + 1024] = jnp.sum(
-            dout[:, at : at + 1024].astype(F32) * out[:, at : at + 1024], axis=0, keepdims=True
-        )
+    dkv[...] = jnp.zeros_like(dkv)
     sharing = Share(mixed, gsend, grecv)
     exchange = [
         remote(heads.at[peer["tp"]], att.at[:, :, own_rows], hsend2.at[k], hrecv2.at[k], peer)
@@ -995,39 +989,96 @@
             jsend.at[1, o], jrecv.at[1, o], {"ctx": owner},
         )
 
+    count = per * nc
+
     def block(i, vsum):
-        o = 1 + i // per
+        turn, step = i // count, lax.rem(i, count)
+        owners = (lax.rem(c + turn * (nc - 1), nc), lax.rem(c + 2 + turn * (nc - 1), nc))
+
+        @pl.when(i == 0)
+        def _():
+            for o, k in order:
+                if o in (0, 2):
+                    send_out(o, k).wait_recv()
+
+        @pl.when(i == count)
+        def _():
+            for o, k in order:
+                if o in (1, 3):
+                    send_out(o, k).wait_recv()
+
+        @pl.when(step == 0)
+        def _():
+            for owner in owners:
+                where_q = aligned(owner * rows, rows)
+                delta[:, where_q] = jnp.sum(
+                    dout[:, where_q].astype(F32) * out[:, where_q], axis=0, keepdims=True
+                )
+
+        o = 1 + step // per
         owner = lax.rem(c + o, nc)
-        sub = lax.rem(i, per)
+        sub = lax.rem(step, per)
         where = aligned(owner * rows + sub * bk, bk)
         key, val, key_t = keys[where, :], vals[where, :], qkv[hd : 2 * hd, where]
-        dk, dv = None, None
-        for at in range(0, total, bq):
-            query = qkv[0:hd, at : at + bq] * BF16(hd**-0.5)
-            grad = dout[:, at : at + bq]
-            p = jnp.exp(dot(key, query, 1, 0) - lse[:, at : at + bq])
-            ds = (p * (dot(val, grad, 1, 0) - delta[:, at : at + bq])).astype(BF16)
-            tv = dot(grad, p.astype(BF16), 1, 1)
-            tk = dot(query, ds, 1, 1)
-            dv = tv if dv is None else dv + tv
-            dk = tk if dk is None else dk + tk
-            dq[:, at : at + bq] += dot(key_t, ds, 1, 0)
+        dk, dv = dkv[0:hd, where], dkv[hd : 2 * hd, where]
+        for source in owners:
+            for half_ in range(rows // bq):
+                at = aligned(source * rows + half_ * bq, bq)
+                query = qkv[0:hd, at] * BF16(hd**-0.5)
+                grad = dout[:, at]
+                p = jnp.exp(dot(key, query, 1, 0) - lse[:, at])
+                ds = (p * (dot(val, grad, 1, 0) - delta[:, at])).astype(BF16)
+                dv = dv + dot(grad, p.astype(BF16), 1, 1)
+                dk = dk + dot(query, ds, 1, 1)
+                dq[:, at] += dot(key_t, ds, 1, 0)
+        dkv[0:hd, where] = dk
+        dkv[hd : 2 * hd, where] = dv
         put = aligned(sub * bk, bk)
-        stage[owner, hd : 2 * hd, put] = dk.astype(BF16)
-        stage[owner, 2 * hd : 3 * hd, put] = dv.astype(BF16)
-
-        @pl.when(jnp.logical_and(sub == per - 1, o < nc))
+
+        @pl.when(turn == 1)
+        def _():
+            stage[owner, hd : 2 * hd, put] = dkv[0:hd, where].astype(BF16)
+            stage[owner, 2 * hd : 3 * hd, put] = dkv[hd : 2 * hd, where].astype(BF16)
+
+        @pl.when(jnp.logical_and(turn == 1, jnp.logical_and(sub == per - 1, o < nc)))
         def _():
             kv_back(o, owner).start()
 
         @pl.when(i == 1)
         def _():
-            low_share.relay()
+            shrink.swapped()
+            shrink.deal()
+
+        @pl.when(i == 0)
+        def _():
             att[:, :, own_rows] = heads[t]
             for copy in exchange:
                 copy.start()
 
+        @pl.when(i == 2)
+        def _():
+            low_share.relay()
+            crossing.start()
+
+        @pl.when(i == 8)
+        def _():
+            crossing.wait_recv()
+            loads[4].wait()
+            value = sh_own[...] + rland[...].astype(F32) + bias[1:2, :]
+            gate = row_of(mod, 5 * width, width, part)
+            mixed[mine] = (middle[...] + gate * value).astype(BF16)
+            sharing.start()
+            gate_row[...] = jnp.sum(
+                cot_own[...].astype(F32) * value, axis=0, keepdims=True
+            )
+
         @pl.when(i == 3)
+        def _():
+            early.swapped()
+            early.deal()
+            late.swap()
+
+        @pl.when(i == 6)
         def _():
             for k in (1, 2):
                 low_share.copy(k).wait_recv()
@@ -1039,43 +1090,35 @@
             output_grad[...] = flat.reshape(output_grad.shape)
             project.swap()
 
-        @pl.when(i == 2)
-        def _():
-            crossing.wait_recv()
-            loads[4].wait()
-            value = sh_own[...] + rland[...].astype(F32) + bias[1:2, :]
-            gate = row_of(mod, 5 * width, width, part)
-            mixed[mine] = (middle[...] + gate * value).astype(BF16)
-            sharing.start()
-            gate_row[...] = jnp.sum(
-                cot_own[...].astype(F32) * value, axis=0, keepdims=True
-            )
-
-        @pl.when(i == 2)
-        def _():
-            early.swapped()
-            early.deal()
-
-        @pl.when(i == 4)
+        @pl.when(i == count - 1)
+        def _():
+            for source in owners:
+                stage[source, 0:hd, :] = (
+                    dq[:, aligned(source * rows, rows)] * (hd**-0.5)
+                ).astype(BF16)
+            q_back(2, owners[1]).start()
+
+        @pl.when(i == 9)
         def _():
             late.swapped()
 
-        @pl.when(i == 6)
+        @pl.when(i == 11)
         def _():
             project.swapped()
+
+        @pl.when(i == 14)
+        def _():
             sharing.relay()
 
-        return vsum + jnp.sum(dv, axis=1, keepdims=True)
-
-    vsum = lax.fori_loop(0, per * nc, block, jnp.zeros((hd, 1), F32))
-    qsum = jnp.zeros((hd, 1), F32)
-    for o in (2, 1, 3, 0):
+        return vsum
+
+    lax.fori_loop(0, 2 * count, block, 0)
+    for o in (1, 3):
         owner = lax.rem(c + o, nc)
-        piece = dq[:, aligned(owner * rows, rows)] * (hd**-0.5)
-        qsum = qsum + jnp.sum(piece, axis=1, keepdims=True)
-        stage[owner, 0:hd, :] = piece.astype(BF16)
-        if o > 0:
-            q_back(o, owner).start()
+        stage[owner, 0:hd, :] = (dq[:, aligned(owner * rows, rows)] * (hd**-0.5)).astype(BF16)
+        q_back(o, owner).start()
+    qsum = jnp.sum(dq[...] * (hd**-0.5), axis=1, keepdims=True)
+    vsum = jnp.sum(dkv[hd : 2 * hd, :], axis=1, keepdims=True)
     late.deal()
     project.deal()
     joint_grad[c] = stage[c]
@@ -1285,8 +1328,7 @@
     for copy in exchange:
         copy.wait_send()
     crossing.wait_send()
-    shrink.drain(swaps=False)
-    for scatter in (early, late, project, kv, query):
+    for scatter in (shrink, early, late, project, kv, query):
         scatter.drain()
     for copy in third:
         copy.wait_recv()
@@ -1296,7 +1338,7 @@
 
 def backward(
     nf, nc, part, attn_own, out_t, att, qkv, out, lse, sh_cross, sh_own, middle, cot, mod, bias,
-    shrink_half, shrink_parts, expand_grad, weight_t, hidden, tok, mid_grad, stats_second, hidden_stats,
+    shrink_half, shrink_grad, expand_grad, weight_t, hidden, tok, mid_grad, stats_second, hidden_stats,
     modw, low,
 ):
     rows, width = cot.shape
@@ -1342,10 +1384,13 @@
             pltpu.VMEM((total, hd), BF16),
             pltpu.VMEM((total, hd), BF16),
             pltpu.VMEM((hd, total), F32),
+            pltpu.VMEM((2 * hd, total), F32),
             pltpu.VMEM((nc, 3 * hd, rows), BF16),
             pltpu.VMEM((own, width), BF16),
             pltpu.VMEM((1, total), F32),
             pltpu.VMEM((nf, nc, deep, heads_wide), BF16),
+            pltpu.VMEM((nf - 1, nc, deep, units // 2), BF16),
+            pltpu.VMEM((nc, deep, units // 2), BF16),
             pltpu.VMEM((nf - 1, nc, deep, units), BF16),
             pltpu.VMEM((nf - 1, nc, deep, heads_wide), BF16),
             pltpu.VMEM((nc, deep, units), BF16),
@@ -1375,7 +1420,7 @@
         ]
         + share_sems() * 4
         + [DMA((4,))] * 2
-        + [DMA((nf,))] * 10
+        + [DMA((nf,))] * 12
         + [DMA((nc,))] * 12
         + [DMA((inner,))] * 2
         + [DMA((group,))] * 2
@@ -1386,7 +1431,7 @@
         ins=(1, 2, 3, 4, 9, 15, 16, 17, 21),
     )(
         attn_own, out_t, att, qkv, out, lse, sh_cross, sh_own, middle, cot, mod, bias,
-        shrink_half, shrink_parts, expand_grad, weight_t, hidden, tok, mid_grad, stats_second,
+        shrink_half, shrink_grad, expand_grad, weight_t, hidden, tok, mid_grad, stats_second,
         hidden_stats, modw, low,
     )
 
@@ -1586,23 +1631,17 @@
 
     condition_low = jax.nn.silu(condition).astype(BF16)
     condition_here = lax.dynamic_slice_in_dim(condition_low, mine * deep, deep, 1)
-    strips = part // 128
-    high = -(-strips // 8) * 8
-    bias_strips = jnp.pad(condition_bias.reshape(strips, 128), ((0, high - strips), (0, 0)))
-    bias_pairs = attention_bias.reshape(heads, 2, HEAD_DIM)
-    offset = jnp.stack(
-        [bias_pairs[:, 0], jnp.zeros_like(bias_pairs[:, 0]), bias_pairs[:, 1]], axis=1
-    ).reshape(-1, 1)
     condition_pad = jnp.pad(condition_here, ((0, 16 - nf), (0, 0)))
     (
         hidden_first, joint_full_t, mod, out_t, qkv, out, lse, att, expand_full,
         value, middle, hidden_two, shrink_early,
     ) = forward(
-        nf, nc, part, tok, joint_weight, condition_pad, modulate_weight, bias_strips, offset,
+        nf, nc, part, tok, joint_weight, condition_pad, modulate_weight, condition_bias[None, :],
+        attention_bias[None, :],
         output_weight, expand_weight, residual_bias, shrink_weight,
     )
     (
-        attn_own, mid_grad, shrink_half, shrink_parts, expand_grad, stats_second, hidden_stats,
+        attn_own, mid_grad, shrink_half, shrink_late, expand_grad, stats_second, hidden_stats,
         sh_cross, sh_own,
     ) = branch(
         nf, nc, part, hidden_two, cot, expand_full, shrink_weight, shrink_early, hidden_bias[None, :], mod, middle, value,
@@ -1612,7 +1651,7 @@
         bias_rows, done,
     ) = backward(
         nf, nc, part, attn_own, out_t, att, qkv, out, lse, sh_cross, sh_own, middle, cot,
-        mod, residual_bias, shrink_half, shrink_parts, expand_grad, joint_full_t, hidden_first,
+        mod, residual_bias, shrink_half, shrink_late, expand_grad, joint_full_t, hidden_first,
         tok, mid_grad, stats_second, hidden_stats, modulate_weight, condition_pad.astype(F32),
     )
     weights = (joint_weight, output_weight, expand_weight, shrink_weight, modulate_weight)

time: 354 us -> 329 us (0.929)
  Pallas kernels: 343 us -> 324 us
    pallas_call x3, Pallas kernels: 331 us -> 312 us  [run(): pl.pallas_call(body, out_shape=outs, in_specs=[pl.BlockSpec(memory_space=...]
where the time goes in v5:
time: 329 us; the launch traced here: 328 us
  Pallas kernels  324 us (98%)
    pallas_call x3, Pallas kernels, run(): pl.pallas_call(body, out_shape=outs, in_specs=[pl.BlockSpec(memory_space=...  312 us
    pallas_call x1, Pallas kernels, adam(): pl.pallas_call(partial(adam_body, count, nf, nc), out_shape=outs, in_spec...  11.6 us

profile of v5, /device:TPU:0, one launch (start us, length us, event | category | flops | bytes accessed | tf_op | source)
XLA Modules:
  0.0 328.4 jit_solution(6170659847583871320)
XLA Ops:
  0.7 0.7 fusion
  1.4 1.3 broadcast_in_dim.12.cbias.refs_19_
  2.7 0.6 pad_convert_fusion
  3.3 132.4 %forward.1 = (bf16[1024,1024]{1,0:T(8,128)(2,1)}, bf16[768,1024]{1,0:T(8,128)(2,1)}, f32[4,16,128]{2,1,0:T(8,128)}, bf16[4,256,1024]{2,1,0:T(8,128)(2,1)}, bf16[...) custom-call(bf16[1024,1024]{1,0:T(8,128)(2,1)} %bitcast.10, ...), custom_call_target="tpu_custom_call" | custom-call | bytes 450000000 | tf_op jit(solution)/shard_map/forward/pallas_call | solution.py:68
  135.7 46.2 %branch.1 = (bf16[256,1024]{1,0:T(8,128)(2,1)}, f32[256,1024]{1,0:T(8,128)}, f32[128,512]{1,0:T(8,128)}, bf16[2,4,128,512]{3,2,1,0:T(8,128)(2,1)}, bf16[1024,102...) custom-call(bf16[4,256,1024]{2,1,0:T(8,128)(2,1)} %get-tuple-element, ...), custom_call_target="tpu_custom_call" | custom-call | bytes 120000000 | tf_op jit(solution)/shard_map/branch/pallas_call | solution.py:68
  181.9 133.6 %backward.1 = (bf16[4,256,1024]{2,1,0:T(8,128)(2,1)}, bf16[4,256,1024]{2,1,0:T(8,128)(2,1)}, f32[128,1024]{1,0:T(8,128)}, f32[128,1024]{1,0:T(8,128)}, f32[128,2...) custom-call(bf16[256,1024]{1,0:T(8,128)(2,1)} %get-tuple-element.81.a, ...), custom_call_target="tpu_custom_call" | custom-call | bytes 450000000 | tf_op jit(solution)/shard_map/backward/pallas_call | solution.py:68
  315.5 11.6 %adam.1 = (f32[128,768]{1,0:T(8,128)}, f32[128,256]{1,0:T(8,128)}, f32[128,1024]{1,0:T(8,128)}, f32[128,1024]{1,0:T(8,128)}, f32[128,1536]{1,0:T(8,128)}, /*inde...) custom-call(f32[8,4,8,128]{3,2,1,0:T(8,128)} %get-tuple-element.97.d, ...), custom_call_target="tpu_custom_call" | custom-call | bytes 30000000 | tf_op jit(solution)/shard_map/adam/pallas_call | solution.py:1579
  327.1 1.3 reduce

commit v6 on v5

--- a/solution.py
+++ b/solution.py
@@ -34,10 +34,15 @@
 
 
 def greet(peers):
-    barrier = pltpu.get_barrier_semaphore()
     for peer in peers:
-        pl.semaphore_signal(barrier, inc=1, device_id=peer, device_id_type=MESH)
-    pl.semaphore_wait(barrier, len(peers))
+        pl.semaphore_signal(
+            pltpu.get_barrier_semaphore(), inc=1, device_id=peer, device_id_type=MESH
+        )
+    return len(peers)
+
+
+def meet(count):
+    pl.semaphore_wait(pltpu.get_barrier_semaphore(), count)
 
 
 def remote(source, target, send_sem, recv_sem, peer):
@@ -392,6 +397,7 @@
     strips = part // 128
     hd = HEAD_DIM
     step = 128
+    greeted = greet(weight_peers(nf, nc) + head_peers(nc))
     loads = load_all(
         (
             (jw_hbm, jweight), (modw_hbm, modw), (tok_hbm, tok), (ow_hbm, oweight),
@@ -405,7 +411,7 @@
     shrink_gather = Gather(sbuf, nf, nc, gsems[20:24], 1)
     loads[0].wait()
     wbuf[slot] = jweight[...].astype(BF16)
-    greet(weight_peers(nf, nc) + head_peers(nc))
+    meet(greeted)
     joint_gather.start()
     loads[1].wait()
     partial_mod = dot(cond[...], modw[...].astype(BF16), 1, 0)
@@ -713,6 +719,7 @@
     group = nf * nc
     deep, units = sweight.shape
     slot = lax.axis_index("fsdp") * nc + lax.axis_index("ctx")
+    greeted = greet(ring_peers("tp", 4) + weight_peers(nf, nc))
     gate_first = row_of(mod, 2 * width, width, part)
     scale_second = row_of(mod, 4 * width, width, part)
     gate_second = row_of(mod, 5 * width, width, part)
@@ -726,7 +733,7 @@
     )
     loads[0].wait()
     sgat[slot, :, split:units] = sweight[:, split:units].astype(BF16)
-    greet(ring_peers("tp", 4) + weight_peers(nf, nc))
+    meet(greeted)
     gather = Gather(sgat, nf, nc, gsems, 2, 1)
     gather.start()
     for copy in loads[1:]:
@@ -932,6 +939,7 @@
     project = Scatter(nf, nc, output_grad, output_parts, oland, odeal, x3s, x3r, d4s, d4r)
     kv = Scatter(nf, nc, kvgrad, kvparts, kvland, kvdeal, x4s, x4r, d5s, d5r)
     query = Scatter(nf, nc, qgrad, qparts, qland, qdeal, x5s, x5r, d6s, d6r)
+    greeted = greet(all_peers(nf, nc))
     own_rows = aligned(mine * own, own)
     loads = load_all(
         (
@@ -945,7 +953,7 @@
     loads[0].wait()
     for k in range(4):
         dost[k] = dot(out_t[k], attn_own[...], 1, 1).astype(BF16).reshape(nc, hd, own)
-    greet(all_peers(nf, nc))
+    meet(greeted)
     where_own = aligned(c * rows + t * own, own)
 
     def send_out(o, k):
@@ -1120,7 +1128,6 @@
     qsum = jnp.sum(dq[...] * (hd**-0.5), axis=1, keepdims=True)
     vsum = jnp.sum(dkv[hd : 2 * hd, :], axis=1, keepdims=True)
     late.deal()
-    project.deal()
     joint_grad[c] = stage[c]
     bias_column = jnp.concatenate([qsum, vsum], axis=0)
     for copy in loads[5:]:
@@ -1237,6 +1244,7 @@
         copy = remote(total_piece, gathered.at[slot], bsend.at[o], brecv.at[o], peer)
         copy.start()
         second.append(copy)
+    project.deal()
     expand_total = early.dealt()
     expand_sum[:, 0:half] = expand_total
     squares = squares + jnp.sum(expand_total * expand_total)
@@ -1672,7 +1680,7 @@
         results[21].reshape(1, rows, width),
         results[20].reshape(1, rows, width),
         results[18],
-        results[19][0, 0],
+        results[19].reshape(()),
     ) + tuple(updated)
 
 

time: 329 us -> 326 us (level)
  no operation moved by 1% of the time
where the time goes in v6:
time: 326 us; the launch traced here: 325 us
  Pallas kernels  321 us (98%)
    pallas_call x3, Pallas kernels, run(): pl.pallas_call(body, out_shape=outs, in_specs=[pl.BlockSpec(memory_space=...  309 us
    pallas_call x1, Pallas kernels, adam(): pl.pallas_call(partial(adam_body, count, nf, nc), out_shape=outs, in_spec...  11.6 us

profile of v6, /device:TPU:0, one launch (start us, length us, event | category | flops | bytes accessed | tf_op | source)
XLA Modules:
  0.0 325.4 jit_solution(8632146557410654284)
XLA Ops:
  0.7 0.7 fusion
  1.4 1.3 broadcast_in_dim.12.cbias.refs_19_
  2.7 0.6 pad_convert_fusion
  3.3 131.2 %forward.1 = (bf16[1024,1024]{1,0:T(8,128)(2,1)}, bf16[768,1024]{1,0:T(8,128)(2,1)}, f32[4,16,128]{2,1,0:T(8,128)}, bf16[4,256,1024]{2,1,0:T(8,128)(2,1)}, bf16[...) custom-call(bf16[1024,1024]{1,0:T(8,128)(2,1)} %bitcast.10, ...), custom_call_target="tpu_custom_call" | custom-call | bytes 450000000 | tf_op jit(solution)/shard_map/forward/pallas_call | solution.py:73
  134.4 45.1 %branch.1 = (bf16[256,1024]{1,0:T(8,128)(2,1)}, f32[256,1024]{1,0:T(8,128)}, f32[128,512]{1,0:T(8,128)}, bf16[2,4,128,512]{3,2,1,0:T(8,128)(2,1)}, bf16[1024,102...) custom-call(bf16[4,256,1024]{2,1,0:T(8,128)(2,1)} %get-tuple-element, ...), custom_call_target="tpu_custom_call" | custom-call | bytes 120000000 | tf_op jit(solution)/shard_map/branch/pallas_call | solution.py:73
  179.5 132.9 %backward.1 = (bf16[4,256,1024]{2,1,0:T(8,128)(2,1)}, bf16[4,256,1024]{2,1,0:T(8,128)(2,1)}, f32[128,1024]{1,0:T(8,128)}, f32[128,1024]{1,0:T(8,128)}, f32[128,2...) custom-call(bf16[256,1024]{1,0:T(8,128)(2,1)} %get-tuple-element.81.a, ...), custom_call_target="tpu_custom_call" | custom-call | bytes 450000000 | tf_op jit(solution)/shard_map/backward/pallas_call | solution.py:73
  312.5 11.6 %adam.1 = (f32[128,768]{1,0:T(8,128)}, f32[128,256]{1,0:T(8,128)}, f32[128,1024]{1,0:T(8,128)}, f32[128,1024]{1,0:T(8,128)}, f32[128,1536]{1,0:T(8,128)}, /*inde...) custom-call(f32[8,4,8,128]{3,2,1,0:T(8,128)} %get-tuple-element.97.d, ...), custom_call_target="tpu_custom_call" | custom-call | bytes 30000000 | tf_op jit(solution)/shard_map/adam/pallas_call | solution.py:1587
  324.1 1.3 reduce
